TPU v7x, 512 devices: a whole 4x8x8 slice. The times are simulated.
512 devices in a mesh: head: 8 (over x, core), tok: 64 (over z, y).
Axes of the slice: x: 4, y: 8, z: 8, core: 2. Of those that a mesh axis runs over, the one named last changes fastest.
Arguments:
- queries: bfloat16 [49152, 1024], P('tok', 'head'), may hold values from -512 to 512
- keys: bfloat16 [49152, 1024], P('tok', 'head'), may hold values from -8 to 8
- values: bfloat16 [49152, 1024], P('tok', 'head'), may hold values from -6 to 6
- out_grad: bfloat16 [49152, 1024], P('tok', 'head'), may hold values from -6 to 6
- w_query: bfloat16 [1024, 1024], P(None, 'head'), may hold values from -0.1875 to 0.1875
- w_key: bfloat16 [1024, 1024], P(None, 'head'), may hold values from -0.1875 to 0.1875
- w_value: bfloat16 [1024, 1024], P(None, 'head'), may hold values from -0.1875 to 0.1875
- w_out: bfloat16 [1024, 1024], P('head'), may hold values from -0.1875 to 0.1875
- page_cluster: int32 [1536], replicated, may hold values from 0 to 63, as said below
Outputs:
- input_grad: bfloat16 [49152, 1024], P('tok', 'head')
Inputs may be any that keep to these rules, and one draw needn't show every extreme that they name: `page_cluster`: the 24 pages k * 24 to k * 24 + 23, for each k, name distinct clusters. No cluster is named by more than 32 pages, and some cluster by exactly 32.
All inputs are finite; a program needn't handle non-finite values.
Results may differ from a plain program's by a relative error of at most 0.014.
Values may be sent and summed in bfloat16 or wider, within the bound.
No kernel may reach another device: no remote copies, remote signals or barrier semaphores. Data moves between devices by JAX's collectives and lax.ppermute only.
A program may use at most 64 MiB of HBM per device.

v0:
```python
import jax
import jax.numpy as jnp
from jax import lax
from jax.sharding import PartitionSpec as P

HEAD_DIM = 128
PAGE = 32


def laid_out(pieces, dim):
    pieces = jnp.moveaxis(pieces, 0, dim)
    lengths = pieces.shape
    return pieces.reshape(*lengths[:dim], lengths[dim] * lengths[dim + 1], *lengths[dim + 2 :])


def sent_to_all(array, axis):
    count = lax.axis_size(axis)
    return lax.all_to_all(
        jnp.broadcast_to(array[None], (count, *array.shape)), axis, 0, 0, tiled=True
    )


def collect(array, axis, dim):
    return laid_out(sent_to_all(array, axis), dim)


def in_one_piece(arrays, axis, split_dim, concat_dim, along):
    widths = [a.shape[along] for a in arrays]
    both = jnp.concatenate(arrays, axis=along)
    out = lax.all_to_all(both, axis, split_axis=split_dim, concat_axis=concat_dim, tiled=True)
    return tuple(jnp.split(out, [sum(widths[:k]) for k in range(1, len(widths))], axis=along))


def in_blocks(array, dim, count):
    before, after = (array.shape[:dim], array.shape[dim + 1 :])
    return jnp.moveaxis(array.reshape(*before, count, -1, *after), dim, 0)


def sent_and_summed(array, axis, dim):
    pieces = in_blocks(array, dim, lax.axis_size(axis))
    arrived = lax.all_to_all(pieces, axis, split_axis=0, concat_axis=0, tiled=True)
    return arrived.astype(jnp.float32).sum(axis=0)


def per_device(queries, keys, values, out_grad, w_query, w_key, w_value, w_out, page_cluster):
    tok_rows, head_cols = queries.shape
    pages_here = tok_rows // PAGE
    heads_here = head_cols // HEAD_DIM
    peers = lax.axis_size("tok")
    myself = lax.axis_index("tok")
    page_total = page_cluster.shape[0]
    slot_count = peers // 2
    cluster_rows = slot_count * PAGE
    score_scale = HEAD_DIM ** (-0.5)
    grad_heads = jnp.einsum(
        "td,hd->th", collect(out_grad, "head", 1), w_out, preferred_element_type=jnp.float32
    ).astype(jnp.bfloat16)
    page_order = jnp.arange(page_total, dtype=jnp.int32)
    peer_order = jnp.arange(peers, dtype=jnp.int32)
    cluster_onehot = (page_cluster[:, None] == peer_order[None, :]).astype(jnp.int32)
    running_count = jnp.cumsum(cluster_onehot, axis=0) - cluster_onehot
    page_rank = jnp.sum(running_count * cluster_onehot, axis=1)
    my_clusters = lax.dynamic_slice_in_dim(page_cluster, myself * pages_here, pages_here)
    going = my_clusters[None, :] == peer_order[:, None]
    going_any = jnp.any(going, axis=1)
    going_index = jnp.sum(
        going.astype(jnp.int32) * jnp.arange(pages_here, dtype=jnp.int32)[None, :], axis=1
    )

    def outgoing(matrix):
        paged = matrix.reshape(pages_here, PAGE, matrix.shape[1])
        picked = jnp.take(paged, going_index, axis=0)
        return jnp.where(going_any[:, None, None], picked, jnp.zeros_like(picked))

    arrived = in_one_piece(
        (outgoing(queries), outgoing(keys), outgoing(values), outgoing(grad_heads)), "tok", 0, 0, 1
    )
    slot_order = jnp.arange(slot_count, dtype=jnp.int32)
    slot_hit = (page_cluster[None, :] == myself) & (page_rank[None, :] == slot_order[:, None])
    filled = jnp.any(slot_hit, axis=1)
    slot_page = jnp.sum(slot_hit.astype(jnp.int32) * page_order[None, :], axis=1)
    slot_source = slot_page // pages_here

    def assemble(matrix):
        picked = jnp.take(matrix, slot_source, axis=0)
        picked = jnp.where(filled[:, None, None], picked, jnp.zeros_like(picked))
        return picked.reshape(cluster_rows, heads_here, HEAD_DIM)

    slot_query = assemble(arrived[0])
    slot_keys = assemble(arrived[1])
    slot_values = assemble(arrived[2])
    slot_grads = assemble(arrived[3])
    inner_index = jnp.arange(PAGE, dtype=jnp.int32)
    key_pos = (slot_page[:, None] * PAGE + inner_index[None, :]).reshape(cluster_rows)
    key_live = jnp.broadcast_to(filled[:, None], (slot_count, PAGE)).reshape(cluster_rows)
    key_order = jnp.arange(cluster_rows, dtype=jnp.int32)
    block_rows = min(512, cluster_rows)
    dkey_sum = jnp.zeros((cluster_rows, heads_here, HEAD_DIM), jnp.float32)
    dvalue_sum = jnp.zeros((cluster_rows, heads_here, HEAD_DIM), jnp.float32)
    query_parts = []
    for block_index in range(cluster_rows // block_rows):
        first_row = block_index * block_rows
        last_row = first_row + block_rows
        part_query = slot_query[first_row:last_row]
        part_grads = slot_grads[first_row:last_row]
        row_pos = key_pos[first_row:last_row]
        row_order = key_order[first_row:last_row]
        allowed = key_live[None, :] & (key_pos[None, :] <= row_pos[:, None]) | (
            key_order[None, :] == row_order[:, None]
        )
        score = (
            jnp.einsum("qhd,khd->hqk", part_query, slot_keys, preferred_element_type=jnp.float32)
            * score_scale
        )
        score = jnp.where(allowed[None], score, -1e30)
        row_max = jnp.max(score, axis=2, keepdims=True)
        raised = jnp.where(allowed[None], jnp.exp(score - row_max), 0.0)
        weights = raised / jnp.sum(raised, axis=2, keepdims=True)
        weights_half = weights.astype(jnp.bfloat16)
        grad_weights = jnp.einsum(
            "qhd,khd->hqk", part_grads, slot_values, preferred_element_type=jnp.float32
        )
        row_delta = jnp.sum(weights * grad_weights, axis=2, keepdims=True)
        grad_score = (weights * (grad_weights - row_delta)).astype(jnp.bfloat16)
        grad_query = (
            jnp.einsum("hqk,khd->qhd", grad_score, slot_keys, preferred_element_type=jnp.float32)
            * score_scale
        )
        query_parts.append(grad_query.astype(jnp.bfloat16))
        dkey_sum = dkey_sum + jnp.einsum(
            "hqk,qhd->khd", grad_score, part_query, preferred_element_type=jnp.float32
        )
        dvalue_sum = dvalue_sum + jnp.einsum(
            "hqk,qhd->khd", weights_half, part_grads, preferred_element_type=jnp.float32
        )
    slot_dquery = jnp.concatenate(query_parts, axis=0).reshape(cluster_rows, head_cols)
    slot_dkey = (dkey_sum * score_scale).astype(jnp.bfloat16).reshape(cluster_rows, head_cols)
    slot_dvalue = dvalue_sum.astype(jnp.bfloat16).reshape(cluster_rows, head_cols)
    back_hit = (slot_source[None, :] == peer_order[:, None]) & filled[None, :]
    back_any = jnp.any(back_hit, axis=1)
    back_slot = jnp.sum(back_hit.astype(jnp.int32) * slot_order[None, :], axis=1)
    share_rows = w_query.shape[0] // lax.axis_size("head")
    total = jnp.einsum("dh,th->dt", w_query, slot_dquery, preferred_element_type=jnp.float32)
    total = total + jnp.einsum("dh,th->dt", w_key, slot_dkey, preferred_element_type=jnp.float32)
    total = total + jnp.einsum(
        "dh,th->dt", w_value, slot_dvalue, preferred_element_type=jnp.float32
    )
    column_share = sent_and_summed(total.astype(jnp.bfloat16), "head", 0).astype(jnp.bfloat16)
    column_share = column_share.reshape(share_rows, slot_count, PAGE)
    picked = jnp.take(column_share, back_slot, axis=1)
    picked = jnp.where(back_any[None, :, None], picked, jnp.zeros_like(picked))
    returned = lax.all_to_all(picked, "tok", split_axis=1, concat_axis=1, tiled=True)
    input_grad = jnp.take(returned, my_clusters, axis=1).reshape(share_rows, tok_rows).T
    return input_grad


def solution(mesh):
    placed = (
        P("tok", "head"),
        P("tok", "head"),
        P("tok", "head"),
        P("tok", "head"),
        P(None, "head"),
        P(None, "head"),
        P(None, "head"),
        P("head", None),
        P(),
    )
    return jax.shard_map(
        per_device, mesh=mesh, in_specs=placed, out_specs=P("tok", "head"), check_vma=False
    )
```

profile of v0, /device:TPU:8, one launch (start us, length us, event | category | flops | bytes accessed | tf_op | source)
XLA Modules:
  0.0 199.9 jit_solution(13699799152277035723)
XLA Ops:
  1.1 1.3 broadcast_in_dim.157
  2.4 4.4 %all-to-all-start = ((bf16[8,768,128]{1,2,0:T(8,128)(2,1)}), bf16[8,768,128]{1,2,0:T(8,128)(2,1)S(1)}, u32[]{:S(2)}, u32[]{:S(2)}) async-start(bf16[8,768,128]{1,2,0:T(8,128)(2,1)} %broadcast_in_dim.157), calls=%async_computation | async-start | bytes 3145728 | tf_op jit(solution)/shard_map/all_to_all | solution.py:18
  8.9 1.4 gather_fusion.4
  10.5 17.9 %all-to-all-done = bf16[8,768,128]{1,2,0:T(8,128)(2,1)S(1)} async-done(((bf16[8,768,128]{1,2,0:T(8,128)(2,1)}), bf16[8,768,128]{1,2,0:T(8,128)(2,1)S(1)}, u32[]{:S(2)}, u32[]{:S(2)}) %all-to-all-start) | async-done | bytes 1572896 | tf_op jit(solution)/shard_map/all_to_all | solution.py:18
  28.4 1.6 convolution_convert_fusion
  30.6 1.4 select_select_fusion.3
  32.0 1.7 pad_maximum_fusion
  33.7 16.6 %all-to-all-start.1 = ((bf16[64,128,128]{2,1,0:T(8,128)(2,1)}), bf16[64,128,128]{2,1,0:T(8,128)(2,1)S(1)}, u32[]{:S(2)}, u32[]{:S(2)}) async-start(bf16[64,128,128]{2,1,0:T(8,128)(2,1)} %pad_maximum_fusion), calls=%async_computation.1 | async-start | bytes 4194304 | tf_op jit(solution)/shard_map/all_to_all | solution.py:30
  50.3 18.1 %reduce-window.6 = s32[64,12,128]{2,1,0:T(8,128)S(1)} reduce-window(s32[64,12,128]{2,1,0:T(8,128)S(1)} %fusion.22, s32[]{:T(128)} %constant.49.clone.1), window={size=1x1x128 pad=0_0x0_0x127_0}, to_apply=%region_0.0 | reduce-window | flops 12484608 | bytes 786436 | tf_op jit(solution)/shard_map/reduce-window
  71.5 31.2 %all-to-all-done.1 = bf16[64,128,128]{2,1,0:T(8,128)(2,1)S(1)} async-done(((bf16[64,128,128]{2,1,0:T(8,128)(2,1)}), bf16[64,128,128]{2,1,0:T(8,128)(2,1)S(1)}, u32[]{:S(2)}, u32[]{:S(2)}) %all-to-all-start.1) | async-done | bytes 2097184 | tf_op jit(solution)/shard_map/all_to_all | solution.py:30
  102.7 1.4 fusion.41
  104.1 1.6 gather_fusion.6
  105.7 1.6 gather_fusion.9
  109.5 1.7 fusion.2
  111.3 2.7 %fusion.6 = (f32[512]{0:T(512)S(1)}, f32[512]{0:T(512)S(1)}) fusion(f32[512,1024]{1,0:T(8,128)S(1)} %get-tuple-element.36, f32[512]{0:T(512)S(1)} %get-tuple-element.9, s32[512]{0:T(512)S(1)} %copy-done.8, s32[512]{0:T(512)S(1)} %le.62, s32[1024]{0:T(1024)S(1)} %add.90, pred[1024]{0:T(1024)(128)(4,1)S(1)} %copy-done.11, f32[512]{0:T(512)S(1)} %get-tuple-element.10, ...), kind=kLoop, calls=%fused_computation.30 | loop fusion | flops 9436160 | bytes 4215808 | tf_op jit(solution)/shard_map/reduce_sum | solution.py:118
  114.0 1.3 multiply_reduce_fusion
  115.4 2.6 %multiply_reduce_fusion.1 = (f32[512]{0:T(512)S(1)}, f32[512,1024]{1,0:T(8,128)S(1)}, bf16[512,1024]{1,0:T(8,128)(2,1)S(1)}, f32[512,1024]{1,0:T(8,128)S(1)}) fusion(f32[512]{0:T(512)S(1)} %get-tuple-element.6, f32[512]{0:T(512)S(1)} %get-tuple-element.9, f32[512,1024]{1,0:T(8,128)S(1)} %get-tuple-element.36, s32[512]{0:T(512)S(1)} %copy-done.8, ...), kind=kOutput, calls=%fused_computation.18 | convolution fusion | flops 146275840 | bytes 11953152 | tf_op jit(solution)/shard_map/qhd,khd->hqk/dot_general | solution.py:120
  122.8 3.9 %fusion.12 = f32[1024,1024]{0,1:T(8,128)} fusion(bf16[1024,128]{1,0:T(8,128)(2,1)S(1)} %copy-done, f32[128,1024]{1,0:T(8,128)} %fusion.46, bf16[512,128]{1,0:T(8,128)(2,1)S(1)} %bitcast.111, bf16[512,1024]{1,0:T(8,128)(2,1)S(1)} %get-tuple-element.27), kind=kOutput, calls=%fused_computation.37 | convolution fusion | flops 403046400 | bytes 6160384 | tf_op jit(solution)/shard_map/dh,th->dt/dot_general | solution.py:144
  126.8 3.8 %fusion.26 = f32[1024,1024]{0,1:T(8,128)} fusion(bf16[1024,128]{1,0:T(8,128)(2,1)} %param.17, bf16[512,1,128]{0,2,1:T(8,128)(2,1)} %fusion.16, bf16[512,1,128]{0,2,1:T(8,128)(2,1)} %fusion.17), kind=kOutput, calls=%fused_computation.61 | convolution fusion | flops 268959744 | bytes 4718592 | tf_op jit(solution)/shard_map/dh,th->dt/dot_general | solution.py:143
  130.6 6.8 %add_convert_fusion = bf16[1024,1024]{0,1:T(8,128)(2,1)} fusion(f32[1024,1024]{0,1:T(8,128)} %fusion.26, f32[1024,1024]{0,1:T(8,128)} %fusion.12, bf16[1024,128]{1,0:T(8,128)(2,1)S(1)} %copy-done.20, f32[128,1024]{1,0:T(8,128)S(1)} %copy-done.4, bf16[512,128]{1,0:T(8,128)(2,1)S(1)} %bitcast.119, f32[512,1024]{1,0:T(8,128)S(1)} %fusion.45, ...), kind=kOutput, calls=%fused_computation.10 | convolution fusion | flops 411303936 | bytes 13513728 | tf_op jit(solution)/shard_map/dh,th->dt/dot_general | solution.py:145
  137.4 3.7 %all-to-all-start.2 = ((bf16[8,128,1024]{2,1,0:T(8,128)(2,1)}), bf16[8,128,1024]{2,1,0:T(8,128)(2,1)S(1)}, u32[]{:S(2)}, u32[]{:S(2)}) async-start(bf16[8,128,1024]{2,1,0:T(8,128)(2,1)} %bitcast.105), calls=%async_computation.2 | async-start | bytes 4194304 | tf_op jit(solution)/shard_map/all_to_all | solution.py:41
  141.4 26.9 %all-to-all-done.2 = bf16[8,128,1024]{2,1,0:T(8,128)(2,1)S(1)} async-done(((bf16[8,128,1024]{2,1,0:T(8,128)(2,1)}), bf16[8,128,1024]{2,1,0:T(8,128)(2,1)S(1)}, u32[]{:S(2)}, u32[]{:S(2)}) %all-to-all-start.2) | async-done | bytes 2097184 | tf_op jit(solution)/shard_map/all_to_all | solution.py:41
  170.5 8.9 %all-to-all-start.3 = ((bf16[128,64,32]{0,2,1:T(8,128)(2,1)}), bf16[128,64,32]{0,2,1:T(8,128)(2,1)S(1)}, u32[]{:S(2)}, u32[]{:S(2)}) async-start(bf16[128,64,32]{0,2,1:T(8,128)(2,1)} %select_bitcast_fusion), calls=%async_computation.3 | async-start | bytes 1048576 | tf_op jit(solution)/shard_map/all_to_all | solution.py:152
  179.6 18.9 %all-to-all-done.3 = bf16[128,64,32]{0,2,1:T(8,128)(2,1)S(1)} async-done(((bf16[128,64,32]{0,2,1:T(8,128)(2,1)}), bf16[128,64,32]{0,2,1:T(8,128)(2,1)S(1)}, u32[]{:S(2)}, u32[]{:S(2)}) %all-to-all-start.3) | async-done | bytes 524320 | tf_op jit(solution)/shard_map/all_to_all | solution.py:152
  (106 shorter events, 18.0 us)
Async XLA Ops:
  0.0 122.8 %copy-start = (bf16[1024,128]{1,0:T(8,128)(2,1)S(1)}, bf16[1024,128]{1,0:T(8,128)(2,1)}, u32[]{:S(2)}) copy-start(bf16[1024,128]{1,0:T(8,128)(2,1)} %param.18) | copy-start | bytes 786436
  1.1 5.7 %copy-start.7 = (s32[1536]{0:T(1024)S(1)}, s32[1536]{0:T(1024)}, u32[]{:S(2)}) copy-start(s32[1536]{0:T(1024)} %param.21) | copy-start | bytes 18436
  1.1 6.5 %copy-start.1 = (bf16[768,128]{1,0:T(8,128)(2,1)S(1)}, bf16[768,128]{1,0:T(8,128)(2,1)}, u32[]{:S(2)}) copy-start(bf16[768,128]{1,0:T(8,128)(2,1)} %param.13) | copy-start | bytes 589828
  2.4 5.9 %copy-start.2 = (bf16[768,128]{1,0:T(8,128)(2,1)S(1)}, bf16[768,128]{1,0:T(8,128)(2,1)}, u32[]{:S(2)}) copy-start(bf16[768,128]{1,0:T(8,128)(2,1)} %param.14) | copy-start | bytes 589828
  2.4 6.5 %copy-start.3 = (bf16[768,128]{1,0:T(8,128)(2,1)S(1)}, bf16[768,128]{1,0:T(8,128)(2,1)}, u32[]{:S(2)}) copy-start(bf16[768,128]{1,0:T(8,128)(2,1)} %param.15) | copy-start | bytes 589828
  2.4 26.0 %all-to-all-start = ((bf16[8,768,128]{1,2,0:T(8,128)(2,1)}), bf16[8,768,128]{1,2,0:T(8,128)(2,1)S(1)}, u32[]{:S(2)}, u32[]{:S(2)}) async-start(bf16[8,768,128]{1,2,0:T(8,128)(2,1)} %broadcast_in_dim.157), calls=%async_computation | async-start | bytes 3145728 | tf_op jit(solution)/shard_map/all_to_all | solution.py:18
  7.5 22.5 %copy-start.18 = (s32[24]{0:T(128)}, s32[24]{0:T(128)S(1)}, u32[]{:S(2)}) copy-start(s32[24]{0:T(128)S(1)} %get-tuple-element.12) | copy-start | bytes 292
  33.7 69.0 %all-to-all-start.1 = ((bf16[64,128,128]{2,1,0:T(8,128)(2,1)}), bf16[64,128,128]{2,1,0:T(8,128)(2,1)S(1)}, u32[]{:S(2)}, u32[]{:S(2)}) async-start(bf16[64,128,128]{2,1,0:T(8,128)(2,1)} %pad_maximum_fusion), calls=%async_computation.1 | async-start | bytes 4194304 | tf_op jit(solution)/shard_map/all_to_all | solution.py:30
  70.0 38.6 %copy-start.9 = (pred[32]{0:T(512)(128)(4,1)}, pred[32]{0:T(512)(128)(4,1)S(1)}, u32[]{:S(2)}) copy-start(pred[32]{0:T(512)(128)(4,1)S(1)} %fusion.31) | copy-start | bytes 100
  71.4 32.7 %copy-start.21 = (s32[32]{0:T(128)}, s32[32]{0:T(128)S(1)}, u32[]{:S(2)}) copy-start(s32[32]{0:T(128)S(1)} %get-tuple-element.16) | copy-start | bytes 388
  108.9 5.1 %copy-start.5 = (bf16[16,32,128]{2,1,0:T(8,128)(2,1)}, bf16[16,32,128]{2,1,0:T(8,128)(2,1)S(1)}, u32[]{:S(2)}) copy-start(bf16[16,32,128]{2,1,0:T(8,128)(2,1)S(1)} %get-tuple-element.22) | copy-start | bytes 393220
  111.2 4.1 %copy-start.13 = (f32[512]{0:T(512)}, f32[512]{0:T(512)S(1)}, u32[]{:S(2)}) copy-start(f32[512]{0:T(512)S(1)} %get-tuple-element.10) | copy-start | bytes 6148
  126.8 3.8 %copy-start.4 = (f32[128,1024]{1,0:T(8,128)S(1)}, f32[128,1024]{1,0:T(8,128)}, u32[]{:S(2)}) copy-start(f32[128,1024]{1,0:T(8,128)} %fusion.20) | copy-start | bytes 1572868
  126.8 3.8 %copy-start.6 = (bf16[16,32,128]{2,1,0:T(8,128)(2,1)S(1)}, bf16[16,32,128]{2,1,0:T(8,128)(2,1)}, u32[]{:S(2)}) copy-start(bf16[16,32,128]{2,1,0:T(8,128)(2,1)} %copy-done.5) | copy-start | bytes 393220
  126.8 3.8 %copy-start.12 = (pred[1024]{0:T(1024)(128)(4,1)S(1)}, pred[1024]{0:T(1024)(128)(4,1)}, u32[]{:S(2)}) copy-start(pred[1024]{0:T(1024)(128)(4,1)} %and.68) | copy-start | bytes 3076
  126.8 3.8 %copy-start.14 = (f32[512]{0:T(512)S(1)}, f32[512]{0:T(512)}, u32[]{:S(2)}) copy-start(f32[512]{0:T(512)} %copy-done.13) | copy-start | bytes 6148
  126.8 3.8 %copy-start.16 = (f32[512]{0:T(512)S(1)}, f32[512]{0:T(512)}, u32[]{:S(2)}) copy-start(f32[512]{0:T(512)} %copy-done.15) | copy-start | bytes 6148
  126.8 3.8 %copy-start.20 = (bf16[1024,128]{1,0:T(8,128)(2,1)S(1)}, bf16[1024,128]{1,0:T(8,128)(2,1)}, u32[]{:S(2)}) copy-start(bf16[1024,128]{1,0:T(8,128)(2,1)} %param.19) | copy-start | bytes 786436
  137.4 3.7 %copy-start.10 = (pred[32]{0:T(512)(128)(4,1)S(1)}, pred[32]{0:T(512)(128)(4,1)}, u32[]{:S(2)}) copy-start(pred[32]{0:T(512)(128)(4,1)} %copy-done.9) | copy-start | bytes 100
  137.4 3.8 %copy-start.22 = (s32[32]{0:T(128)S(1)}, s32[32]{0:T(128)}, u32[]{:S(2)}) copy-start(s32[32]{0:T(128)} %copy-done.21) | copy-start | bytes 388
  137.4 30.8 %all-to-all-start.2 = ((bf16[8,128,1024]{2,1,0:T(8,128)(2,1)}), bf16[8,128,1024]{2,1,0:T(8,128)(2,1)S(1)}, u32[]{:S(2)}, u32[]{:S(2)}) async-start(bf16[8,128,1024]{2,1,0:T(8,128)(2,1)} %bitcast.105), calls=%async_computation.2 | async-start | bytes 4194304 | tf_op jit(solution)/shard_map/all_to_all | solution.py:41
  169.5 9.9 %copy-start.17 = (pred[24]{0:T(512)(128)(4,1)S(1)}, pred[24]{0:T(512)(128)(4,1)}, u32[]{:S(2)}) copy-start(pred[24]{0:T(512)(128)(4,1)} %get-tuple-element.11) | copy-start | bytes 76
  169.5 10.1 %copy-start.19 = (s32[24]{0:T(128)S(1)}, s32[24]{0:T(128)}, u32[]{:S(2)}) copy-start(s32[24]{0:T(128)} %copy-done.18) | copy-start | bytes 292
  170.5 28.0 %all-to-all-start.3 = ((bf16[128,64,32]{0,2,1:T(8,128)(2,1)}), bf16[128,64,32]{0,2,1:T(8,128)(2,1)S(1)}, u32[]{:S(2)}, u32[]{:S(2)}) async-start(bf16[128,64,32]{0,2,1:T(8,128)(2,1)} %select_bitcast_fusion), calls=%async_computation.3 | async-start | bytes 1048576 | tf_op jit(solution)/shard_map/all_to_all | solution.py:152
  (3 other events, 2.7 us)
where the time goes:
time: 201 us; the launch traced here: 200 us
  waiting for transfers between devices  94.9 us (47%)
  starting transfers between devices  33.7 us (17%)
  other arithmetic  28.5 us (14%)
  matrix products  26.8 us (13%)
  local copies, waits for them, and re-layouts  15.7 us (8%)
    all_to_all x1, waiting for transfers between devices, in_one_piece(): lax.all_to_all(both, axis, split_axis=split_dim, concat_axis=concat_dim,...  31.2 us
    all_to_all x1, waiting for transfers between devices, sent_and_summed(): lax.all_to_all(pieces, axis, split_axis=0, concat_axis=0, tiled=True)  26.9 us
    all_to_all x1, waiting for transfers between devices, per_device(): lax.all_to_all(picked, 'tok', split_axis=1, concat_axis=1, tiled=True)  18.9 us
    another operation x3, other arithmetic  18.4 us
    all_to_all x1, waiting for transfers between devices, sent_to_all(): lax.all_to_all(jnp.broadcast_to(array[None], (count, *array.shape)), axis...  17.9 us
    all_to_all x1, starting transfers between devices, in_one_piece(): lax.all_to_all(both, axis, split_axis=split_dim, concat_axis=concat_dim,...  16.6 us
    all_to_all x1, starting transfers between devices, per_device(): lax.all_to_all(picked, 'tok', split_axis=1, concat_axis=1, tiled=True)  8.91 us
    dot_general x1, matrix products, per_device(): jnp.einsum('dh,th->dt', w_value, slot_dvalue, preferred_element_type=jnp....  6.8 us
  transfers between devices with their start and end apart: 4, of which 4 were waited for; matrix products, arithmetic and copies ran while one was open for 13% of the time, Pallas kernels for 0%

commit v1 on v0

v1 whole, which is shorter than its diff:
```python
import math

import jax
import jax.numpy as jnp
from jax import lax
from jax.experimental import pallas as pl
from jax.experimental.pallas import tpu as pltpu
from jax.sharding import PartitionSpec as P

HEAD_DIM = 128
PAGE = 32
SLOTS = 32
BLOCK = 256
NEG = -1e30
VMEM = pl.BlockSpec(memory_space=pltpu.VMEM)
SMEM = pl.BlockSpec(memory_space=pltpu.SMEM)


def mm(a, b, dims):
    return lax.dot_general(a, b, (dims, ((), ())), preferred_element_type=jnp.float32)


def rows(page):
    return pl.ds(pl.multiple_of(page * PAGE, PAGE), PAGE)


def pack_kernel(dest, core, query, key, value, even, odd, w_out, sent, grad):
    count = even.shape[0]
    total = None
    for x in range(count):
        for got, side in ((even, core[0]), (odd, 1 - core[0])):
            part = mm(got[x], w_out[2 * x + side], ((1,), (1,)))
            total = part if total is None else total + part
    grad[...] = total.astype(grad.dtype)
    for page in range(dest.shape[0]):
        peer = dest[page]
        for part, array in enumerate((query, key, value, grad)):
            sent[peer, part * PAGE : (part + 1) * PAGE] = array[page * PAGE : (page + 1) * PAGE]


def attention_kernel(source, arrived, grads, query, key, value, grad, dkey, dvalue):
    scale = HEAD_DIM ** (-0.5)
    arrays = (query, key, value, grad)

    def assemble(slot, carry):
        peer = source[slot]

        @pl.when(peer >= 0)
        def _():
            for part, array in enumerate(arrays):
                array[rows(slot)] = arrived[peer, part * PAGE : (part + 1) * PAGE]

        @pl.when(peer < 0)
        def _():
            for array in arrays:
                array[rows(slot)] = jnp.zeros((PAGE, HEAD_DIM), array.dtype)

        return carry

    lax.fori_loop(0, source.shape[0], assemble, 0)
    total = query.shape[0]
    block = min(BLOCK, total)
    row_order = lax.broadcasted_iota(jnp.int32, (block, block), 0)
    causal = lax.broadcasted_iota(jnp.int32, (block, block), 1) <= row_order
    for first in range(0, total, block):
        last = first + block
        here = slice(first, last)
        spans = ([slice(0, first)] if first else []) + [here]
        part_query, part_grad = query[here], grad[here]
        score = [mm(part_query, key[span], ((1,), (1,))) for span in spans]
        score[-1] = jnp.where(causal, score[-1], NEG)
        row_max = score[-1].max(axis=1, keepdims=True)
        if first:
            row_max = jnp.maximum(row_max, score[0].max(axis=1, keepdims=True))
        raised = [jnp.exp2((s - row_max) * (scale * math.log2(math.e))) for s in score]
        row_sum = sum(r.sum(axis=1, keepdims=True) for r in raised)
        inverse = 1.0 / row_sum
        weights = [r * inverse for r in raised]
        grad_weights = [mm(part_grad, value[span], ((1,), (1,))) for span in spans]
        row_delta = sum((w * g).sum(axis=1, keepdims=True) for w, g in zip(weights, grad_weights))
        grad_score = [
            (w * (g - row_delta)).astype(jnp.bfloat16) for w, g in zip(weights, grad_weights)
        ]
        dquery = sum(mm(d, key[span], ((1,), (0,))) for d, span in zip(grad_score, spans))
        grads[here, 0:HEAD_DIM] = (dquery * scale).astype(grads.dtype)
        for w, d, span in zip(weights, grad_score, spans):
            more_key = mm(d, part_query, ((0,), (0,)))
            more_value = mm(w.astype(jnp.bfloat16), part_grad, ((0,), (0,)))
            if span is here:
                dkey[span] = more_key
                dvalue[span] = more_value
            else:
                dkey[span] += more_key
                dvalue[span] += more_value
    grads[:, HEAD_DIM : 2 * HEAD_DIM] = (dkey[...] * scale).astype(grads.dtype)
    grads[:, 2 * HEAD_DIM : 3 * HEAD_DIM] = dvalue[...].astype(grads.dtype)


def project_kernel(mine, theirs, w_mine, w_theirs, out):
    total = mm(mine[...], w_mine[...], ((1,), (1,))) + mm(theirs[...], w_theirs[...], ((1,), (1,)))
    for x in range(out.shape[0]):
        out[x] = total[:, x * HEAD_DIM : (x + 1) * HEAD_DIM].astype(out.dtype)


def sum_kernel(source, parts, sent):
    def one(slot, carry):
        peer = source[slot]

        @pl.when(peer >= 0)
        def _():
            total = parts[0, rows(slot)].astype(jnp.float32)
            for x in range(1, parts.shape[0]):
                total = total + parts[x, rows(slot)].astype(jnp.float32)
            sent[peer] = total.astype(sent.dtype)

        return carry

    lax.fori_loop(0, source.shape[0], one, 0)


def unpack_kernel(dest, returned, out):
    for page in range(dest.shape[0]):
        out[page * PAGE : (page + 1) * PAGE] = returned[dest[page]]


def per_device(queries, keys, values, out_grad, w_query, w_key, w_value, w_out, page_cluster):
    tok_rows = queries.shape[0]
    pages_here = tok_rows // PAGE
    peers = lax.axis_size("tok")
    heads = lax.axis_size("head")
    chips = heads // 2
    myself = lax.axis_index("tok")
    core = lax.axis_index("head") % 2
    across = [[2 * x + side for x in range(chips)] for side in range(2)]
    swap = [(h, h ^ 1) for h in range(heads)]
    slot_rows = SLOTS * PAGE
    half = queries.dtype

    table = page_cluster.reshape(peers, pages_here)
    dest = lax.dynamic_index_in_dim(table, myself, 0, keepdims=False)
    has = jnp.any(table == myself, axis=1).astype(jnp.int32)
    peer_order = jnp.arange(peers, dtype=jnp.int32)
    rank = jnp.sum(jnp.where(peer_order[:, None] < peer_order[None, :], has[:, None], 0), axis=0)
    slot_order = jnp.arange(SLOTS, dtype=jnp.int32)
    hit = (rank[None, :] == slot_order[:, None]) & (has[None, :] == 1)
    source = jnp.sum(jnp.where(hit, peer_order[None, :] + 1, 0), axis=1) - 1

    w_blocks = w_out.reshape(HEAD_DIM, heads, HEAD_DIM).transpose(1, 0, 2)

    same_core = lax.all_to_all(
        jnp.broadcast_to(out_grad[None], (chips, *out_grad.shape)),
        "head", 0, 0, axis_index_groups=across, tiled=True,
    )
    other_core = lax.ppermute(same_core, "head", swap)
    sent = pl.pallas_call(
        pack_kernel,
        out_shape=jax.ShapeDtypeStruct((peers, 4 * PAGE, HEAD_DIM), half),
        in_specs=[SMEM, SMEM] + [VMEM] * 6,
        out_specs=VMEM,
        scratch_shapes=[pltpu.VMEM((tok_rows, HEAD_DIM), half)],
        name="pack",
    )(dest, core[None], queries, keys, values, same_core, other_core, w_blocks)
    sent, w_query, w_key, w_value = lax.optimization_barrier((sent, w_query, w_key, w_value))
    arrived = lax.all_to_all(sent, "tok", 0, 0, tiled=True)
    weights = jnp.concatenate([w_query, w_key, w_value], axis=1)
    weights = weights.reshape(chips, 2, HEAD_DIM, 3 * HEAD_DIM)
    w_mine = lax.dynamic_index_in_dim(weights, core, 1, keepdims=False)
    w_away = lax.dynamic_index_in_dim(weights, 1 - core, 1, keepdims=False)
    w_theirs = lax.ppermute(w_away, "head", swap)
    w_mine = w_mine.reshape(chips * HEAD_DIM, 3 * HEAD_DIM)
    w_theirs = w_theirs.reshape(chips * HEAD_DIM, 3 * HEAD_DIM)
    arrived, w_mine, w_theirs = lax.optimization_barrier((arrived, w_mine, w_theirs))
    grads = pl.pallas_call(
        attention_kernel,
        out_shape=jax.ShapeDtypeStruct((slot_rows, 3 * HEAD_DIM), half),
        in_specs=[SMEM, VMEM],
        out_specs=VMEM,
        scratch_shapes=[pltpu.VMEM((slot_rows, HEAD_DIM), half)] * 4
        + [pltpu.VMEM((slot_rows, HEAD_DIM), jnp.float32)] * 2,
        name="attention",
    )(source, arrived)
    their_grads = lax.ppermute(grads, "head", swap)
    step = min(BLOCK, slot_rows)
    row_block = pl.BlockSpec((step, 3 * HEAD_DIM), lambda i: (i, 0))
    w_block = pl.BlockSpec(w_mine.shape, lambda i: (0, 0))
    partial = pl.pallas_call(
        project_kernel,
        out_shape=jax.ShapeDtypeStruct((chips, slot_rows, HEAD_DIM), half),
        grid=(slot_rows // step,),
        in_specs=[row_block, row_block, w_block, w_block],
        out_specs=pl.BlockSpec((chips, step, HEAD_DIM), lambda i: (0, i, 0)),
        name="project",
    )(grads, their_grads, w_mine, w_theirs)
    parts = lax.all_to_all(partial, "head", 0, 0, axis_index_groups=across, tiled=True)
    summed = pl.pallas_call(
        sum_kernel,
        out_shape=jax.ShapeDtypeStruct((peers, PAGE, HEAD_DIM), half),
        in_specs=[SMEM, VMEM],
        out_specs=VMEM,
        name="sum",
    )(source, parts)
    returned = lax.all_to_all(summed, "tok", 0, 0, tiled=True)
    return pl.pallas_call(
        unpack_kernel,
        out_shape=jax.ShapeDtypeStruct((tok_rows, HEAD_DIM), half),
        in_specs=[SMEM, VMEM],
        out_specs=VMEM,
        name="unpack",
    )(dest, returned)


def solution(mesh):
    placed = (
        P("tok", "head"),
        P("tok", "head"),
        P("tok", "head"),
        P("tok", "head"),
        P(None, "head"),
        P(None, "head"),
        P(None, "head"),
        P("head", None),
        P(),
    )
    return jax.shard_map(
        per_device, mesh=mesh, in_specs=placed, out_specs=P("tok", "head"), check_vma=False
    )
```

time: 201 us -> 166 us (0.83)
  blocking collectives: 0 us -> 63.5 us
  waiting for transfers between devices: 94.9 us -> 51.9 us
  other arithmetic: 28.5 us -> 0.95 us
  matrix products: 26.8 us -> 0 us
  Pallas kernels: 0 us -> 19.2 us
  starting transfers between devices: 33.7 us -> 22.4 us
  local copies, waits for them, and re-layouts: 15.7 us -> 6.74 us
    all_to_all x0 -> x3, blocking collectives: none -> 63.5 us  [the longest x1 27.2 us: per_device(): returned = lax.all_to_all(summed, 'tok', 0, 0, tiled=True)]
    all_to_all x4 -> x1, waiting for transfers between devices: 94.9 us -> 47.8 us  [per_device(): arrived = lax.all_to_all(sent, 'tok', 0, 0, tiled=True)]
    dot_general x12 -> x0, matrix products: 26.8 us -> none  [the longest x1 6.8 us: per_device(): jnp.einsum('dh,th->dt', w_value, slot_dvalue, preferred_element_type=jnp....]
    pallas_call x0 -> x5, Pallas kernels: none -> 19.2 us  [the longest x1 6.46 us: per_device(): pl.pallas_call(attention_kernel, out_shape=jax.ShapeDtypeStruct((slot_row...]
    another operation x3 -> x0, other arithmetic: 18.4 us -> none
    all_to_all x4 -> x1, starting transfers between devices: 33.7 us -> 16.7 us  [per_device(): arrived = lax.all_to_all(sent, 'tok', 0, 0, tiled=True)]
    gather x10 -> x0, local copies, waits for them, and re-layouts: 9.13 us -> none  [the longest x4 4.5 us: assemble(): picked = jnp.take(matrix, slot_source, axis=0)]
    ppermute x0 -> x3, starting transfers between devices: none -> 5.73 us  [the longest x1 1.91 us: per_device(): other_core = lax.ppermute(same_core, 'head', swap)]
  transfers between devices with their start and end apart: 4 -> 4, of which waited for: 4 -> 4; matrix products, arithmetic and copies ran while one was open for 13% -> 2% of each run, Pallas kernels for 0% -> 0%
where the time goes in v1:
time: 166 us; the launch traced here: 165 us
  blocking collectives  63.5 us (38%)
  waiting for transfers between devices  51.9 us (31%)
  starting transfers between devices  22.4 us (13%)
  Pallas kernels  19.2 us (12%)
  local copies, waits for them, and re-layouts  6.74 us (4%)
    all_to_all x1, waiting for transfers between devices, per_device(): arrived = lax.all_to_all(sent, 'tok', 0, 0, tiled=True)  47.8 us
    all_to_all x1, blocking collectives, per_device(): returned = lax.all_to_all(summed, 'tok', 0, 0, tiled=True)  27.2 us
    all_to_all x1, blocking collectives, per_device(): lax.all_to_all(partial, 'head', 0, 0, axis_index_groups=across, tiled=True)  20 us
    all_to_all x1, starting transfers between devices, per_device(): arrived = lax.all_to_all(sent, 'tok', 0, 0, tiled=True)  16.7 us
    all_to_all x1, blocking collectives, per_device(): lax.all_to_all(jnp.broadcast_to(out_grad[None], (chips, *out_grad.shape))...  16.4 us
    pallas_call x1, Pallas kernels, per_device(): pl.pallas_call(attention_kernel, out_shape=jax.ShapeDtypeStruct((slot_row...  6.46 us
    pallas_call x1, Pallas kernels, per_device(): pl.pallas_call(project_kernel, out_shape=jax.ShapeDtypeStruct((chips, slo...  4.74 us
    pallas_call x1, Pallas kernels, per_device(): pl.pallas_call(pack_kernel, out_shape=jax.ShapeDtypeStruct((peers, 4 * PA...  3.62 us
  transfers between devices with their start and end apart: 4, of which 4 were waited for; matrix products, arithmetic and copies ran while one was open for 2% of the time, Pallas kernels for 0%

profile of v1, /device:TPU:8, one launch (start us, length us, event | category | flops | bytes accessed | tf_op | source)
XLA Modules:
  0.0 164.9 jit_solution(1556424868252545605)
XLA Ops:
  0.0 1.1 broadcast_in_dim.45
  1.1 16.4 %all_to_all.20.even = bf16[4,768,128]{2,1,0:T(8,128)(2,1)S(1)} all-to-all(bf16[4,768,128]{2,1,0:T(8,128)(2,1)S(1)} %broadcast_in_dim.45), channel_id=1, replica_groups={{0,128,256,384},{64,192,320,448},{1,129,257,385},{65,193,321,449},{2,13..., dimensions={0} | all-to-all | bytes 1572864 | tf_op jit(solution)/shard_map/all_to_all | solution.py:150
  17.5 1.9 %collective-permute-start = (bf16[4,768,128]{2,1,0:T(8,128)(2,1)S(1)}, bf16[4,768,128]{2,1,0:T(8,128)(2,1)S(1)}, u32[]{:S(2)}, u32[]{:S(2)}) collective-permute-start(bf16[4,768,128]{2,1,0:T(8,128)(2,1)S(1)} %all_to_all.20.even), channel_id=1, source_target_pairs={{0,64},{64,0},{128,192},{192,128},{256,320},{320,256},{384,448},{4... | collective-permute-start | bytes 2359304 | tf_op jit(solution)/shard_map/ppermute | solution.py:154
  19.7 0.8 copy.15
  20.5 0.5 fusion.1.dest
  21.1 0.6 collective-permute-done.odd
  21.6 0.9 copy-done.2
  22.5 3.6 %pack.1 = bf16[64,128,128]{2,1,0:T(8,128)(2,1)} custom-call(s32[24]{0:T(128)} %fusion.1.dest, s32[1]{0:T(128)} %bitcast.1.core, bf16[768,128]{1,0:T(8,128)(2,1)} %query.1, bf16[768,128]{1,0:T(8,128)(2,1)} %key.1, bf16[768,128]{1,0:T(8,128)(2,1)} %value.1, bf16[4,768,128]{2,1,0:T(8,128)(2,1)} %copy-done.1, bf16[4,768,128]{2,1,0:T(8,128)(2,1)} %copy-done.2, ...), custom_call_target="tpu_custom_call" | custom-call | tf_op jit(solution)/shard_map/pack/pallas_call | solution.py:155
  26.2 16.7 %all-to-all-start.1 = ((bf16[64,128,128]{2,1,0:T(8,128)(2,1)}), bf16[64,128,128]{2,1,0:T(8,128)(2,1)S(1)}, u32[]{:S(2)}, u32[]{:S(2)}) async-start(bf16[64,128,128]{2,1,0:T(8,128)(2,1)} %pack.1), calls=%async_computation.1 | async-start | bytes 4194304 | tf_op jit(solution)/shard_map/all_to_all | solution.py:164
  43.3 0.9 dynamic-slice_bitcast_fusion
  44.1 1.9 %collective-permute-start.1 = (bf16[4,128,384]{2,1,0:T(8,128)(2,1)S(1)}, bf16[4,128,384]{2,1,0:T(8,128)(2,1)S(1)}, u32[]{:S(2)}, u32[]{:S(2)}) collective-permute-start(bf16[4,128,384]{2,1,0:T(8,128)(2,1)S(1)} %get-tuple-element.19), channel_id=1, source_target_pairs={{0,64},{64,0},{128,192},{192,128},{256,320},{320,256},{384,448},{4... | collective-permute-start | bytes 1179656 | tf_op jit(solution)/shard_map/ppermute | solution.py:169
  46.2 0.5 broadcast_add_fusion.source
  46.7 1.0 collective-permute-done.1
  47.7 47.8 %all-to-all-done.1.arrived = bf16[64,128,128]{2,1,0:T(8,128)(2,1)S(1)} async-done(((bf16[64,128,128]{2,1,0:T(8,128)(2,1)}), bf16[64,128,128]{2,1,0:T(8,128)(2,1)S(1)}, u32[]{:S(2)}, u32[]{:S(2)}) %all-to-all-start.1) | async-done | bytes 2097184 | tf_op jit(solution)/shard_map/all_to_all | solution.py:164
  95.6 1.3 copy-done
  96.9 6.5 %attention.1.mine = bf16[1024,384]{1,0:T(8,128)(2,1)} custom-call(s32[32]{0:T(128)} %broadcast_add_fusion.source, bf16[64,128,128]{2,1,0:T(8,128)(2,1)} %copy-done), custom_call_target="tpu_custom_call" | custom-call | tf_op jit(solution)/shard_map/attention/pallas_call | solution.py:173
  103.4 1.9 %collective-permute-start.2 = (bf16[1024,384]{1,0:T(8,128)(2,1)}, bf16[1024,384]{1,0:T(8,128)(2,1)S(1)}, u32[]{:S(2)}, u32[]{:S(2)}) collective-permute-start(bf16[1024,384]{1,0:T(8,128)(2,1)} %attention.1.mine), channel_id=1, source_target_pairs={{0,64},{64,0},{128,192},{192,128},{256,320},{320,256},{384,448},{4... | collective-permute-start | bytes 2359304 | tf_op jit(solution)/shard_map/ppermute | solution.py:182
  105.3 2.5 %collective-permute-done.2.theirs = bf16[1024,384]{1,0:T(8,128)(2,1)S(1)} collective-permute-done((bf16[1024,384]{1,0:T(8,128)(2,1)}, bf16[1024,384]{1,0:T(8,128)(2,1)S(1)}, u32[]{:S(2)}, u32[]{:S(2)}) %collective-permute-start.2) | collective-permute-done | bytes 786464 | tf_op jit(solution)/shard_map/ppermute | solution.py:182
  107.8 0.9 copy-done.3
  108.7 4.7 %project.1 = bf16[4,1024,128]{2,1,0:T(8,128)(2,1)} custom-call(bf16[1024,384]{1,0:T(8,128)(2,1)} %attention.1.mine, bf16[1024,384]{1,0:T(8,128)(2,1)} %copy-done.3, bf16[512,384]{1,0:T(8,128)(2,1)} %bitcast.13, bf16[512,384]{1,0:T(8,128)(2,1)} %bitcast.16), custom_call_target="tpu_custom_call" | custom-call | tf_op jit(solution)/shard_map/project/pallas_call | solution.py:186
  113.4 20.0 %all_to_all.21.parts = bf16[4,1024,128]{2,1,0:T(8,128)(2,1)} all-to-all(bf16[4,1024,128]{2,1,0:T(8,128)(2,1)} %project.1), channel_id=1, replica_groups={{0,128,256,384},{64,192,320,448},{1,129,257,385},{65,193,321,449},{2,13..., dimensions={0} | all-to-all | bytes 2097152 | tf_op jit(solution)/shard_map/all_to_all | solution.py:194
  133.4 2.6 %sum.1 = bf16[64,32,128]{2,1,0:T(8,128)(2,1)} custom-call(s32[32]{0:T(128)} %broadcast_add_fusion.source, bf16[4,1024,128]{2,1,0:T(8,128)(2,1)} %all_to_all.21.parts), custom_call_target="tpu_custom_call" | custom-call | tf_op jit(solution)/shard_map/sum/pallas_call | solution.py:195
  136.0 27.2 %all_to_all.22.returned = bf16[64,32,128]{2,1,0:T(8,128)(2,1)} all-to-all(bf16[64,32,128]{2,1,0:T(8,128)(2,1)} %sum.1), channel_id=1, replica_groups=mesh['head'=8,'tok'=64] {'tok'}, dimensions={0} | all-to-all | bytes 1048576 | tf_op jit(solution)/shard_map/all_to_all | solution.py:202
  163.2 1.7 %unpack.1 = bf16[768,128]{1,0:T(8,128)(2,1)} custom-call(s32[24]{0:T(128)} %fusion.1.dest, bf16[64,32,128]{2,1,0:T(8,128)(2,1)} %all_to_all.22.returned), custom_call_target="tpu_custom_call" | custom-call | tf_op jit(solution)/shard_map/unpack/pallas_call | solution.py:203
  (25 shorter events, 0.7 us)
Async XLA Ops:
  0.0 19.4 %copy-start.9 = (s32[1536]{0:T(1024)S(1)}, s32[1536]{0:T(1024)}, u32[]{:S(2)}) copy-start(s32[1536]{0:T(1024)} %param.17) | copy-start | bytes 18436
  0.0 19.5 %copy-start.5 = (bf16[128,1024]{1,0:T(8,128)(2,1)S(1)}, bf16[128,1024]{1,0:T(8,128)(2,1)}, u32[]{:S(2)}) copy-start(bf16[128,1024]{1,0:T(8,128)(2,1)} %param.16) | copy-start | bytes 786436
  17.5 4.2 %copy-start.1 = (bf16[4,768,128]{2,1,0:T(8,128)(2,1)}, bf16[4,768,128]{2,1,0:T(8,128)(2,1)S(1)}, u32[]{:S(2)}) copy-start(bf16[4,768,128]{2,1,0:T(8,128)(2,1)S(1)} %all_to_all.20.even) | copy-start | bytes 2359300
  17.5 4.2 %collective-permute-start = (bf16[4,768,128]{2,1,0:T(8,128)(2,1)S(1)}, bf16[4,768,128]{2,1,0:T(8,128)(2,1)S(1)}, u32[]{:S(2)}, u32[]{:S(2)}) collective-permute-start(bf16[4,768,128]{2,1,0:T(8,128)(2,1)S(1)} %all_to_all.20.even), channel_id=1, source_target_pairs={{0,64},{64,0},{128,192},{192,128},{256,320},{320,256},{384,448},{4... | collective-permute-start | bytes 2359304 | tf_op jit(solution)/shard_map/ppermute | solution.py:154
  21.6 0.9 copy-start.2
  26.1 17.0 %copy-start.6 = (bf16[1024,128]{1,0:T(8,128)(2,1)S(1)}, bf16[1024,128]{1,0:T(8,128)(2,1)}, u32[]{:S(2)}) copy-start(bf16[1024,128]{1,0:T(8,128)(2,1)} %param.15) | copy-start | bytes 786436
  26.1 17.0 %copy-start.7 = (bf16[1024,128]{1,0:T(8,128)(2,1)S(1)}, bf16[1024,128]{1,0:T(8,128)(2,1)}, u32[]{:S(2)}) copy-start(bf16[1024,128]{1,0:T(8,128)(2,1)} %param.14) | copy-start | bytes 786436
  26.1 17.0 %copy-start.8 = (bf16[1024,128]{1,0:T(8,128)(2,1)S(1)}, bf16[1024,128]{1,0:T(8,128)(2,1)}, u32[]{:S(2)}) copy-start(bf16[1024,128]{1,0:T(8,128)(2,1)} %param.13) | copy-start | bytes 786436
  26.2 69.4 %all-to-all-start.1 = ((bf16[64,128,128]{2,1,0:T(8,128)(2,1)}), bf16[64,128,128]{2,1,0:T(8,128)(2,1)S(1)}, u32[]{:S(2)}, u32[]{:S(2)}) async-start(bf16[64,128,128]{2,1,0:T(8,128)(2,1)} %pack.1), calls=%async_computation.1 | async-start | bytes 4194304 | tf_op jit(solution)/shard_map/all_to_all | solution.py:164
  44.1 3.6 %collective-permute-start.1 = (bf16[4,128,384]{2,1,0:T(8,128)(2,1)S(1)}, bf16[4,128,384]{2,1,0:T(8,128)(2,1)S(1)}, u32[]{:S(2)}, u32[]{:S(2)}) collective-permute-start(bf16[4,128,384]{2,1,0:T(8,128)(2,1)S(1)} %get-tuple-element.19), channel_id=1, source_target_pairs={{0,64},{64,0},{128,192},{192,128},{256,320},{320,256},{384,448},{4... | collective-permute-start | bytes 1179656 | tf_op jit(solution)/shard_map/ppermute | solution.py:169
  47.7 60.0 %copy-start.4 = (bf16[4,128,384]{2,1,0:T(8,128)(2,1)}, bf16[4,128,384]{2,1,0:T(8,128)(2,1)S(1)}, u32[]{:S(2)}) copy-start(bf16[4,128,384]{2,1,0:T(8,128)(2,1)S(1)} %collective-permute-done.1) | copy-start | bytes 1179652
  95.6 1.3 copy-start
  103.4 4.4 %collective-permute-start.2 = (bf16[1024,384]{1,0:T(8,128)(2,1)}, bf16[1024,384]{1,0:T(8,128)(2,1)S(1)}, u32[]{:S(2)}, u32[]{:S(2)}) collective-permute-start(bf16[1024,384]{1,0:T(8,128)(2,1)} %attention.1.mine), channel_id=1, source_target_pairs={{0,64},{64,0},{128,192},{192,128},{256,320},{320,256},{384,448},{4... | collective-permute-start | bytes 2359304 | tf_op jit(solution)/shard_map/ppermute | solution.py:182
  107.8 0.9 copy-start.3

commit v2 on v1

--- a/solution.py
+++ b/solution.py
@@ -6,6 +6,7 @@
 from jax.experimental import pallas as pl
 from jax.experimental.pallas import tpu as pltpu
 from jax.sharding import PartitionSpec as P
+
 
 HEAD_DIM = 128
 PAGE = 32
@@ -20,44 +21,52 @@
     return lax.dot_general(a, b, (dims, ((), ())), preferred_element_type=jnp.float32)
 
 
-def rows(page):
-    return pl.ds(pl.multiple_of(page * PAGE, PAGE), PAGE)
-
-
-def pack_kernel(dest, core, query, key, value, even, odd, w_out, sent, grad):
-    count = even.shape[0]
+def pack_kernel(dest, query, key, value, sent):
+    for page in range(dest.shape[0]):
+        peer = dest[page]
+        for part, array in enumerate((query, key, value)):
+            sent[peer, part * PAGE : (part + 1) * PAGE] = array[page * PAGE : (page + 1) * PAGE]
+
+
+def grad_kernel(place, here, mine, theirs, w_out, *refs):
+    outs, grad, pages = refs[:-2], refs[-2], refs[-1]
+    count = mine.shape[0]
     total = None
-    for x in range(count):
-        for got, side in ((even, core[0]), (odd, 1 - core[0])):
-            part = mm(got[x], w_out[2 * x + side], ((1,), (1,)))
+    for step in range(count):
+        chip = lax.rem(here[0] - step + count, count)
+        for got, side in ((mine, here[1]), (theirs, 1 - here[1])):
+            part = mm(got[step], w_out[2 * chip + side], ((1,), (0,)))
             total = part if total is None else total + part
     grad[...] = total.astype(grad.dtype)
-    for page in range(dest.shape[0]):
-        peer = dest[page]
-        for part, array in enumerate((query, key, value, grad)):
-            sent[peer, part * PAGE : (part + 1) * PAGE] = array[page * PAGE : (page + 1) * PAGE]
-
-
-def attention_kernel(source, arrived, grads, query, key, value, grad, dkey, dvalue):
+    for page in range(place.shape[0]):
+        pages[place[page]] = grad[page * PAGE : (page + 1) * PAGE]
+    for step, out in enumerate(outs):
+        out[...] = pages[step * out.shape[0] : (step + 1) * out.shape[0]]
+
+
+def turn_kernel(here, *refs):
+    side = len(refs) // 2
+    for step, out in enumerate(refs[side:]):
+        column = lax.rem(here[0] + step, side)
+        for other in range(side):
+            out[other] = refs[other][column]
+
+
+def attention_kernel(source, arrived, *refs):
+    side = len(refs) - 8
+    turned, grads = refs[:side], refs[side]
+    query, key, value, grad, dkey, dvalue, pages = refs[side + 1 :]
     scale = HEAD_DIM ** (-0.5)
-    arrays = (query, key, value, grad)
-
-    def assemble(slot, carry):
-        peer = source[slot]
-
-        @pl.when(peer >= 0)
-        def _():
-            for part, array in enumerate(arrays):
-                array[rows(slot)] = arrived[peer, part * PAGE : (part + 1) * PAGE]
-
-        @pl.when(peer < 0)
-        def _():
-            for array in arrays:
-                array[rows(slot)] = jnp.zeros((PAGE, HEAD_DIM), array.dtype)
-
-        return carry
-
-    lax.fori_loop(0, source.shape[0], assemble, 0)
+    for step, ref in enumerate(turned):
+        pages[step * side : (step + 1) * side] = ref[...]
+    for slot in range(source.shape[0]):
+        code = source[slot]
+        peer, place, live = code & 255, (code >> 8) & 255, code >> 16
+        at = slice(slot * PAGE, (slot + 1) * PAGE)
+        for part, array in enumerate((query, key, value)):
+            array[at] = arrived[peer, part * PAGE : (part + 1) * PAGE]
+        page = pages[place].astype(jnp.float32) * live.astype(jnp.float32)
+        grad[at] = page.astype(grad.dtype)
     total = query.shape[0]
     block = min(BLOCK, total)
     row_order = lax.broadcasted_iota(jnp.int32, (block, block), 0)
@@ -97,25 +106,18 @@
 
 
 def project_kernel(mine, theirs, w_mine, w_theirs, out):
-    total = mm(mine[...], w_mine[...], ((1,), (1,))) + mm(theirs[...], w_theirs[...], ((1,), (1,)))
+    total = mm(mine[...], w_mine[...], ((1,), (0,))) + mm(theirs[...], w_theirs[...], ((1,), (0,)))
     for x in range(out.shape[0]):
         out[x] = total[:, x * HEAD_DIM : (x + 1) * HEAD_DIM].astype(out.dtype)
 
 
 def sum_kernel(source, parts, sent):
-    def one(slot, carry):
-        peer = source[slot]
-
-        @pl.when(peer >= 0)
-        def _():
-            total = parts[0, rows(slot)].astype(jnp.float32)
-            for x in range(1, parts.shape[0]):
-                total = total + parts[x, rows(slot)].astype(jnp.float32)
-            sent[peer] = total.astype(sent.dtype)
-
-        return carry
-
-    lax.fori_loop(0, source.shape[0], one, 0)
+    for slot in reversed(range(source.shape[0])):
+        at = slice(slot * PAGE, (slot + 1) * PAGE)
+        total = parts[0, at].astype(jnp.float32)
+        for x in range(1, parts.shape[0]):
+            total = total + parts[x, at].astype(jnp.float32)
+        sent[source[slot] & 255] = total.astype(sent.dtype)
 
 
 def unpack_kernel(dest, returned, out):
@@ -129,56 +131,103 @@
     peers = lax.axis_size("tok")
     heads = lax.axis_size("head")
     chips = heads // 2
+    side = math.isqrt(peers)
     myself = lax.axis_index("tok")
+    my_z, my_y = myself // side, myself % side
     core = lax.axis_index("head") % 2
-    across = [[2 * x + side for x in range(chips)] for side in range(2)]
+    chip = lax.axis_index("head") // 2
+    across = [[2 * x + c for x in range(chips)] for c in range(2)]
     swap = [(h, h ^ 1) for h in range(heads)]
     slot_rows = SLOTS * PAGE
     half = queries.dtype
 
+    gathered = [out_grad]
+    for d in range(1, chips):
+        pairs = [(h, (h + 2 * d) % heads) for h in range(heads)]
+        gathered.append(lax.ppermute(out_grad, "head", pairs))
+
     table = page_cluster.reshape(peers, pages_here)
     dest = lax.dynamic_index_in_dim(table, myself, 0, keepdims=False)
+    place = ((dest // side - my_z) % side) * side + dest % side
+
+    sent = pl.pallas_call(
+        pack_kernel,
+        out_shape=jax.ShapeDtypeStruct((peers, 3 * PAGE, HEAD_DIM), half),
+        in_specs=[SMEM] + [VMEM] * 3,
+        out_specs=VMEM,
+        name="pack",
+    )(dest, queries, keys, values)
+    sent, w_query, w_key, w_value, page_cluster = lax.optimization_barrier(
+        (sent, w_query, w_key, w_value, page_cluster)
+    )
+    arrived = lax.all_to_all(sent, "tok", 0, 0, tiled=True)
+
+    table = page_cluster.reshape(peers, pages_here)
     has = jnp.any(table == myself, axis=1).astype(jnp.int32)
     peer_order = jnp.arange(peers, dtype=jnp.int32)
     rank = jnp.sum(jnp.where(peer_order[:, None] < peer_order[None, :], has[:, None], 0), axis=0)
     slot_order = jnp.arange(SLOTS, dtype=jnp.int32)
+    first_hit = (rank[None, :] == 0) & (has[None, :] == 1)
     hit = (rank[None, :] == slot_order[:, None]) & (has[None, :] == 1)
-    source = jnp.sum(jnp.where(hit, peer_order[None, :] + 1, 0), axis=1) - 1
-
-    w_blocks = w_out.reshape(HEAD_DIM, heads, HEAD_DIM).transpose(1, 0, 2)
-
-    same_core = lax.all_to_all(
-        jnp.broadcast_to(out_grad[None], (chips, *out_grad.shape)),
-        "head", 0, 0, axis_index_groups=across, tiled=True,
-    )
-    other_core = lax.ppermute(same_core, "head", swap)
-    sent = pl.pallas_call(
-        pack_kernel,
-        out_shape=jax.ShapeDtypeStruct((peers, 4 * PAGE, HEAD_DIM), half),
-        in_specs=[SMEM, SMEM] + [VMEM] * 6,
-        out_specs=VMEM,
-        scratch_shapes=[pltpu.VMEM((tok_rows, HEAD_DIM), half)],
-        name="pack",
-    )(dest, core[None], queries, keys, values, same_core, other_core, w_blocks)
-    sent, w_query, w_key, w_value = lax.optimization_barrier((sent, w_query, w_key, w_value))
-    arrived = lax.all_to_all(sent, "tok", 0, 0, tiled=True)
+    live = (slot_order < jnp.sum(has)).astype(jnp.int32)
+    hit = jnp.where(live[:, None] == 1, hit, first_hit)
+    where_y = (my_y - peer_order % side) % side
+    where_z = (my_z - peer_order // side) % side
+    code = peer_order + (where_y * side + where_z) * 256
+    source = jnp.sum(jnp.where(hit, code[None, :], 0), axis=1) + live * 65536
+
+    mine = jnp.stack(gathered)
+    theirs = lax.ppermute(mine, "head", swap)
+    w_blocks = w_out.reshape(HEAD_DIM, heads, HEAD_DIM).transpose(1, 2, 0)
+    bundle = jax.ShapeDtypeStruct((side, PAGE, HEAD_DIM), half)
+    by_z = pl.pallas_call(
+        grad_kernel,
+        out_shape=[bundle] * side,
+        in_specs=[SMEM, SMEM] + [VMEM] * 3,
+        out_specs=[VMEM] * side,
+        scratch_shapes=[
+            pltpu.VMEM((tok_rows, HEAD_DIM), half),
+            pltpu.VMEM((peers, PAGE, HEAD_DIM), half),
+        ],
+        name="grad",
+    )(place, jnp.stack([chip, core]), mine, theirs, w_blocks)
+    along_z = [by_z[0]]
+    for d in range(1, side):
+        pairs = [(s, (s // side + d) % side * side + s % side) for s in range(peers)]
+        along_z.append(lax.ppermute(by_z[d], "tok", pairs))
+    by_y = pl.pallas_call(
+        turn_kernel,
+        out_shape=[bundle] * side,
+        in_specs=[SMEM] + [VMEM] * side,
+        out_specs=[VMEM] * side,
+        name="turn",
+    )(my_y[None], *along_z)
+    turned = [by_y[0]]
+    for d in range(1, side):
+        pairs = [(s, s // side * side + (s % side + d) % side) for s in range(peers)]
+        turned.append(lax.ppermute(by_y[d], "tok", pairs))
+
     weights = jnp.concatenate([w_query, w_key, w_value], axis=1)
     weights = weights.reshape(chips, 2, HEAD_DIM, 3 * HEAD_DIM)
     w_mine = lax.dynamic_index_in_dim(weights, core, 1, keepdims=False)
     w_away = lax.dynamic_index_in_dim(weights, 1 - core, 1, keepdims=False)
+    w_mine = w_mine.reshape(chips * HEAD_DIM, 3 * HEAD_DIM).T
+    w_away = w_away.reshape(chips * HEAD_DIM, 3 * HEAD_DIM).T
     w_theirs = lax.ppermute(w_away, "head", swap)
-    w_mine = w_mine.reshape(chips * HEAD_DIM, 3 * HEAD_DIM)
-    w_theirs = w_theirs.reshape(chips * HEAD_DIM, 3 * HEAD_DIM)
-    arrived, w_mine, w_theirs = lax.optimization_barrier((arrived, w_mine, w_theirs))
+    arrived, w_mine, w_theirs, source, *turned = lax.optimization_barrier(
+        (arrived, w_mine, w_theirs, source, *turned)
+    )
+
     grads = pl.pallas_call(
         attention_kernel,
         out_shape=jax.ShapeDtypeStruct((slot_rows, 3 * HEAD_DIM), half),
-        in_specs=[SMEM, VMEM],
+        in_specs=[SMEM, VMEM] + [VMEM] * side,
         out_specs=VMEM,
         scratch_shapes=[pltpu.VMEM((slot_rows, HEAD_DIM), half)] * 4
-        + [pltpu.VMEM((slot_rows, HEAD_DIM), jnp.float32)] * 2,
+        + [pltpu.VMEM((slot_rows, HEAD_DIM), jnp.float32)] * 2
+        + [pltpu.VMEM((peers, PAGE, HEAD_DIM), half)],
         name="attention",
-    )(source, arrived)
+    )(source, arrived, *turned)
     their_grads = lax.ppermute(grads, "head", swap)
     step = min(BLOCK, slot_rows)
     row_block = pl.BlockSpec((step, 3 * HEAD_DIM), lambda i: (i, 0))

time: 166 us -> 184 us (1.11)
  starting transfers between devices: 22.4 us -> 92.3 us
  waiting for transfers between devices: 51.9 us -> 7.16 us
  blocking collectives: 63.5 us -> 47.8 us
  other arithmetic: 0.95 us -> 5.32 us
  Pallas kernels: 19.2 us -> 21.5 us
    ppermute x1 -> x18, starting transfers between devices: 1.91 us -> 71.7 us  [the longest x7 30 us: per_device(): along_z.append(lax.ppermute(by_z[d], 'tok', pairs))]
    all_to_all x1, waiting for transfers between devices: 47.8 us -> 0.01 us  [per_device(): arrived = lax.all_to_all(sent, 'tok', 0, 0, tiled=True)]
    all_to_all x1 -> x0, blocking collectives: 16.4 us -> none  [per_device(): lax.all_to_all(jnp.broadcast_to(out_grad[None], (chips, *out_grad.shape))...]
    ppermute x1 -> x18, waiting for transfers between devices: 0.58 us -> 4.69 us  [the longest x7 2.38 us: per_device(): along_z.append(lax.ppermute(by_z[d], 'tok', pairs))]
    pallas_call x1 -> x3, Pallas kernels: 3.62 us -> 7.09 us  [the longest x1 2.83 us: per_device(): pl.pallas_call(grad_kernel, out_shape=[bundle] * side, in_specs=[SMEM, SM...]
    unnamed x21 -> x47, local copies, waits for them, and re-layouts: 3.35 us -> 5.41 us
  transfers between devices with their start and end apart: 4 -> 21, of which waited for: 4 -> 4; matrix products, arithmetic and copies ran while one was open for 2% -> 5% of each run, Pallas kernels for 0% -> 3%
where the time goes in v2:
time: 184 us; the launch traced here: 183 us
  starting transfers between devices  92.3 us (50%)
  blocking collectives  47.8 us (26%)
  Pallas kernels  21.5 us (12%)
  local copies, waits for them, and re-layouts  8.26 us (4%)
  waiting for transfers between devices  7.16 us (4%)
  other arithmetic  5.32 us (3%)
    ppermute x7, starting transfers between devices, per_device(): along_z.append(lax.ppermute(by_z[d], 'tok', pairs))  30 us
    ppermute x7, starting transfers between devices, per_device(): turned.append(lax.ppermute(by_y[d], 'tok', pairs))  29 us
    all_to_all x1, blocking collectives, per_device(): returned = lax.all_to_all(summed, 'tok', 0, 0, tiled=True)  27.8 us
    all_to_all x1, blocking collectives, per_device(): lax.all_to_all(partial, 'head', 0, 0, axis_index_groups=across, tiled=True)  20 us
    all_to_all x1, starting transfers between devices, per_device(): arrived = lax.all_to_all(sent, 'tok', 0, 0, tiled=True)  16.7 us
    ppermute x3, starting transfers between devices, per_device(): gathered.append(lax.ppermute(out_grad, 'head', pairs))  10.8 us
    pallas_call x1, Pallas kernels, per_device(): pl.pallas_call(attention_kernel, out_shape=jax.ShapeDtypeStruct((slot_row...  5.87 us
    unnamed x47, local copies, waits for them, and re-layouts  5.41 us
  transfers between devices with their start and end apart: 21, of which 4 were waited for; matrix products, arithmetic and copies ran while one was open for 5% of the time, Pallas kernels for 3%

profile of v2, /device:TPU:8, one launch (start us, length us, event | category | flops | bytes accessed | tf_op | source)
XLA Modules:
  0.0 183.0 jit_solution(4599804526161584805)
XLA Ops:
  3.7 16.7 %all-to-all-start = ((bf16[64,96,128]{2,1,0:T(8,128)(2,1)}), bf16[64,96,128]{2,1,0:T(8,128)(2,1)S(1)}, u32[]{:S(2)}, u32[]{:S(2)}) async-start(bf16[64,96,128]{2,1,0:T(8,128)(2,1)} %pack.1), calls=%async_computation | async-start | bytes 3145728 | tf_op jit(solution)/shard_map/all_to_all | solution.py:163
  20.5 3.4 %collective-permute-start.1 = (bf16[768,128]{1,0:T(8,128)(2,1)S(1)}, bf16[768,128]{1,0:T(8,128)(2,1)S(1)}, u32[]{:S(2)}, u32[]{:S(2)}) collective-permute-start(bf16[768,128]{1,0:T(8,128)(2,1)S(1)} %copy-done.7), channel_id=1, source_target_pairs={{0,128},{64,192},{128,256},{192,320},{256,384},{320,448},{384,0},{... | collective-permute-start | bytes 589832 | tf_op jit(solution)/shard_map/ppermute | solution.py:147
  23.9 3.7 %collective-permute-start.3 = (bf16[768,128]{1,0:T(8,128)(2,1)S(1)}, bf16[768,128]{1,0:T(8,128)(2,1)}, u32[]{:S(2)}, u32[]{:S(2)}) collective-permute-start(bf16[768,128]{1,0:T(8,128)(2,1)S(1)} %copy-done.7), channel_id=1, source_target_pairs={{0,384},{64,448},{128,0},{192,64},{256,128},{320,192},{384,256},{4... | collective-permute-start | bytes 589832 | tf_op jit(solution)/shard_map/ppermute | solution.py:147
  27.5 3.7 %collective-permute-start.2 = (bf16[768,128]{1,0:T(8,128)(2,1)S(1)}, bf16[768,128]{1,0:T(8,128)(2,1)}, u32[]{:S(2)}, u32[]{:S(2)}) collective-permute-start(bf16[768,128]{1,0:T(8,128)(2,1)S(1)} %copy-done.7), channel_id=1, source_target_pairs={{0,256},{64,320},{128,384},{192,448},{256,0},{320,64},{384,128},{4... | collective-permute-start | bytes 589832 | tf_op jit(solution)/shard_map/ppermute | solution.py:147
  44.2 2.8 %grad.1 = (bf16[8,32,128]{2,1,0:T(8,128)(2,1)}, bf16[8,32,128]{2,1,0:T(8,128)(2,1)}, bf16[8,32,128]{2,1,0:T(8,128)(2,1)}, bf16[8,32,128]{2,1,0:T(8,128)(2,1)}, b...) custom-call(s32[24]{0:T(128)} %get-tuple-element.71.place, ...), custom_call_target="tpu_custom_call" | custom-call | tf_op jit(solution)/shard_map/grad/pallas_call | solution.py:183
  47.0 3.4 %collective-permute-start.5 = (bf16[8,32,128]{2,1,0:T(8,128)(2,1)}, bf16[8,32,128]{2,1,0:T(8,128)(2,1)S(1)}, u32[]{:S(2)}, u32[]{:S(2)}) collective-permute-start(bf16[8,32,128]{2,1,0:T(8,128)(2,1)} %get-tuple-element.44), channel_id=1, source_target_pairs={{0,8},{1,9},{2,10},{3,11},{4,12},{5,13},{6,14},{7,15},{8,16},{9,17... | collective-permute-start | bytes 196616 | tf_op jit(solution)/shard_map/ppermute | solution.py:197
  50.4 4.3 %collective-permute-start.6 = (bf16[8,32,128]{2,1,0:T(8,128)(2,1)}, bf16[8,32,128]{2,1,0:T(8,128)(2,1)S(1)}, u32[]{:S(2)}, u32[]{:S(2)}) collective-permute-start(bf16[8,32,128]{2,1,0:T(8,128)(2,1)} %get-tuple-element.45), channel_id=1, source_target_pairs={{0,16},{1,17},{2,18},{3,19},{4,20},{5,21},{6,22},{7,23},{8,24},{9,... | collective-permute-start | bytes 196616 | tf_op jit(solution)/shard_map/ppermute | solution.py:197
  54.7 4.7 %collective-permute-start.7 = (bf16[8,32,128]{2,1,0:T(8,128)(2,1)}, bf16[8,32,128]{2,1,0:T(8,128)(2,1)S(1)}, u32[]{:S(2)}, u32[]{:S(2)}) collective-permute-start(bf16[8,32,128]{2,1,0:T(8,128)(2,1)} %get-tuple-element.46), channel_id=1, source_target_pairs={{0,24},{1,25},{2,26},{3,27},{4,28},{5,29},{6,30},{7,31},{8,32},{9,... | collective-permute-start | bytes 196616 | tf_op jit(solution)/shard_map/ppermute | solution.py:197
  59.4 4.1 %collective-permute-start.8 = (bf16[8,32,128]{2,1,0:T(8,128)(2,1)}, bf16[8,32,128]{2,1,0:T(8,128)(2,1)S(1)}, u32[]{:S(2)}, u32[]{:S(2)}) collective-permute-start(bf16[8,32,128]{2,1,0:T(8,128)(2,1)} %get-tuple-element.47), channel_id=1, source_target_pairs={{0,32},{1,33},{2,34},{3,35},{4,36},{5,37},{6,38},{7,39},{8,40},{9,... | collective-permute-start | bytes 196616 | tf_op jit(solution)/shard_map/ppermute | solution.py:197
  63.5 4.8 %collective-permute-start.9 = (bf16[8,32,128]{2,1,0:T(8,128)(2,1)}, bf16[8,32,128]{2,1,0:T(8,128)(2,1)S(1)}, u32[]{:S(2)}, u32[]{:S(2)}) collective-permute-start(bf16[8,32,128]{2,1,0:T(8,128)(2,1)} %get-tuple-element.48), channel_id=1, source_target_pairs={{0,40},{1,41},{2,42},{3,43},{4,44},{5,45},{6,46},{7,47},{8,48},{9,... | collective-permute-start | bytes 196616 | tf_op jit(solution)/shard_map/ppermute | solution.py:197
  68.4 5.4 %collective-permute-start.10 = (bf16[8,32,128]{2,1,0:T(8,128)(2,1)}, bf16[8,32,128]{2,1,0:T(8,128)(2,1)S(1)}, u32[]{:S(2)}, u32[]{:S(2)}) collective-permute-start(bf16[8,32,128]{2,1,0:T(8,128)(2,1)} %get-tuple-element.49), channel_id=1, source_target_pairs={{0,48},{1,49},{2,50},{3,51},{4,52},{5,53},{6,54},{7,55},{8,56},{9,... | collective-permute-start | bytes 196616 | tf_op jit(solution)/shard_map/ppermute | solution.py:197
  73.8 3.3 %collective-permute-start.11 = (bf16[8,32,128]{2,1,0:T(8,128)(2,1)}, bf16[8,32,128]{2,1,0:T(8,128)(2,1)S(1)}, u32[]{:S(2)}, u32[]{:S(2)}) collective-permute-start(bf16[8,32,128]{2,1,0:T(8,128)(2,1)} %get-tuple-element.50), channel_id=1, source_target_pairs={{0,56},{1,57},{2,58},{3,59},{4,60},{5,61},{6,62},{7,63},{8,0},{9,1... | collective-permute-start | bytes 196616 | tf_op jit(solution)/shard_map/ppermute | solution.py:197
  82.7 3.4 %collective-permute-start.12 = (bf16[8,32,128]{2,1,0:T(8,128)(2,1)}, bf16[8,32,128]{2,1,0:T(8,128)(2,1)S(1)}, u32[]{:S(2)}, u32[]{:S(2)}) collective-permute-start(bf16[8,32,128]{2,1,0:T(8,128)(2,1)} %get-tuple-element.52), channel_id=1, source_target_pairs={{0,1},{1,2},{2,3},{3,4},{4,5},{5,6},{6,7},{7,0},{8,9},{9,10},{10,1... | collective-permute-start | bytes 196616 | tf_op jit(solution)/shard_map/ppermute | solution.py:208
  86.1 5.5 %collective-permute-start.13 = (bf16[8,32,128]{2,1,0:T(8,128)(2,1)}, bf16[8,32,128]{2,1,0:T(8,128)(2,1)S(1)}, u32[]{:S(2)}, u32[]{:S(2)}) collective-permute-start(bf16[8,32,128]{2,1,0:T(8,128)(2,1)} %get-tuple-element.53), channel_id=1, source_target_pairs={{0,2},{1,3},{2,4},{3,5},{4,6},{5,7},{6,0},{7,1},{8,10},{9,11},{10,... | collective-permute-start | bytes 196616 | tf_op jit(solution)/shard_map/ppermute | solution.py:208
  91.8 2.5 %collective-permute-start.14 = (bf16[8,32,128]{2,1,0:T(8,128)(2,1)}, bf16[8,32,128]{2,1,0:T(8,128)(2,1)S(1)}, u32[]{:S(2)}, u32[]{:S(2)}) collective-permute-start(bf16[8,32,128]{2,1,0:T(8,128)(2,1)} %get-tuple-element.54), channel_id=1, source_target_pairs={{0,3},{1,4},{2,5},{3,6},{4,7},{5,0},{6,1},{7,2},{8,11},{9,12},{10,... | collective-permute-start | bytes 196616 | tf_op jit(solution)/shard_map/ppermute | solution.py:208
  94.3 5.1 %collective-permute-start.15 = (bf16[8,32,128]{2,1,0:T(8,128)(2,1)}, bf16[8,32,128]{2,1,0:T(8,128)(2,1)S(1)}, u32[]{:S(2)}, u32[]{:S(2)}) collective-permute-start(bf16[8,32,128]{2,1,0:T(8,128)(2,1)} %get-tuple-element.55), channel_id=1, source_target_pairs={{0,4},{1,5},{2,6},{3,7},{4,0},{5,1},{6,2},{7,3},{8,12},{9,13},{10,... | collective-permute-start | bytes 196616 | tf_op jit(solution)/shard_map/ppermute | solution.py:208
  99.4 3.7 %collective-permute-start.16 = (bf16[8,32,128]{2,1,0:T(8,128)(2,1)}, bf16[8,32,128]{2,1,0:T(8,128)(2,1)S(1)}, u32[]{:S(2)}, u32[]{:S(2)}) collective-permute-start(bf16[8,32,128]{2,1,0:T(8,128)(2,1)} %get-tuple-element.56), channel_id=1, source_target_pairs={{0,5},{1,6},{2,7},{3,0},{4,1},{5,2},{6,3},{7,4},{8,13},{9,14},{10,... | collective-permute-start | bytes 196616 | tf_op jit(solution)/shard_map/ppermute | solution.py:208
  103.1 4.3 %collective-permute-start.17 = (bf16[8,32,128]{2,1,0:T(8,128)(2,1)}, bf16[8,32,128]{2,1,0:T(8,128)(2,1)S(1)}, u32[]{:S(2)}, u32[]{:S(2)}) collective-permute-start(bf16[8,32,128]{2,1,0:T(8,128)(2,1)} %get-tuple-element.57), channel_id=1, source_target_pairs={{0,6},{1,7},{2,0},{3,1},{4,2},{5,3},{6,4},{7,5},{8,14},{9,15},{10,... | collective-permute-start | bytes 196616 | tf_op jit(solution)/shard_map/ppermute | solution.py:208
  107.5 4.6 %collective-permute-start.18 = (bf16[8,32,128]{2,1,0:T(8,128)(2,1)}, bf16[8,32,128]{2,1,0:T(8,128)(2,1)S(1)}, u32[]{:S(2)}, u32[]{:S(2)}) collective-permute-start(bf16[8,32,128]{2,1,0:T(8,128)(2,1)} %get-tuple-element.58), channel_id=1, source_target_pairs={{0,7},{1,0},{2,1},{3,2},{4,3},{5,4},{6,5},{7,6},{8,15},{9,8},{10,9... | collective-permute-start | bytes 196616 | tf_op jit(solution)/shard_map/ppermute | solution.py:208
  115.5 5.9 %attention.1.mine = bf16[1024,384]{1,0:T(8,128)(2,1)} custom-call(s32[32]{0:T(128)} %fusion.2.source, bf16[64,96,128]{2,1,0:T(8,128)(2,1)} %copy-done, bf16[8,32,128]{2,1,0:T(8,128)(2,1)} %get-tuple-element.61.refs_0_, bf16[8,32,128]{2,1,0:T(8,128)(2,1)} %copy-done.8, bf16[8,32,128]{2,1,0:T(8,128)(2,1)} %copy-done.9, bf16[8,32,128]{2,1,0:T(8,128)(2,1)} %copy-done.11, ...), custom_call_target="tpu_custom_call" | custom-call | tf_op jit(solution)/shard_map/attention/pallas_call | solution.py:221
  123.3 2.5 %collective-permute-done.19.theirs = bf16[1024,384]{1,0:T(8,128)(2,1)S(1)} collective-permute-done((bf16[1024,384]{1,0:T(8,128)(2,1)}, bf16[1024,384]{1,0:T(8,128)(2,1)S(1)}, u32[]{:S(2)}, u32[]{:S(2)}) %collective-permute-start.19) | collective-permute-done | bytes 786464 | tf_op jit(solution)/shard_map/ppermute | solution.py:231
  126.6 4.7 %project.1 = bf16[4,1024,128]{2,1,0:T(8,128)(2,1)} custom-call(bf16[1024,384]{1,0:T(8,128)(2,1)} %attention.1.mine, bf16[1024,384]{1,0:T(8,128)(2,1)} %copy-done.3, bf16[384,512]{1,0:T(8,128)(2,1)} %bitcast.21, bf16[384,512]{1,0:T(8,128)(2,1)} %collective-permute-done.w_theirs), custom_call_target="tpu_custom_call" | custom-call | tf_op jit(solution)/shard_map/project/pallas_call | solution.py:235
  131.3 20.0 %all_to_all.15.parts = bf16[4,1024,128]{2,1,0:T(8,128)(2,1)} all-to-all(bf16[4,1024,128]{2,1,0:T(8,128)(2,1)} %project.1), channel_id=1, replica_groups={{0,128,256,384},{64,192,320,448},{1,129,257,385},{65,193,321,449},{2,13..., dimensions={0} | all-to-all | bytes 2097152 | tf_op jit(solution)/shard_map/all_to_all | solution.py:243
  153.4 27.8 %all_to_all.16.returned = bf16[64,32,128]{2,1,0:T(8,128)(2,1)} all-to-all(bf16[64,32,128]{2,1,0:T(8,128)(2,1)} %sum.1), channel_id=1, replica_groups=mesh['head'=8,'tok'=64] {'tok'}, dimensions={0} | all-to-all | bytes 1048576 | tf_op jit(solution)/shard_map/all_to_all | solution.py:251
  (93 shorter events, 32.2 us)
Async XLA Ops:
  3.7 27.6 %copy-start.4 = (bf16[1024,128]{1,0:T(8,128)(2,1)S(1)}, bf16[1024,128]{1,0:T(8,128)(2,1)}, u32[]{:S(2)}) copy-start(bf16[1024,128]{1,0:T(8,128)(2,1)} %param.15) | copy-start | bytes 786436
  3.7 27.6 %copy-start.5 = (bf16[1024,128]{1,0:T(8,128)(2,1)S(1)}, bf16[1024,128]{1,0:T(8,128)(2,1)}, u32[]{:S(2)}) copy-start(bf16[1024,128]{1,0:T(8,128)(2,1)} %param.14) | copy-start | bytes 786436
  3.7 27.6 %copy-start.6 = (bf16[1024,128]{1,0:T(8,128)(2,1)S(1)}, bf16[1024,128]{1,0:T(8,128)(2,1)}, u32[]{:S(2)}) copy-start(bf16[1024,128]{1,0:T(8,128)(2,1)} %param.13) | copy-start | bytes 786436
  3.7 110.5 %all-to-all-start = ((bf16[64,96,128]{2,1,0:T(8,128)(2,1)}), bf16[64,96,128]{2,1,0:T(8,128)(2,1)S(1)}, u32[]{:S(2)}, u32[]{:S(2)}) async-start(bf16[64,96,128]{2,1,0:T(8,128)(2,1)} %pack.1), calls=%async_computation | async-start | bytes 3145728 | tf_op jit(solution)/shard_map/all_to_all | solution.py:163
  20.5 14.0 %collective-permute-start.1 = (bf16[768,128]{1,0:T(8,128)(2,1)S(1)}, bf16[768,128]{1,0:T(8,128)(2,1)S(1)}, u32[]{:S(2)}, u32[]{:S(2)}) collective-permute-start(bf16[768,128]{1,0:T(8,128)(2,1)S(1)} %copy-done.7), channel_id=1, source_target_pairs={{0,128},{64,192},{128,256},{192,320},{256,384},{320,448},{384,0},{... | collective-permute-start | bytes 589832 | tf_op jit(solution)/shard_map/ppermute | solution.py:147
  23.9 11.2 %collective-permute-start.3 = (bf16[768,128]{1,0:T(8,128)(2,1)S(1)}, bf16[768,128]{1,0:T(8,128)(2,1)}, u32[]{:S(2)}, u32[]{:S(2)}) collective-permute-start(bf16[768,128]{1,0:T(8,128)(2,1)S(1)} %copy-done.7), channel_id=1, source_target_pairs={{0,384},{64,448},{128,0},{192,64},{256,128},{320,192},{384,256},{4... | collective-permute-start | bytes 589832 | tf_op jit(solution)/shard_map/ppermute | solution.py:147
  27.5 9.2 %collective-permute-start.2 = (bf16[768,128]{1,0:T(8,128)(2,1)S(1)}, bf16[768,128]{1,0:T(8,128)(2,1)}, u32[]{:S(2)}, u32[]{:S(2)}) collective-permute-start(bf16[768,128]{1,0:T(8,128)(2,1)S(1)} %copy-done.7), channel_id=1, source_target_pairs={{0,256},{64,320},{128,384},{192,448},{256,0},{320,64},{384,128},{4... | collective-permute-start | bytes 589832 | tf_op jit(solution)/shard_map/ppermute | solution.py:147
  32.5 66.9 %collective-permute-start = (bf16[384,512]{1,0:T(8,128)(2,1)}, bf16[384,512]{1,0:T(8,128)(2,1)}, u32[]{:S(2)}, u32[]{:S(2)}) collective-permute-start(bf16[384,512]{1,0:T(8,128)(2,1)} %bitcast.3), channel_id=1, source_target_pairs={{0,64},{64,0},{128,192},{192,128},{256,320},{320,256},{384,448},{4... | collective-permute-start | bytes 1179656 | tf_op jit(solution)/shard_map/ppermute | solution.py:216
  37.8 5.4 %collective-permute-start.4 = (bf16[4,768,128]{2,1,0:T(8,128)(2,1)S(1)}, bf16[4,768,128]{2,1,0:T(8,128)(2,1)S(1)}, u32[]{:S(2)}, u32[]{:S(2)}) collective-permute-start(bf16[4,768,128]{2,1,0:T(8,128)(2,1)S(1)} %pad_maximum_fusion.1.mine), channel_id=1, source_target_pairs={{0,64},{64,0},{128,192},{192,128},{256,320},{320,256},{384,448},{4... | collective-permute-start | bytes 2359304 | tf_op jit(solution)/shard_map/ppermute | solution.py:180
  47.0 16.5 %collective-permute-start.5 = (bf16[8,32,128]{2,1,0:T(8,128)(2,1)}, bf16[8,32,128]{2,1,0:T(8,128)(2,1)S(1)}, u32[]{:S(2)}, u32[]{:S(2)}) collective-permute-start(bf16[8,32,128]{2,1,0:T(8,128)(2,1)} %get-tuple-element.44), channel_id=1, source_target_pairs={{0,8},{1,9},{2,10},{3,11},{4,12},{5,13},{6,14},{7,15},{8,16},{9,17... | collective-permute-start | bytes 196616 | tf_op jit(solution)/shard_map/ppermute | solution.py:197
  50.4 18.0 %collective-permute-start.6 = (bf16[8,32,128]{2,1,0:T(8,128)(2,1)}, bf16[8,32,128]{2,1,0:T(8,128)(2,1)S(1)}, u32[]{:S(2)}, u32[]{:S(2)}) collective-permute-start(bf16[8,32,128]{2,1,0:T(8,128)(2,1)} %get-tuple-element.45), channel_id=1, source_target_pairs={{0,16},{1,17},{2,18},{3,19},{4,20},{5,21},{6,22},{7,23},{8,24},{9,... | collective-permute-start | bytes 196616 | tf_op jit(solution)/shard_map/ppermute | solution.py:197
  54.7 19.1 %collective-permute-start.7 = (bf16[8,32,128]{2,1,0:T(8,128)(2,1)}, bf16[8,32,128]{2,1,0:T(8,128)(2,1)S(1)}, u32[]{:S(2)}, u32[]{:S(2)}) collective-permute-start(bf16[8,32,128]{2,1,0:T(8,128)(2,1)} %get-tuple-element.46), channel_id=1, source_target_pairs={{0,24},{1,25},{2,26},{3,27},{4,28},{5,29},{6,30},{7,31},{8,32},{9,... | collective-permute-start | bytes 196616 | tf_op jit(solution)/shard_map/ppermute | solution.py:197
  59.4 18.3 %collective-permute-start.8 = (bf16[8,32,128]{2,1,0:T(8,128)(2,1)}, bf16[8,32,128]{2,1,0:T(8,128)(2,1)S(1)}, u32[]{:S(2)}, u32[]{:S(2)}) collective-permute-start(bf16[8,32,128]{2,1,0:T(8,128)(2,1)} %get-tuple-element.47), channel_id=1, source_target_pairs={{0,32},{1,33},{2,34},{3,35},{4,36},{5,37},{6,38},{7,39},{8,40},{9,... | collective-permute-start | bytes 196616 | tf_op jit(solution)/shard_map/ppermute | solution.py:197
  63.5 14.2 %collective-permute-start.9 = (bf16[8,32,128]{2,1,0:T(8,128)(2,1)}, bf16[8,32,128]{2,1,0:T(8,128)(2,1)S(1)}, u32[]{:S(2)}, u32[]{:S(2)}) collective-permute-start(bf16[8,32,128]{2,1,0:T(8,128)(2,1)} %get-tuple-element.48), channel_id=1, source_target_pairs={{0,40},{1,41},{2,42},{3,43},{4,44},{5,45},{6,46},{7,47},{8,48},{9,... | collective-permute-start | bytes 196616 | tf_op jit(solution)/shard_map/ppermute | solution.py:197
  68.4 9.4 %collective-permute-start.10 = (bf16[8,32,128]{2,1,0:T(8,128)(2,1)}, bf16[8,32,128]{2,1,0:T(8,128)(2,1)S(1)}, u32[]{:S(2)}, u32[]{:S(2)}) collective-permute-start(bf16[8,32,128]{2,1,0:T(8,128)(2,1)} %get-tuple-element.49), channel_id=1, source_target_pairs={{0,48},{1,49},{2,50},{3,51},{4,52},{5,53},{6,54},{7,55},{8,56},{9,... | collective-permute-start | bytes 196616 | tf_op jit(solution)/shard_map/ppermute | solution.py:197
  73.8 6.4 %collective-permute-start.11 = (bf16[8,32,128]{2,1,0:T(8,128)(2,1)}, bf16[8,32,128]{2,1,0:T(8,128)(2,1)S(1)}, u32[]{:S(2)}, u32[]{:S(2)}) collective-permute-start(bf16[8,32,128]{2,1,0:T(8,128)(2,1)} %get-tuple-element.50), channel_id=1, source_target_pairs={{0,56},{1,57},{2,58},{3,59},{4,60},{5,61},{6,62},{7,63},{8,0},{9,1... | collective-permute-start | bytes 196616 | tf_op jit(solution)/shard_map/ppermute | solution.py:197
  82.7 20.4 %collective-permute-start.12 = (bf16[8,32,128]{2,1,0:T(8,128)(2,1)}, bf16[8,32,128]{2,1,0:T(8,128)(2,1)S(1)}, u32[]{:S(2)}, u32[]{:S(2)}) collective-permute-start(bf16[8,32,128]{2,1,0:T(8,128)(2,1)} %get-tuple-element.52), channel_id=1, source_target_pairs={{0,1},{1,2},{2,3},{3,4},{4,5},{5,6},{6,7},{7,0},{8,9},{9,10},{10,1... | collective-permute-start | bytes 196616 | tf_op jit(solution)/shard_map/ppermute | solution.py:208
  86.1 21.4 %collective-permute-start.13 = (bf16[8,32,128]{2,1,0:T(8,128)(2,1)}, bf16[8,32,128]{2,1,0:T(8,128)(2,1)S(1)}, u32[]{:S(2)}, u32[]{:S(2)}) collective-permute-start(bf16[8,32,128]{2,1,0:T(8,128)(2,1)} %get-tuple-element.53), channel_id=1, source_target_pairs={{0,2},{1,3},{2,4},{3,5},{4,6},{5,7},{6,0},{7,1},{8,10},{9,11},{10,... | collective-permute-start | bytes 196616 | tf_op jit(solution)/shard_map/ppermute | solution.py:208
  91.8 22.4 %collective-permute-start.14 = (bf16[8,32,128]{2,1,0:T(8,128)(2,1)}, bf16[8,32,128]{2,1,0:T(8,128)(2,1)S(1)}, u32[]{:S(2)}, u32[]{:S(2)}) collective-permute-start(bf16[8,32,128]{2,1,0:T(8,128)(2,1)} %get-tuple-element.54), channel_id=1, source_target_pairs={{0,3},{1,4},{2,5},{3,6},{4,7},{5,0},{6,1},{7,2},{8,11},{9,12},{10,... | collective-permute-start | bytes 196616 | tf_op jit(solution)/shard_map/ppermute | solution.py:208
  94.3 19.9 %collective-permute-start.15 = (bf16[8,32,128]{2,1,0:T(8,128)(2,1)}, bf16[8,32,128]{2,1,0:T(8,128)(2,1)S(1)}, u32[]{:S(2)}, u32[]{:S(2)}) collective-permute-start(bf16[8,32,128]{2,1,0:T(8,128)(2,1)} %get-tuple-element.55), channel_id=1, source_target_pairs={{0,4},{1,5},{2,6},{3,7},{4,0},{5,1},{6,2},{7,3},{8,12},{9,13},{10,... | collective-permute-start | bytes 196616 | tf_op jit(solution)/shard_map/ppermute | solution.py:208
  99.4 14.8 %collective-permute-start.16 = (bf16[8,32,128]{2,1,0:T(8,128)(2,1)}, bf16[8,32,128]{2,1,0:T(8,128)(2,1)S(1)}, u32[]{:S(2)}, u32[]{:S(2)}) collective-permute-start(bf16[8,32,128]{2,1,0:T(8,128)(2,1)} %get-tuple-element.56), channel_id=1, source_target_pairs={{0,5},{1,6},{2,7},{3,0},{4,1},{5,2},{6,3},{7,4},{8,13},{9,14},{10,... | collective-permute-start | bytes 196616 | tf_op jit(solution)/shard_map/ppermute | solution.py:208
  103.1 11.1 %collective-permute-start.17 = (bf16[8,32,128]{2,1,0:T(8,128)(2,1)}, bf16[8,32,128]{2,1,0:T(8,128)(2,1)S(1)}, u32[]{:S(2)}, u32[]{:S(2)}) collective-permute-start(bf16[8,32,128]{2,1,0:T(8,128)(2,1)} %get-tuple-element.57), channel_id=1, source_target_pairs={{0,6},{1,7},{2,0},{3,1},{4,2},{5,3},{6,4},{7,5},{8,14},{9,15},{10,... | collective-permute-start | bytes 196616 | tf_op jit(solution)/shard_map/ppermute | solution.py:208
  107.5 6.8 %collective-permute-start.18 = (bf16[8,32,128]{2,1,0:T(8,128)(2,1)}, bf16[8,32,128]{2,1,0:T(8,128)(2,1)S(1)}, u32[]{:S(2)}, u32[]{:S(2)}) collective-permute-start(bf16[8,32,128]{2,1,0:T(8,128)(2,1)} %get-tuple-element.58), channel_id=1, source_target_pairs={{0,7},{1,0},{2,1},{3,2},{4,3},{5,4},{6,5},{7,6},{8,15},{9,8},{10,9... | collective-permute-start | bytes 196616 | tf_op jit(solution)/shard_map/ppermute | solution.py:208
  121.3 4.4 %collective-permute-start.19 = (bf16[1024,384]{1,0:T(8,128)(2,1)}, bf16[1024,384]{1,0:T(8,128)(2,1)S(1)}, u32[]{:S(2)}, u32[]{:S(2)}) collective-permute-start(bf16[1024,384]{1,0:T(8,128)(2,1)} %attention.1.mine), channel_id=1, source_target_pairs={{0,64},{64,0},{128,192},{192,128},{256,320},{320,256},{384,448},{4... | collective-permute-start | bytes 2359304 | tf_op jit(solution)/shard_map/ppermute | solution.py:231
  (20 other events, 97.4 us)

commit v3 on v1

--- a/solution.py
+++ b/solution.py
@@ -20,8 +20,8 @@
     return lax.dot_general(a, b, (dims, ((), ())), preferred_element_type=jnp.float32)
 
 
-def rows(page):
-    return pl.ds(pl.multiple_of(page * PAGE, PAGE), PAGE)
+def small(mib):
+    return pltpu.CompilerParams(vmem_limit_bytes=mib * 1024 * 1024)
 
 
 def pack_kernel(dest, core, query, key, value, even, odd, w_out, sent, grad):
@@ -29,7 +29,7 @@
     total = None
     for x in range(count):
         for got, side in ((even, core[0]), (odd, 1 - core[0])):
-            part = mm(got[x], w_out[2 * x + side], ((1,), (1,)))
+            part = mm(got[x], w_out[2 * x + side], ((1,), (0,)))
             total = part if total is None else total + part
     grad[...] = total.astype(grad.dtype)
     for page in range(dest.shape[0]):
@@ -40,24 +40,13 @@
 
 def attention_kernel(source, arrived, grads, query, key, value, grad, dkey, dvalue):
     scale = HEAD_DIM ** (-0.5)
-    arrays = (query, key, value, grad)
-
-    def assemble(slot, carry):
-        peer = source[slot]
-
-        @pl.when(peer >= 0)
-        def _():
-            for part, array in enumerate(arrays):
-                array[rows(slot)] = arrived[peer, part * PAGE : (part + 1) * PAGE]
-
-        @pl.when(peer < 0)
-        def _():
-            for array in arrays:
-                array[rows(slot)] = jnp.zeros((PAGE, HEAD_DIM), array.dtype)
-
-        return carry
-
-    lax.fori_loop(0, source.shape[0], assemble, 0)
+    for slot in range(source.shape[0]):
+        peer, live = source[slot] & 255, source[slot] >> 8
+        at = slice(slot * PAGE, (slot + 1) * PAGE)
+        for part, array in enumerate((query, key, value)):
+            array[at] = arrived[peer, part * PAGE : (part + 1) * PAGE]
+        page = arrived[peer, 3 * PAGE : 4 * PAGE].astype(jnp.float32) * live.astype(jnp.float32)
+        grad[at] = page.astype(grad.dtype)
     total = query.shape[0]
     block = min(BLOCK, total)
     row_order = lax.broadcasted_iota(jnp.int32, (block, block), 0)
@@ -97,25 +86,24 @@
 
 
 def project_kernel(mine, theirs, w_mine, w_theirs, out):
-    total = mm(mine[...], w_mine[...], ((1,), (1,))) + mm(theirs[...], w_theirs[...], ((1,), (1,)))
-    for x in range(out.shape[0]):
-        out[x] = total[:, x * HEAD_DIM : (x + 1) * HEAD_DIM].astype(out.dtype)
+    total_rows = mine.shape[0]
+    step = min(BLOCK, total_rows)
+    for first in range(0, total_rows, step):
+        here = slice(first, first + step)
+        for x in range(out.shape[0]):
+            cols = slice(x * HEAD_DIM, (x + 1) * HEAD_DIM)
+            total = mm(mine[here], w_mine[:, cols], ((1,), (0,)))
+            total += mm(theirs[here], w_theirs[:, cols], ((1,), (0,)))
+            out[x, here] = total.astype(out.dtype)
 
 
 def sum_kernel(source, parts, sent):
-    def one(slot, carry):
-        peer = source[slot]
-
-        @pl.when(peer >= 0)
-        def _():
-            total = parts[0, rows(slot)].astype(jnp.float32)
-            for x in range(1, parts.shape[0]):
-                total = total + parts[x, rows(slot)].astype(jnp.float32)
-            sent[peer] = total.astype(sent.dtype)
-
-        return carry
-
-    lax.fori_loop(0, source.shape[0], one, 0)
+    for slot in reversed(range(source.shape[0])):
+        at = slice(slot * PAGE, (slot + 1) * PAGE)
+        total = parts[0, at].astype(jnp.float32)
+        for x in range(1, parts.shape[0]):
+            total = total + parts[x, at].astype(jnp.float32)
+        sent[source[slot] & 255] = total.astype(sent.dtype)
 
 
 def unpack_kernel(dest, returned, out):
@@ -138,14 +126,7 @@
 
     table = page_cluster.reshape(peers, pages_here)
     dest = lax.dynamic_index_in_dim(table, myself, 0, keepdims=False)
-    has = jnp.any(table == myself, axis=1).astype(jnp.int32)
-    peer_order = jnp.arange(peers, dtype=jnp.int32)
-    rank = jnp.sum(jnp.where(peer_order[:, None] < peer_order[None, :], has[:, None], 0), axis=0)
-    slot_order = jnp.arange(SLOTS, dtype=jnp.int32)
-    hit = (rank[None, :] == slot_order[:, None]) & (has[None, :] == 1)
-    source = jnp.sum(jnp.where(hit, peer_order[None, :] + 1, 0), axis=1) - 1
-
-    w_blocks = w_out.reshape(HEAD_DIM, heads, HEAD_DIM).transpose(1, 0, 2)
+    w_blocks = w_out.reshape(HEAD_DIM, heads, HEAD_DIM).transpose(1, 2, 0)
 
     same_core = lax.all_to_all(
         jnp.broadcast_to(out_grad[None], (chips, *out_grad.shape)),
@@ -158,18 +139,32 @@
         in_specs=[SMEM, SMEM] + [VMEM] * 6,
         out_specs=VMEM,
         scratch_shapes=[pltpu.VMEM((tok_rows, HEAD_DIM), half)],
+        compiler_params=small(12),
         name="pack",
     )(dest, core[None], queries, keys, values, same_core, other_core, w_blocks)
-    sent, w_query, w_key, w_value = lax.optimization_barrier((sent, w_query, w_key, w_value))
+    sent, w_query, w_key, w_value, page_cluster = lax.optimization_barrier(
+        (sent, w_query, w_key, w_value, page_cluster)
+    )
     arrived = lax.all_to_all(sent, "tok", 0, 0, tiled=True)
+    table = page_cluster.reshape(peers, pages_here)
+    has = jnp.any(table == myself, axis=1).astype(jnp.int32)
+    peer_order = jnp.arange(peers, dtype=jnp.int32)
+    rank = jnp.sum(jnp.where(peer_order[:, None] < peer_order[None, :], has[:, None], 0), axis=0)
+    slot_order = jnp.arange(SLOTS, dtype=jnp.int32)
+    live = (slot_order < jnp.sum(has)).astype(jnp.int32)
+    wanted = jnp.where(live == 1, slot_order, 0)
+    hit = (rank[None, :] == wanted[:, None]) & (has[None, :] == 1)
+    source = jnp.sum(jnp.where(hit, peer_order[None, :], 0), axis=1) + live * 256
     weights = jnp.concatenate([w_query, w_key, w_value], axis=1)
     weights = weights.reshape(chips, 2, HEAD_DIM, 3 * HEAD_DIM)
     w_mine = lax.dynamic_index_in_dim(weights, core, 1, keepdims=False)
     w_away = lax.dynamic_index_in_dim(weights, 1 - core, 1, keepdims=False)
+    w_mine = w_mine.reshape(chips * HEAD_DIM, 3 * HEAD_DIM).T
+    w_away = w_away.reshape(chips * HEAD_DIM, 3 * HEAD_DIM).T
     w_theirs = lax.ppermute(w_away, "head", swap)
-    w_mine = w_mine.reshape(chips * HEAD_DIM, 3 * HEAD_DIM)
-    w_theirs = w_theirs.reshape(chips * HEAD_DIM, 3 * HEAD_DIM)
-    arrived, w_mine, w_theirs = lax.optimization_barrier((arrived, w_mine, w_theirs))
+    arrived, w_mine, w_theirs, source = lax.optimization_barrier(
+        (arrived, w_mine, w_theirs, source)
+    )
     grads = pl.pallas_call(
         attention_kernel,
         out_shape=jax.ShapeDtypeStruct((slot_rows, 3 * HEAD_DIM), half),
@@ -177,18 +172,16 @@
         out_specs=VMEM,
         scratch_shapes=[pltpu.VMEM((slot_rows, HEAD_DIM), half)] * 4
         + [pltpu.VMEM((slot_rows, HEAD_DIM), jnp.float32)] * 2,
+        compiler_params=small(24),
         name="attention",
     )(source, arrived)
     their_grads = lax.ppermute(grads, "head", swap)
-    step = min(BLOCK, slot_rows)
-    row_block = pl.BlockSpec((step, 3 * HEAD_DIM), lambda i: (i, 0))
-    w_block = pl.BlockSpec(w_mine.shape, lambda i: (0, 0))
     partial = pl.pallas_call(
         project_kernel,
         out_shape=jax.ShapeDtypeStruct((chips, slot_rows, HEAD_DIM), half),
-        grid=(slot_rows // step,),
-        in_specs=[row_block, row_block, w_block, w_block],
-        out_specs=pl.BlockSpec((chips, step, HEAD_DIM), lambda i: (0, i, 0)),
+        in_specs=[VMEM] * 4,
+        out_specs=VMEM,
+        compiler_params=small(12),
         name="project",
     )(grads, their_grads, w_mine, w_theirs)
     parts = lax.all_to_all(partial, "head", 0, 0, axis_index_groups=across, tiled=True)
@@ -197,6 +190,7 @@
         out_shape=jax.ShapeDtypeStruct((peers, PAGE, HEAD_DIM), half),
         in_specs=[SMEM, VMEM],
         out_specs=VMEM,
+        compiler_params=small(8),
         name="sum",
     )(source, parts)
     returned = lax.all_to_all(summed, "tok", 0, 0, tiled=True)
@@ -205,6 +199,7 @@
         out_shape=jax.ShapeDtypeStruct((tok_rows, HEAD_DIM), half),
         in_specs=[SMEM, VMEM],
         out_specs=VMEM,
+        compiler_params=small(8),
         name="unpack",
     )(dest, returned)
 

time: 166 us -> 151 us (0.910)
  Pallas kernels: 19.2 us -> 10.2 us
  local copies, waits for them, and re-layouts: 6.74 us -> 2.73 us
  blocking collectives: 63.5 us -> 61.4 us
    unnamed x21 -> x17, local copies, waits for them, and re-layouts: 3.35 us -> 0.21 us
    pallas_call x1, Pallas kernels: 4.74 us -> 1.83 us  [per_device(): pl.pallas_call(project_kernel, out_shape=jax.ShapeDtypeStruct((chips, slo...]
    pallas_call x1, Pallas kernels: 6.46 us -> 3.94 us  [per_device(): pl.pallas_call(attention_kernel, out_shape=jax.ShapeDtypeStruct((slot_row...]
    pallas_call x1, Pallas kernels: 2.61 us -> 0.67 us  [per_device(): pl.pallas_call(sum_kernel, out_shape=jax.ShapeDtypeStruct((peers, PAGE, H...]
    all_to_all x1, blocking collectives: 20 us -> 18.1 us  [per_device(): lax.all_to_all(partial, 'head', 0, 0, axis_index_groups=across, tiled=True)]
  transfers between devices with their start and end apart: 4 -> 4, of which waited for: 4 -> 3; matrix products, arithmetic and copies ran while one was open for 2% -> 3% of each run, Pallas kernels for 0% -> 0%
where the time goes in v3:
time: 151 us
  blocking collectives  61.4 us (41%)
  waiting for transfers between devices  51.1 us (34%)
  starting transfers between devices  22.4 us (15%)
  Pallas kernels  10.2 us (7%)
  local copies, waits for them, and re-layouts  2.73 us (2%)
  other arithmetic  2.45 us (2%)
    all_to_all x1, waiting for transfers between devices, per_device(): arrived = lax.all_to_all(sent, 'tok', 0, 0, tiled=True)  46.9 us
    all_to_all x1, blocking collectives, per_device(): returned = lax.all_to_all(summed, 'tok', 0, 0, tiled=True)  27 us
    all_to_all x1, blocking collectives, per_device(): lax.all_to_all(partial, 'head', 0, 0, axis_index_groups=across, tiled=True)  18.1 us
    all_to_all x1, starting transfers between devices, per_device(): arrived = lax.all_to_all(sent, 'tok', 0, 0, tiled=True)  16.7 us
    all_to_all x1, blocking collectives, per_device(): lax.all_to_all(jnp.broadcast_to(out_grad[None], (chips, *out_grad.shape))...  16.4 us
    pallas_call x1, Pallas kernels, per_device(): pl.pallas_call(attention_kernel, out_shape=jax.ShapeDtypeStruct((slot_row...  3.94 us
  transfers between devices with their start and end apart: 4, of which 3 were waited for; matrix products, arithmetic and copies ran while one was open for 3% of the time, Pallas kernels for 0%

profile of v3, /device:TPU:8, one launch (start us, length us, event | category | flops | bytes accessed | tf_op | source)
XLA Modules:
  0.0 150.5 jit_solution(8380822979060057475)
XLA Ops:
  0.0 1.1 broadcast_in_dim.45
  1.1 16.4 %all_to_all.20.even = bf16[4,768,128]{2,1,0:T(8,128)(2,1)S(1)} all-to-all(bf16[4,768,128]{2,1,0:T(8,128)(2,1)S(1)} %broadcast_in_dim.45), channel_id=1, replica_groups={{0,128,256,384},{64,192,320,448},{1,129,257,385},{65,193,321,449},{2,13..., dimensions={0} | all-to-all | bytes 1572864 | tf_op jit(solution)/shard_map/all_to_all | solution.py:131
  17.5 1.9 %collective-permute-start = (bf16[4,768,128]{2,1,0:T(8,128)(2,1)S(1)}, bf16[4,768,128]{2,1,0:T(8,128)(2,1)S(1)}, u32[]{:S(2)}, u32[]{:S(2)}) collective-permute-start(bf16[4,768,128]{2,1,0:T(8,128)(2,1)S(1)} %all_to_all.20.even), channel_id=1, source_target_pairs={{0,64},{64,0},{128,192},{192,128},{256,320},{320,256},{384,448},{4... | collective-permute-start | bytes 2359304 | tf_op jit(solution)/shard_map/ppermute | solution.py:135
  19.5 0.2 copy.16
  19.8 1.9 %collective-permute-done.odd = bf16[4,768,128]{2,1,0:T(8,128)(2,1)S(1)} collective-permute-done((bf16[4,768,128]{2,1,0:T(8,128)(2,1)S(1)}, bf16[4,768,128]{2,1,0:T(8,128)(2,1)S(1)}, u32[]{:S(2)}, u32[]{:S(2)}) %collective-permute-start) | collective-permute-done | bytes 786464 | tf_op jit(solution)/shard_map/ppermute | solution.py:135
  21.7 2.5 %pack.1 = bf16[64,128,128]{2,1,0:T(8,128)(2,1)} custom-call(s32[24]{0:T(128)S(1)} %fusion.1.dest, s32[1]{0:T(128)} %bitcast.1.core, bf16[768,128]{1,0:T(8,128)(2,1)S(1)} %copy-done, bf16[768,128]{1,0:T(8,128)(2,1)S(1)} %copy-done.1, bf16[768,128]{1,0:T(8,128)(2,1)S(1)} %copy-done.2, bf16[4,768,128]{2,1,0:T(8,128)(2,1)S(1)} %all_to_all.20.even, ...), custom_call_target="tpu_custom_call" | custom-call | tf_op jit(solution)/shard_map/pack/pallas_call | solution.py:136
  24.2 16.7 %all-to-all-start.1 = ((bf16[64,128,128]{2,1,0:T(8,128)(2,1)}), bf16[64,128,128]{2,1,0:T(8,128)(2,1)S(1)}, u32[]{:S(2)}, u32[]{:S(2)}) async-start(bf16[64,128,128]{2,1,0:T(8,128)(2,1)} %pack.1), calls=%async_computation.1 | async-start | bytes 4194304 | tf_op jit(solution)/shard_map/all_to_all | solution.py:148
  41.2 0.9 copy.22
  42.1 1.9 %collective-permute-start.1 = (bf16[384,512]{1,0:T(8,128)(2,1)}, bf16[384,512]{1,0:T(8,128)(2,1)S(1)}, u32[]{:S(2)}, u32[]{:S(2)}) collective-permute-start(bf16[384,512]{1,0:T(8,128)(2,1)} %bitcast.6), channel_id=1, source_target_pairs={{0,64},{64,0},{128,192},{192,128},{256,320},{320,256},{384,448},{4... | collective-permute-start | bytes 1179656 | tf_op jit(solution)/shard_map/ppermute | solution.py:164
  44.1 0.1 reduce_or.9
  44.2 0.6 convert_reduce_fusion
  45.0 0.6 compare_select_fusion
  45.6 0.2 copy.21
  45.8 0.2 select_reduce_fusion.1
  46.0 0.7 fusion.source
  46.7 46.9 %all-to-all-done.1.arrived = bf16[64,128,128]{2,1,0:T(8,128)(2,1)S(1)} async-done(((bf16[64,128,128]{2,1,0:T(8,128)(2,1)}), bf16[64,128,128]{2,1,0:T(8,128)(2,1)S(1)}, u32[]{:S(2)}, u32[]{:S(2)}) %all-to-all-start.1) | async-done | bytes 2097184 | tf_op jit(solution)/shard_map/all_to_all | solution.py:148
  93.6 3.9 %attention.1.mine = bf16[1024,384]{1,0:T(8,128)(2,1)S(1)} custom-call(s32[32]{0:T(128)S(1)} %fusion.source, bf16[64,128,128]{2,1,0:T(8,128)(2,1)S(1)} %all-to-all-done.1.arrived), custom_call_target="tpu_custom_call" | custom-call | tf_op jit(solution)/shard_map/attention/pallas_call | solution.py:168
  97.5 1.9 %collective-permute-start.2 = (bf16[1024,384]{1,0:T(8,128)(2,1)S(1)}, bf16[1024,384]{1,0:T(8,128)(2,1)S(1)}, u32[]{:S(2)}, u32[]{:S(2)}) collective-permute-start(bf16[1024,384]{1,0:T(8,128)(2,1)S(1)} %attention.1.mine), channel_id=1, source_target_pairs={{0,64},{64,0},{128,192},{192,128},{256,320},{320,256},{384,448},{4... | collective-permute-start | bytes 2359304 | tf_op jit(solution)/shard_map/ppermute | solution.py:178
  99.5 2.3 %collective-permute-done.2.theirs = bf16[1024,384]{1,0:T(8,128)(2,1)S(1)} collective-permute-done((bf16[1024,384]{1,0:T(8,128)(2,1)S(1)}, bf16[1024,384]{1,0:T(8,128)(2,1)S(1)}, u32[]{:S(2)}, u32[]{:S(2)}) %collective-permute-start.2) | collective-permute-done | bytes 786464 | tf_op jit(solution)/shard_map/ppermute | solution.py:178
  101.7 1.8 %project.1 = bf16[4,1024,128]{2,1,0:T(8,128)(2,1)S(1)} custom-call(bf16[1024,384]{1,0:T(8,128)(2,1)S(1)} %attention.1.mine, bf16[1024,384]{1,0:T(8,128)(2,1)S(1)} %collective-permute-done.2.theirs, bf16[384,512]{1,0:T(8,128)(2,1)S(1)} %bitcast.11, bf16[384,512]{1,0:T(8,128)(2,1)S(1)} %collective-permute-done.1.w_theirs), custom_call_target="tpu_custom_call" | custom-call | tf_op jit(solution)/shard_map/project/pallas_call | solution.py:179
  103.5 18.1 %all_to_all.21.parts = bf16[4,1024,128]{2,1,0:T(8,128)(2,1)S(1)} all-to-all(bf16[4,1024,128]{2,1,0:T(8,128)(2,1)S(1)} %project.1), channel_id=1, replica_groups={{0,128,256,384},{64,192,320,448},{1,129,257,385},{65,193,321,449},{2,13..., dimensions={0} | all-to-all | bytes 2097152 | tf_op jit(solution)/shard_map/all_to_all | solution.py:187
  121.6 0.7 sum.1
  122.3 27.0 %all_to_all.22.returned = bf16[64,32,128]{2,1,0:T(8,128)(2,1)S(1)} all-to-all(bf16[64,32,128]{2,1,0:T(8,128)(2,1)S(1)} %sum.1), channel_id=1, replica_groups=mesh['head'=8,'tok'=64] {'tok'}, dimensions={0} | all-to-all | bytes 1048576 | tf_op jit(solution)/shard_map/all_to_all | solution.py:196
  149.3 1.2 unpack.1
  (25 shorter events, 0.5 us)
Async XLA Ops:
  0.0 19.4 %copy-start.7 = (s32[1536]{0:T(1024)S(1)}, s32[1536]{0:T(1024)}, u32[]{:S(2)}) copy-start(s32[1536]{0:T(1024)} %param.17) | copy-start | bytes 18436
  0.0 19.5 %copy-start.3 = (bf16[128,1024]{1,0:T(8,128)(2,1)S(1)}, bf16[128,1024]{1,0:T(8,128)(2,1)}, u32[]{:S(2)}) copy-start(bf16[128,1024]{1,0:T(8,128)(2,1)} %param.16) | copy-start | bytes 786436
  0.0 21.7 %copy-start = (bf16[768,128]{1,0:T(8,128)(2,1)S(1)}, bf16[768,128]{1,0:T(8,128)(2,1)}, u32[]{:S(2)}) copy-start(bf16[768,128]{1,0:T(8,128)(2,1)} %query.1) | copy-start | bytes 589828
  0.0 21.7 %copy-start.1 = (bf16[768,128]{1,0:T(8,128)(2,1)S(1)}, bf16[768,128]{1,0:T(8,128)(2,1)}, u32[]{:S(2)}) copy-start(bf16[768,128]{1,0:T(8,128)(2,1)} %key.1) | copy-start | bytes 589828
  0.0 21.7 %copy-start.2 = (bf16[768,128]{1,0:T(8,128)(2,1)S(1)}, bf16[768,128]{1,0:T(8,128)(2,1)}, u32[]{:S(2)}) copy-start(bf16[768,128]{1,0:T(8,128)(2,1)} %value.1) | copy-start | bytes 589828
  17.5 4.2 %collective-permute-start = (bf16[4,768,128]{2,1,0:T(8,128)(2,1)S(1)}, bf16[4,768,128]{2,1,0:T(8,128)(2,1)S(1)}, u32[]{:S(2)}, u32[]{:S(2)}) collective-permute-start(bf16[4,768,128]{2,1,0:T(8,128)(2,1)S(1)} %all_to_all.20.even), channel_id=1, source_target_pairs={{0,64},{64,0},{128,192},{192,128},{256,320},{320,256},{384,448},{4... | collective-permute-start | bytes 2359304 | tf_op jit(solution)/shard_map/ppermute | solution.py:135
  24.2 16.7 %copy-start.4 = (bf16[1024,128]{1,0:T(8,128)(2,1)S(1)}, bf16[1024,128]{1,0:T(8,128)(2,1)}, u32[]{:S(2)}) copy-start(bf16[1024,128]{1,0:T(8,128)(2,1)} %param.15) | copy-start | bytes 786436
  24.2 16.7 %copy-start.5 = (bf16[1024,128]{1,0:T(8,128)(2,1)S(1)}, bf16[1024,128]{1,0:T(8,128)(2,1)}, u32[]{:S(2)}) copy-start(bf16[1024,128]{1,0:T(8,128)(2,1)} %param.14) | copy-start | bytes 786436
  24.2 16.8 %copy-start.6 = (bf16[1024,128]{1,0:T(8,128)(2,1)S(1)}, bf16[1024,128]{1,0:T(8,128)(2,1)}, u32[]{:S(2)}) copy-start(bf16[1024,128]{1,0:T(8,128)(2,1)} %param.13) | copy-start | bytes 786436
  24.2 69.4 %all-to-all-start.1 = ((bf16[64,128,128]{2,1,0:T(8,128)(2,1)}), bf16[64,128,128]{2,1,0:T(8,128)(2,1)S(1)}, u32[]{:S(2)}, u32[]{:S(2)}) async-start(bf16[64,128,128]{2,1,0:T(8,128)(2,1)} %pack.1), calls=%async_computation.1 | async-start | bytes 4194304 | tf_op jit(solution)/shard_map/all_to_all | solution.py:148
  42.1 4.6 %collective-permute-start.1 = (bf16[384,512]{1,0:T(8,128)(2,1)}, bf16[384,512]{1,0:T(8,128)(2,1)S(1)}, u32[]{:S(2)}, u32[]{:S(2)}) collective-permute-start(bf16[384,512]{1,0:T(8,128)(2,1)} %bitcast.6), channel_id=1, source_target_pairs={{0,64},{64,0},{128,192},{192,128},{256,320},{320,256},{384,448},{4... | collective-permute-start | bytes 1179656 | tf_op jit(solution)/shard_map/ppermute | solution.py:164
  97.5 4.2 %collective-permute-start.2 = (bf16[1024,384]{1,0:T(8,128)(2,1)S(1)}, bf16[1024,384]{1,0:T(8,128)(2,1)S(1)}, u32[]{:S(2)}, u32[]{:S(2)}) collective-permute-start(bf16[1024,384]{1,0:T(8,128)(2,1)S(1)} %attention.1.mine), channel_id=1, source_target_pairs={{0,64},{64,0},{128,192},{192,128},{256,320},{320,256},{384,448},{4... | collective-permute-start | bytes 2359304 | tf_op jit(solution)/shard_map/ppermute | solution.py:178

commit v4 on v3

v4 whole, which is shorter than its diff:
```python
import math

import jax
import jax.numpy as jnp
from jax import lax
from jax.experimental import pallas as pl
from jax.experimental.pallas import tpu as pltpu
from jax.sharding import PartitionSpec as P


HEAD_DIM = 128
PAGE = 32
SLOTS = 32
BLOCK = 256
NEG = -1e30
VMEM = pl.BlockSpec(memory_space=pltpu.VMEM)
SMEM = pl.BlockSpec(memory_space=pltpu.SMEM)


def mm(a, b, dims):
    return lax.dot_general(a, b, (dims, ((), ())), preferred_element_type=jnp.float32)


def small(mib):
    return pltpu.CompilerParams(vmem_limit_bytes=mib * 1024 * 1024)


def pack_kernel(dest, query, key, value, sent, done):
    copies = []
    for page in range(dest.shape[0]):
        peer = dest[page]
        for part, array in enumerate((query, key, value)):
            copy = pltpu.make_async_copy(
                array.at[pl.ds(page * PAGE, PAGE)],
                sent.at[peer, pl.ds(part * PAGE, PAGE)],
                done.at[page * 3 + part],
            )
            copy.start()
            copies.append(copy)
    for copy in copies:
        copy.wait()


def grad_kernel(dest, here, *refs):
    count = len(refs) - 4
    mine, (theirs, w_out, sent, grad) = refs[:count], refs[count:]
    total = None
    for step in range(count):
        chip = lax.rem(here[0] - step + count, count)
        for got, side in ((mine[step][...], here[1]), (theirs[step], 1 - here[1])):
            part = mm(got, w_out[2 * chip + side], ((1,), (0,)))
            total = part if total is None else total + part
    grad[...] = total.astype(grad.dtype)
    for page in range(dest.shape[0]):
        sent[dest[page]] = grad[page * PAGE : (page + 1) * PAGE]


def spans_of(total):
    block = min(BLOCK, total)
    for first in range(0, total, block):
        here = slice(first, first + block)
        yield here, ([slice(0, first)] if first else []) + [here]


def softmax_of(query, key, here, spans):
    score = [mm(query[here], key[span], ((1,), (1,))) for span in spans]
    row_order = lax.broadcasted_iota(jnp.int32, score[-1].shape, 0)
    causal = lax.broadcasted_iota(jnp.int32, score[-1].shape, 1) <= row_order
    score[-1] = jnp.where(causal, score[-1], NEG)
    row_max = score[-1].max(axis=1, keepdims=True)
    if len(spans) > 1:
        row_max = jnp.maximum(row_max, score[0].max(axis=1, keepdims=True))
    factor = HEAD_DIM ** (-0.5) * math.log2(math.e)
    raised = [jnp.exp2((s - row_max) * factor) for s in score]
    inverse = 1.0 / sum(r.sum(axis=1, keepdims=True) for r in raised)
    return [r * inverse for r in raised]


def weights_kernel(source, arrived, query, key, value, weights):
    for slot in range(source.shape[0]):
        peer = source[slot] & 255
        at = slice(slot * PAGE, (slot + 1) * PAGE)
        for part, array in enumerate((query, key, value)):
            array[at] = arrived[peer, part * PAGE : (part + 1) * PAGE]
    here, spans = list(spans_of(query.shape[0]))[-1]
    for part, span in zip(softmax_of(query, key, here, spans), spans):
        weights[:, span] = part


def attention_kernel(
    source, query, key, value, weights, arrived, grads, grad, dkey, dvalue
):
    scale = HEAD_DIM ** (-0.5)
    for slot in range(source.shape[0]):
        peer, live = source[slot] & 255, source[slot] >> 8
        at = slice(slot * PAGE, (slot + 1) * PAGE)
        page = arrived[peer].astype(jnp.float32) * live.astype(jnp.float32)
        grad[at] = page.astype(grad.dtype)
    for here, spans in spans_of(query.shape[0]):
        part_query, part_grad = query[here], grad[here]
        if here.stop == query.shape[0]:
            part_weights = [weights[:, span] for span in spans]
        else:
            part_weights = softmax_of(query, key, here, spans)
        grad_weights = [mm(part_grad, value[span], ((1,), (1,))) for span in spans]
        row_delta = sum(
            (w * g).sum(axis=1, keepdims=True) for w, g in zip(part_weights, grad_weights)
        )
        grad_score = [
            (w * (g - row_delta)).astype(jnp.bfloat16)
            for w, g in zip(part_weights, grad_weights)
        ]
        dquery = sum(mm(d, key[span], ((1,), (0,))) for d, span in zip(grad_score, spans))
        grads[here, 0:HEAD_DIM] = (dquery * scale).astype(grads.dtype)
        for w, d, span in zip(part_weights, grad_score, spans):
            more_key = mm(d, part_query, ((0,), (0,)))
            more_value = mm(w.astype(jnp.bfloat16), part_grad, ((0,), (0,)))
            if span is here:
                dkey[span] = more_key
                dvalue[span] = more_value
            else:
                dkey[span] += more_key
                dvalue[span] += more_value
    grads[:, HEAD_DIM : 2 * HEAD_DIM] = (dkey[...] * scale).astype(grads.dtype)
    grads[:, 2 * HEAD_DIM : 3 * HEAD_DIM] = dvalue[...].astype(grads.dtype)


def project_kernel(*refs):
    grads, weights, out = refs[-3:]
    total_rows = grads.shape[0]
    step = min(BLOCK, total_rows)
    for first in range(0, total_rows, step):
        here = slice(first, first + step)
        for x in range(out.shape[0]):
            cols = slice(x * HEAD_DIM, (x + 1) * HEAD_DIM)
            total = mm(grads[here], weights[:, cols], ((1,), (0,)))
            if len(refs) > 3:
                total += refs[0][x, here]
            out[x, here] = total.astype(out.dtype)


def sum_kernel(source, parts, sent):
    for slot in reversed(range(source.shape[0])):
        at = slice(slot * PAGE, (slot + 1) * PAGE)
        total = parts[0, at].astype(jnp.float32)
        for x in range(1, parts.shape[0]):
            total = total + parts[x, at].astype(jnp.float32)
        sent[source[slot] & 255] = total.astype(sent.dtype)


def unpack_kernel(dest, returned, out):
    for page in range(dest.shape[0]):
        out[page * PAGE : (page + 1) * PAGE] = returned[dest[page]]


def per_device(queries, keys, values, out_grad, w_query, w_key, w_value, w_out, page_cluster):
    tok_rows = queries.shape[0]
    pages_here = tok_rows // PAGE
    peers = lax.axis_size("tok")
    heads = lax.axis_size("head")
    chips = heads // 2
    myself = lax.axis_index("tok")
    core = lax.axis_index("head") % 2
    chip = lax.axis_index("head") // 2
    across = [[2 * x + c for x in range(chips)] for c in range(2)]
    swap = [(h, h ^ 1) for h in range(heads)]
    slot_rows = SLOTS * PAGE
    half = queries.dtype

    def moved(array, pairs):
        return lax.ppermute(array, "head", pairs)

    def work(products, moved_bytes):
        return pl.CostEstimate(flops=2 * products, bytes_accessed=moved_bytes, transcendentals=0)

    table = page_cluster.reshape(peers, pages_here)
    dest = lax.dynamic_index_in_dim(table, myself, 0, keepdims=False)
    sent = pl.pallas_call(
        pack_kernel,
        out_shape=jax.ShapeDtypeStruct((peers, 3 * PAGE, HEAD_DIM), half),
        in_specs=[SMEM] + [VMEM] * 3,
        out_specs=pl.BlockSpec(memory_space=pl.ANY),
        scratch_shapes=[pltpu.SemaphoreType.DMA((3 * pages_here,))],
        compiler_params=small(8),
        name="pack",
    )(dest, queries, keys, values)
    sent, w_query, w_key, w_value, page_cluster = lax.optimization_barrier(
        (sent, w_query, w_key, w_value, page_cluster)
    )
    arrived = lax.all_to_all(sent, "tok", 0, 0, tiled=True)

    gathered = [out_grad]
    for d in range(1, chips):
        pairs = [(h, (h + 2 * d) % heads) for h in range(heads)]
        gathered.append(moved(out_grad, pairs))
    theirs = moved(jnp.stack(gathered), swap)
    w_blocks = w_out.reshape(HEAD_DIM, heads, HEAD_DIM).transpose(1, 2, 0)
    sent_grad = pl.pallas_call(
        grad_kernel,
        out_shape=jax.ShapeDtypeStruct((peers, PAGE, HEAD_DIM), half),
        in_specs=[SMEM, SMEM] + [VMEM] * (chips + 2),
        out_specs=VMEM,
        scratch_shapes=[pltpu.VMEM((tok_rows, HEAD_DIM), half)],
        compiler_params=small(12),
        cost_estimate=work(tok_rows * heads * HEAD_DIM**2, 4 * tok_rows * heads * HEAD_DIM),
        name="grad",
    )(dest, jnp.stack([chip, core]), *gathered, theirs, w_blocks)
    table = page_cluster.reshape(peers, pages_here)
    has = jnp.any(table == myself, axis=1).astype(jnp.int32)
    peer_order = jnp.arange(peers, dtype=jnp.int32)
    rank = jnp.sum(jnp.where(peer_order[:, None] < peer_order[None, :], has[:, None], 0), axis=0)
    slot_order = jnp.arange(SLOTS, dtype=jnp.int32)
    live = (slot_order < jnp.sum(has)).astype(jnp.int32)
    wanted = jnp.where(live == 1, slot_order, 0)
    hit = (rank[None, :] == wanted[:, None]) & (has[None, :] == 1)
    source = jnp.sum(jnp.where(hit, peer_order[None, :], 0), axis=1) + live * 256
    weights = jnp.concatenate([w_query, w_key, w_value], axis=1)
    weights = weights.reshape(chips, 2, HEAD_DIM, 3 * HEAD_DIM)
    w_mine = lax.dynamic_index_in_dim(weights, core, 1, keepdims=False)
    w_away = lax.dynamic_index_in_dim(weights, 1 - core, 1, keepdims=False)
    w_mine = w_mine.reshape(chips * HEAD_DIM, 3 * HEAD_DIM).T
    w_away = w_away.reshape(chips * HEAD_DIM, 3 * HEAD_DIM).T
    w_theirs = moved(w_away, swap)
    arrived, w_mine, w_theirs, source, sent_grad = lax.optimization_barrier(
        (arrived, w_mine, w_theirs, source, sent_grad)
    )
    arrived_grad = lax.all_to_all(sent_grad, "tok", 0, 0, tiled=True)
    flat = jax.ShapeDtypeStruct((slot_rows, HEAD_DIM), half)
    *paged, weighted = pl.pallas_call(
        weights_kernel,
        out_shape=[flat] * 3
        + [jax.ShapeDtypeStruct((min(BLOCK, slot_rows), slot_rows), jnp.float32)],
        in_specs=[SMEM, VMEM],
        out_specs=[VMEM] * 4,
        compiler_params=small(24),
        cost_estimate=work(BLOCK * slot_rows * HEAD_DIM, 4 * BLOCK * slot_rows),
        name="softmax",
    )(source, arrived)
    grads = pl.pallas_call(
        attention_kernel,
        out_shape=jax.ShapeDtypeStruct((slot_rows, 3 * HEAD_DIM), half),
        in_specs=[SMEM] + [VMEM] * 5,
        out_specs=VMEM,
        scratch_shapes=[pltpu.VMEM((slot_rows, HEAD_DIM), half)]
        + [pltpu.VMEM((slot_rows, HEAD_DIM), jnp.float32)] * 2,
        compiler_params=small(24),
        cost_estimate=work(3 * slot_rows**2 * HEAD_DIM, 4 * slot_rows**2),
        name="attention",
    )(source, *paged, weighted, arrived_grad)

    def projected(*arrays, dtype):
        return pl.pallas_call(
            project_kernel,
            out_shape=jax.ShapeDtypeStruct((chips, slot_rows, HEAD_DIM), dtype),
            in_specs=[VMEM] * len(arrays),
            out_specs=VMEM,
            compiler_params=small(16),
            cost_estimate=work(slot_rows * w_mine.size, 8 * slot_rows * w_mine.shape[1]),
        )(*arrays)

    their_grads = moved(grads, swap)
    partial = projected(grads, w_mine, dtype=jnp.float32)
    partial = projected(partial, their_grads, w_theirs, dtype=half)
    parts = lax.all_to_all(partial, "head", 0, 0, axis_index_groups=across, tiled=True)
    summed = pl.pallas_call(
        sum_kernel,
        out_shape=jax.ShapeDtypeStruct((peers, PAGE, HEAD_DIM), half),
        in_specs=[SMEM, VMEM],
        out_specs=VMEM,
        compiler_params=small(8),
        name="sum",
    )(source, parts)
    returned = lax.all_to_all(summed, "tok", 0, 0, tiled=True)
    return pl.pallas_call(
        unpack_kernel,
        out_shape=jax.ShapeDtypeStruct((tok_rows, HEAD_DIM), half),
        in_specs=[SMEM, VMEM],
        out_specs=VMEM,
        compiler_params=small(8),
        name="unpack",
    )(dest, returned)


def solution(mesh):
    placed = (
        P("tok", "head"),
        P("tok", "head"),
        P("tok", "head"),
        P("tok", "head"),
        P(None, "head"),
        P(None, "head"),
        P(None, "head"),
        P("head", None),
        P(),
    )
    return jax.shard_map(
        per_device, mesh=mesh, in_specs=placed, out_specs=P("tok", "head"), check_vma=False
    )
```

time: 151 us -> 147 us (0.974)
  blocking collectives: 61.4 us -> 42.9 us
  waiting for transfers between devices: 51.1 us -> 32.6 us
  starting transfers between devices: 22.4 us -> 40.7 us
  local copies, waits for them, and re-layouts: 2.73 us -> 12.7 us
  Pallas kernels: 10.2 us -> 13.2 us
    all_to_all x1, waiting for transfers between devices: 46.9 us -> 14 us  [per_device(): arrived = lax.all_to_all(sent, 'tok', 0, 0, tiled=True)]
    all_to_all x1 -> x0, blocking collectives: 16.4 us -> none  [per_device(): lax.all_to_all(jnp.broadcast_to(out_grad[None], (chips, *out_grad.shape))...]
    all_to_all x0 -> x1, waiting for transfers between devices: none -> 15 us  [per_device(): arrived_grad = lax.all_to_all(sent_grad, 'tok', 0, 0, tiled=True)]
    ppermute x3 -> x6, starting transfers between devices: 5.74 us -> 16 us  [moved(): return lax.ppermute(array, 'head', pairs)]
    unnamed x17 -> x33, local copies, waits for them, and re-layouts: 0.21 us -> 8.85 us
    all_to_all x0 -> x1, starting transfers between devices: none -> 7.98 us  [per_device(): arrived_grad = lax.all_to_all(sent_grad, 'tok', 0, 0, tiled=True)]
    all_to_all x1, blocking collectives: 27 us -> 23.4 us  [per_device(): returned = lax.all_to_all(summed, 'tok', 0, 0, tiled=True)]
    pallas_call x2 -> x5, Pallas kernels: 4.31 us -> 7.71 us  [the longest x1 2.56 us: per_device(): pl.pallas_call(grad_kernel, out_shape=jax.ShapeDtypeStruct((peers, PAGE,...]
  transfers between devices with their start and end apart: 4 -> 8, of which waited for: 3 -> 5; matrix products, arithmetic and copies ran while one was open for 3% -> 5% of each run, Pallas kernels for 0% -> 3%
where the time goes in v4:
time: 147 us; the launch traced here: 146 us
  blocking collectives  42.9 us (29%)
  starting transfers between devices  40.7 us (28%)
  waiting for transfers between devices  32.6 us (22%)
  Pallas kernels  13.2 us (9%)
  local copies, waits for them, and re-layouts  12.7 us (9%)
  other arithmetic  3.51 us (2%)
    all_to_all x1, blocking collectives, per_device(): returned = lax.all_to_all(summed, 'tok', 0, 0, tiled=True)  23.4 us
    all_to_all x1, blocking collectives, per_device(): lax.all_to_all(partial, 'head', 0, 0, axis_index_groups=across, tiled=True)  19.5 us
    all_to_all x1, starting transfers between devices, per_device(): arrived = lax.all_to_all(sent, 'tok', 0, 0, tiled=True)  16.7 us
    ppermute x6, starting transfers between devices, moved(): return lax.ppermute(array, 'head', pairs)  16 us
    all_to_all x1, waiting for transfers between devices, per_device(): arrived_grad = lax.all_to_all(sent_grad, 'tok', 0, 0, tiled=True)  15 us
    all_to_all x1, waiting for transfers between devices, per_device(): arrived = lax.all_to_all(sent, 'tok', 0, 0, tiled=True)  14 us
    unnamed x33, local copies, waits for them, and re-layouts  8.85 us
    all_to_all x1, starting transfers between devices, per_device(): arrived_grad = lax.all_to_all(sent_grad, 'tok', 0, 0, tiled=True)  7.98 us
  transfers between devices with their start and end apart: 8, of which 5 were waited for; matrix products, arithmetic and copies ran while one was open for 5% of the time, Pallas kernels for 3%

profile of v4, /device:TPU:8, one launch (start us, length us, event | category | flops | bytes accessed | tf_op | source)
XLA Modules:
  0.0 146.1 jit_solution(11460620851342662732)
XLA Ops:
  3.6 2.1 %pack.1 = bf16[64,96,128]{2,1,0:T(8,128)(2,1)} custom-call(s32[24]{0:T(128)S(1)} %fusion.1.dest, bf16[768,128]{1,0:T(8,128)(2,1)S(1)} %copy-done.9, bf16[768,128]{1,0:T(8,128)(2,1)S(1)} %copy-done.10, bf16[768,128]{1,0:T(8,128)(2,1)S(1)} %copy-done.11), custom_call_target="tpu_custom_call" | custom-call | tf_op jit(solution)/shard_map/pack/pallas_call | solution.py:178
  5.7 16.7 %all-to-all-start = ((bf16[64,96,128]{2,1,0:T(8,128)(2,1)}), bf16[64,96,128]{2,1,0:T(8,128)(2,1)S(1)}, u32[]{:S(2)}, u32[]{:S(2)}) async-start(bf16[64,96,128]{2,1,0:T(8,128)(2,1)} %pack.1), calls=%async_computation | async-start | bytes 3145728 | tf_op jit(solution)/shard_map/all_to_all | solution.py:190
  22.4 4.7 %collective-permute-start.3 = (bf16[768,128]{1,0:T(8,128)(2,1)S(1)}, bf16[768,128]{1,0:T(8,128)(2,1)S(1)}, u32[]{:S(2)}, u32[]{:S(2)}) collective-permute-start(bf16[768,128]{1,0:T(8,128)(2,1)S(1)} %copy-done), channel_id=1, source_target_pairs={{0,384},{64,448},{128,0},{192,64},{256,128},{320,192},{384,256},{4... | collective-permute-start | bytes 589832 | tf_op jit(solution)/shard_map/ppermute | solution.py:171
  27.1 2.7 %collective-permute-start.2 = (bf16[768,128]{1,0:T(8,128)(2,1)S(1)}, bf16[768,128]{1,0:T(8,128)(2,1)S(1)}, u32[]{:S(2)}, u32[]{:S(2)}) collective-permute-start(bf16[768,128]{1,0:T(8,128)(2,1)S(1)} %copy-done), channel_id=1, source_target_pairs={{0,256},{64,320},{128,384},{192,448},{256,0},{320,64},{384,128},{4... | collective-permute-start | bytes 589832 | tf_op jit(solution)/shard_map/ppermute | solution.py:171
  29.8 2.8 %collective-permute-start.1 = (bf16[768,128]{1,0:T(8,128)(2,1)S(1)}, bf16[768,128]{1,0:T(8,128)(2,1)S(1)}, u32[]{:S(2)}, u32[]{:S(2)}) collective-permute-start(bf16[768,128]{1,0:T(8,128)(2,1)S(1)} %copy-done), channel_id=1, source_target_pairs={{0,128},{64,192},{128,256},{192,320},{256,384},{320,448},{384,0},{... | collective-permute-start | bytes 589832 | tf_op jit(solution)/shard_map/ppermute | solution.py:171
  34.6 1.9 %collective-permute-start = (bf16[384,512]{1,0:T(8,128)(2,1)}, bf16[384,512]{1,0:T(8,128)(2,1)S(1)}, u32[]{:S(2)}, u32[]{:S(2)}) collective-permute-start(bf16[384,512]{1,0:T(8,128)(2,1)} %bitcast.25), channel_id=1, source_target_pairs={{0,64},{64,0},{128,192},{192,128},{256,320},{320,256},{384,448},{4... | collective-permute-start | bytes 1179656 | tf_op jit(solution)/shard_map/ppermute | solution.py:171
  38.3 2.2 %collective-permute-done.1.refs_1_ = bf16[768,128]{1,0:T(8,128)(2,1)S(1)} collective-permute-done((bf16[768,128]{1,0:T(8,128)(2,1)S(1)}, bf16[768,128]{1,0:T(8,128)(2,1)S(1)}, u32[]{:S(2)}, u32[]{:S(2)}) %collective-permute-start.1) | collective-permute-done | bytes 196640 | tf_op jit(solution)/shard_map/ppermute | solution.py:171
  40.5 1.0 pad_maximum_fusion.1
  41.5 1.9 %collective-permute-start.4 = (bf16[4,768,128]{2,1,0:T(8,128)(2,1)}, bf16[4,768,128]{2,1,0:T(8,128)(2,1)}, u32[]{:S(2)}, u32[]{:S(2)}) collective-permute-start(bf16[4,768,128]{2,1,0:T(8,128)(2,1)} %pad_maximum_fusion.1), channel_id=1, source_target_pairs={{0,64},{64,0},{128,192},{192,128},{256,320},{320,256},{384,448},{4... | collective-permute-start | bytes 2359304 | tf_op jit(solution)/shard_map/ppermute | solution.py:171
  43.6 1.1 copy.18
  44.7 1.2 copy.21
  46.8 2.6 %grad.1 = bf16[64,32,128]{2,1,0:T(8,128)(2,1)} custom-call(s32[24]{0:T(128)S(1)} %fusion.1.dest, s32[2]{0:T(128)S(1)} %pad_add_fusion.here, bf16[768,128]{1,0:T(8,128)(2,1)S(1)} %copy-done, bf16[768,128]{1,0:T(8,128)(2,1)S(1)} %collective-permute-done.1.refs_1_, bf16[768,128]{1,0:T(8,128)(2,1)S(1)} %collective-permute-done.2.refs_2_, ...), custom_call_target="tpu_custom_call" | custom-call | flops 201326592 | bytes 3145728 | tf_op jit(solution)/shard_map/grad/pallas_call | solution.py:198
  49.3 14.0 %all-to-all-done.arrived = bf16[64,96,128]{2,1,0:T(8,128)(2,1)S(1)} async-done(((bf16[64,96,128]{2,1,0:T(8,128)(2,1)}), bf16[64,96,128]{2,1,0:T(8,128)(2,1)S(1)}, u32[]{:S(2)}, u32[]{:S(2)}) %all-to-all-start) | async-done | bytes 1572896 | tf_op jit(solution)/shard_map/all_to_all | solution.py:190
  63.3 8.0 %all-to-all-start.1 = ((bf16[64,32,128]{2,1,0:T(8,128)(2,1)}), bf16[64,32,128]{2,1,0:T(8,128)(2,1)S(1)}, u32[]{:S(2)}, u32[]{:S(2)}) async-start(bf16[64,32,128]{2,1,0:T(8,128)(2,1)} %grad.1), calls=%async_computation.1 | async-start | bytes 1048576 | tf_op jit(solution)/shard_map/all_to_all | solution.py:227
  71.3 1.1 softmax.1
  74.5 15.0 %all-to-all-done.1.arrived = bf16[64,32,128]{2,1,0:T(8,128)(2,1)S(1)} async-done(((bf16[64,32,128]{2,1,0:T(8,128)(2,1)}), bf16[64,32,128]{2,1,0:T(8,128)(2,1)S(1)}, u32[]{:S(2)}, u32[]{:S(2)}) %all-to-all-start.1) | async-done | bytes 524320 | tf_op jit(solution)/shard_map/all_to_all | solution.py:227
  92.3 3.6 %attention.1.refs_0_ = bf16[1024,384]{1,0:T(8,128)(2,1)S(1)} custom-call(s32[32]{0:T(128)S(1)} %fusion.source, bf16[1024,128]{1,0:T(8,128)(2,1)S(1)} %copy-done.4, bf16[1024,128]{1,0:T(8,128)(2,1)S(1)} %copy-done.6, bf16[1024,128]{1,0:T(8,128)(2,1)S(1)} %copy-done.8, f32[256,1024]{1,0:T(8,128)S(1)} %get-tuple-element.29.weights, ...), custom_call_target="tpu_custom_call" | custom-call | flops 805306368 | bytes 4194304 | tf_op jit(solution)/shard_map/attention/pallas_call | solution.py:239
  96.0 2.1 %collective-permute-start.5 = (bf16[1024,384]{1,0:T(8,128)(2,1)S(1)}, bf16[1024,384]{1,0:T(8,128)(2,1)S(1)}, u32[]{:S(2)}, u32[]{:S(2)}) collective-permute-start(bf16[1024,384]{1,0:T(8,128)(2,1)S(1)} %attention.1.refs_0_), channel_id=1, source_target_pairs={{0,64},{64,0},{128,192},{192,128},{256,320},{320,256},{384,448},{4... | collective-permute-start | bytes 2359304 | tf_op jit(solution)/shard_map/ppermute | solution.py:171
  98.0 1.0 shard_map.91.refs_0_
  99.0 1.3 collective-permute-done.5.refs_1_
  100.3 1.0 shard_map.92
  101.3 19.5 %all_to_all.20.parts = bf16[4,1024,128]{2,1,0:T(8,128)(2,1)S(1)} all-to-all(bf16[4,1024,128]{2,1,0:T(8,128)(2,1)S(1)} %shard_map.92), channel_id=1, replica_groups={{0,128,256,384},{64,192,320,448},{1,129,257,385},{65,193,321,449},{2,13..., dimensions={0} | all-to-all | bytes 2097152 | tf_op jit(solution)/shard_map/all_to_all | solution.py:264
  121.4 23.4 %all_to_all.21.returned = bf16[64,32,128]{2,1,0:T(8,128)(2,1)S(1)} all-to-all(bf16[64,32,128]{2,1,0:T(8,128)(2,1)S(1)} %sum.1), channel_id=1, replica_groups=mesh['head'=8,'tok'=64] {'tok'}, dimensions={0} | all-to-all | bytes 1048576 | tf_op jit(solution)/shard_map/all_to_all | solution.py:273
  144.9 1.2 unpack.1
  (52 shorter events, 13.8 us)
Async XLA Ops:
  0.8 0.9 copy-start.9
  1.7 0.9 copy-start.10
  2.7 0.9 copy-start.11
  5.7 16.8 %copy-start = (bf16[768,128]{1,0:T(8,128)(2,1)S(1)}, bf16[768,128]{1,0:T(8,128)(2,1)}, u32[]{:S(2)}) copy-start(bf16[768,128]{1,0:T(8,128)(2,1)} %refs_0_.1) | copy-start | bytes 589828
  5.7 27.0 %copy-start.12 = (bf16[1024,128]{1,0:T(8,128)(2,1)S(1)}, bf16[1024,128]{1,0:T(8,128)(2,1)}, u32[]{:S(2)}) copy-start(bf16[1024,128]{1,0:T(8,128)(2,1)} %param.15) | copy-start | bytes 786436
  5.7 27.0 %copy-start.13 = (bf16[1024,128]{1,0:T(8,128)(2,1)S(1)}, bf16[1024,128]{1,0:T(8,128)(2,1)}, u32[]{:S(2)}) copy-start(bf16[1024,128]{1,0:T(8,128)(2,1)} %param.14) | copy-start | bytes 786436
  5.7 27.0 %copy-start.14 = (bf16[1024,128]{1,0:T(8,128)(2,1)S(1)}, bf16[1024,128]{1,0:T(8,128)(2,1)}, u32[]{:S(2)}) copy-start(bf16[1024,128]{1,0:T(8,128)(2,1)} %param.13) | copy-start | bytes 786436
  5.7 57.6 %all-to-all-start = ((bf16[64,96,128]{2,1,0:T(8,128)(2,1)}), bf16[64,96,128]{2,1,0:T(8,128)(2,1)S(1)}, u32[]{:S(2)}, u32[]{:S(2)}) async-start(bf16[64,96,128]{2,1,0:T(8,128)(2,1)} %pack.1), calls=%async_computation | async-start | bytes 3145728 | tf_op jit(solution)/shard_map/all_to_all | solution.py:190
  22.4 15.6 %collective-permute-start.3 = (bf16[768,128]{1,0:T(8,128)(2,1)S(1)}, bf16[768,128]{1,0:T(8,128)(2,1)S(1)}, u32[]{:S(2)}, u32[]{:S(2)}) collective-permute-start(bf16[768,128]{1,0:T(8,128)(2,1)S(1)} %copy-done), channel_id=1, source_target_pairs={{0,384},{64,448},{128,0},{192,64},{256,128},{320,192},{384,256},{4... | collective-permute-start | bytes 589832 | tf_op jit(solution)/shard_map/ppermute | solution.py:171
  27.1 11.2 %collective-permute-start.2 = (bf16[768,128]{1,0:T(8,128)(2,1)S(1)}, bf16[768,128]{1,0:T(8,128)(2,1)S(1)}, u32[]{:S(2)}, u32[]{:S(2)}) collective-permute-start(bf16[768,128]{1,0:T(8,128)(2,1)S(1)} %copy-done), channel_id=1, source_target_pairs={{0,256},{64,320},{128,384},{192,448},{256,0},{320,64},{384,128},{4... | collective-permute-start | bytes 589832 | tf_op jit(solution)/shard_map/ppermute | solution.py:171
  29.8 10.7 %collective-permute-start.1 = (bf16[768,128]{1,0:T(8,128)(2,1)S(1)}, bf16[768,128]{1,0:T(8,128)(2,1)S(1)}, u32[]{:S(2)}, u32[]{:S(2)}) collective-permute-start(bf16[768,128]{1,0:T(8,128)(2,1)S(1)} %copy-done), channel_id=1, source_target_pairs={{0,128},{64,192},{128,256},{192,320},{256,384},{320,448},{384,0},{... | collective-permute-start | bytes 589832 | tf_op jit(solution)/shard_map/ppermute | solution.py:171
  32.8 3.7 %copy-start.15 = (s32[1536]{0:T(1024)S(1)}, s32[1536]{0:T(1024)}, u32[]{:S(2)}) copy-start(s32[1536]{0:T(1024)} %param.17) | copy-start | bytes 18436
  34.6 14.7 %collective-permute-start = (bf16[384,512]{1,0:T(8,128)(2,1)}, bf16[384,512]{1,0:T(8,128)(2,1)S(1)}, u32[]{:S(2)}, u32[]{:S(2)}) collective-permute-start(bf16[384,512]{1,0:T(8,128)(2,1)} %bitcast.25), channel_id=1, source_target_pairs={{0,64},{64,0},{128,192},{192,128},{256,320},{320,256},{384,448},{4... | collective-permute-start | bytes 1179656 | tf_op jit(solution)/shard_map/ppermute | solution.py:171
  41.5 5.2 %collective-permute-start.4 = (bf16[4,768,128]{2,1,0:T(8,128)(2,1)}, bf16[4,768,128]{2,1,0:T(8,128)(2,1)}, u32[]{:S(2)}, u32[]{:S(2)}) collective-permute-start(bf16[4,768,128]{2,1,0:T(8,128)(2,1)} %pad_maximum_fusion.1), channel_id=1, source_target_pairs={{0,64},{64,0},{128,192},{192,128},{256,320},{320,256},{384,448},{4... | collective-permute-start | bytes 2359304 | tf_op jit(solution)/shard_map/ppermute | solution.py:171
  49.3 14.0 %copy-start.1 = (bf16[384,512]{1,0:T(8,128)(2,1)}, bf16[384,512]{1,0:T(8,128)(2,1)S(1)}, u32[]{:S(2)}) copy-start(bf16[384,512]{1,0:T(8,128)(2,1)S(1)} %collective-permute-done.refs_2_) | copy-start | bytes 1179652
  63.3 26.2 %all-to-all-start.1 = ((bf16[64,32,128]{2,1,0:T(8,128)(2,1)}), bf16[64,32,128]{2,1,0:T(8,128)(2,1)S(1)}, u32[]{:S(2)}, u32[]{:S(2)}) async-start(bf16[64,32,128]{2,1,0:T(8,128)(2,1)} %grad.1), calls=%async_computation.1 | async-start | bytes 1048576 | tf_op jit(solution)/shard_map/all_to_all | solution.py:227
  72.4 0.7 copy-start.3
  73.1 0.7 copy-start.5
  73.8 0.7 copy-start.7
  89.5 1.0 copy-start.4
  90.4 0.9 copy-start.6
  91.4 0.9 copy-start.8
  96.0 4.3 %copy-start.2 = (bf16[384,512]{1,0:T(8,128)(2,1)S(1)}, bf16[384,512]{1,0:T(8,128)(2,1)}, u32[]{:S(2)}) copy-start(bf16[384,512]{1,0:T(8,128)(2,1)} %copy-done.1) | copy-start | bytes 1179652
  96.0 4.3 %collective-permute-start.5 = (bf16[1024,384]{1,0:T(8,128)(2,1)S(1)}, bf16[1024,384]{1,0:T(8,128)(2,1)S(1)}, u32[]{:S(2)}, u32[]{:S(2)}) collective-permute-start(bf16[1024,384]{1,0:T(8,128)(2,1)S(1)} %attention.1.refs_0_), channel_id=1, source_target_pairs={{0,64},{64,0},{128,192},{192,128},{256,320},{320,256},{384,448},{4... | collective-permute-start | bytes 2359304 | tf_op jit(solution)/shard_map/ppermute | solution.py:171

commit v5 on v4

--- a/solution.py
+++ b/solution.py
@@ -25,10 +25,12 @@
     return pltpu.CompilerParams(vmem_limit_bytes=mib * 1024 * 1024)
 
 
-def pack_kernel(dest, query, key, value, sent, done):
+def pack_kernel(table, query, key, value, sent, done):
     copies = []
-    for page in range(dest.shape[0]):
-        peer = dest[page]
+    pages = query.shape[0] // PAGE
+    first = lax.axis_index("tok") * pages
+    for page in range(pages):
+        peer = table[first + page]
         for part, array in enumerate((query, key, value)):
             copy = pltpu.make_async_copy(
                 array.at[pl.ds(page * PAGE, PAGE)],
@@ -76,20 +78,16 @@
     return [r * inverse for r in raised]
 
 
-def weights_kernel(source, arrived, query, key, value, weights):
+def assemble_kernel(source, arrived, paged):
     for slot in range(source.shape[0]):
         peer = source[slot] & 255
         at = slice(slot * PAGE, (slot + 1) * PAGE)
-        for part, array in enumerate((query, key, value)):
-            array[at] = arrived[peer, part * PAGE : (part + 1) * PAGE]
-    here, spans = list(spans_of(query.shape[0]))[-1]
-    for part, span in zip(softmax_of(query, key, here, spans), spans):
-        weights[:, span] = part
-
-
-def attention_kernel(
-    source, query, key, value, weights, arrived, grads, grad, dkey, dvalue
-):
+        for part in range(3):
+            paged[part, at] = arrived[peer, part * PAGE : (part + 1) * PAGE]
+
+
+def attention_kernel(source, paged, arrived, grads, grad, dkey, dvalue):
+    query, key, value = paged.at[0], paged.at[1], paged.at[2]
     scale = HEAD_DIM ** (-0.5)
     for slot in range(source.shape[0]):
         peer, live = source[slot] & 255, source[slot] >> 8
@@ -98,10 +96,7 @@
         grad[at] = page.astype(grad.dtype)
     for here, spans in spans_of(query.shape[0]):
         part_query, part_grad = query[here], grad[here]
-        if here.stop == query.shape[0]:
-            part_weights = [weights[:, span] for span in spans]
-        else:
-            part_weights = softmax_of(query, key, here, spans)
+        part_weights = softmax_of(query, key, here, spans)
         grad_weights = [mm(part_grad, value[span], ((1,), (1,))) for span in spans]
         row_delta = sum(
             (w * g).sum(axis=1, keepdims=True) for w, g in zip(part_weights, grad_weights)
@@ -173,21 +168,19 @@
     def work(products, moved_bytes):
         return pl.CostEstimate(flops=2 * products, bytes_accessed=moved_bytes, transcendentals=0)
 
-    table = page_cluster.reshape(peers, pages_here)
-    dest = lax.dynamic_index_in_dim(table, myself, 0, keepdims=False)
     sent = pl.pallas_call(
         pack_kernel,
         out_shape=jax.ShapeDtypeStruct((peers, 3 * PAGE, HEAD_DIM), half),
         in_specs=[SMEM] + [VMEM] * 3,
         out_specs=pl.BlockSpec(memory_space=pl.ANY),
         scratch_shapes=[pltpu.SemaphoreType.DMA((3 * pages_here,))],
-        compiler_params=small(8),
         name="pack",
-    )(dest, queries, keys, values)
+    )(page_cluster, queries, keys, values)
     sent, w_query, w_key, w_value, page_cluster = lax.optimization_barrier(
         (sent, w_query, w_key, w_value, page_cluster)
     )
     arrived = lax.all_to_all(sent, "tok", 0, 0, tiled=True)
+    dest = lax.dynamic_slice_in_dim(page_cluster, myself * pages_here, pages_here)
 
     gathered = [out_grad]
     for d in range(1, chips):
@@ -225,28 +218,26 @@
         (arrived, w_mine, w_theirs, source, sent_grad)
     )
     arrived_grad = lax.all_to_all(sent_grad, "tok", 0, 0, tiled=True)
-    flat = jax.ShapeDtypeStruct((slot_rows, HEAD_DIM), half)
-    *paged, weighted = pl.pallas_call(
-        weights_kernel,
-        out_shape=[flat] * 3
-        + [jax.ShapeDtypeStruct((min(BLOCK, slot_rows), slot_rows), jnp.float32)],
+    paged = pl.pallas_call(
+        assemble_kernel,
+        out_shape=jax.ShapeDtypeStruct((3, slot_rows, HEAD_DIM), half),
         in_specs=[SMEM, VMEM],
-        out_specs=[VMEM] * 4,
-        compiler_params=small(24),
-        cost_estimate=work(BLOCK * slot_rows * HEAD_DIM, 4 * BLOCK * slot_rows),
-        name="softmax",
+        out_specs=VMEM,
+        compiler_params=small(8),
+        cost_estimate=work(slot_rows**2, 12 * slot_rows * HEAD_DIM),
+        name="assemble",
     )(source, arrived)
     grads = pl.pallas_call(
         attention_kernel,
         out_shape=jax.ShapeDtypeStruct((slot_rows, 3 * HEAD_DIM), half),
-        in_specs=[SMEM] + [VMEM] * 5,
+        in_specs=[SMEM] + [VMEM] * 2,
         out_specs=VMEM,
         scratch_shapes=[pltpu.VMEM((slot_rows, HEAD_DIM), half)]
         + [pltpu.VMEM((slot_rows, HEAD_DIM), jnp.float32)] * 2,
         compiler_params=small(24),
         cost_estimate=work(3 * slot_rows**2 * HEAD_DIM, 4 * slot_rows**2),
         name="attention",
-    )(source, *paged, weighted, arrived_grad)
+    )(source, paged, arrived_grad)
 
     def projected(*arrays, dtype):
         return pl.pallas_call(

time: 147 us -> 141 us (0.959)
  local copies, waits for them, and re-layouts: 12.7 us -> 5.03 us
  waiting for transfers between devices: 32.6 us -> 34.5 us
    unnamed x33 -> x15, local copies, waits for them, and re-layouts: 8.85 us -> 1.91 us
    all_to_all x1, waiting for transfers between devices: 15 us -> 17.6 us  [per_device(): arrived_grad = lax.all_to_all(sent_grad, 'tok', 0, 0, tiled=True)]
  transfers between devices with their start and end apart: 8 -> 8, of which waited for: 5 -> 5; matrix products, arithmetic and copies ran while one was open for 5% -> 6% of each run, Pallas kernels for 3% -> 3%
where the time goes in v5:
time: 141 us
  blocking collectives  42.9 us (30%)
  starting transfers between devices  40.7 us (29%)
  waiting for transfers between devices  34.5 us (24%)
  Pallas kernels  13.6 us (10%)
  local copies, waits for them, and re-layouts  5.03 us (4%)
  other arithmetic  3.5 us (2%)
    all_to_all x1, blocking collectives, per_device(): returned = lax.all_to_all(summed, 'tok', 0, 0, tiled=True)  23.4 us
    all_to_all x1, blocking collectives, per_device(): lax.all_to_all(partial, 'head', 0, 0, axis_index_groups=across, tiled=True)  19.5 us
    all_to_all x1, waiting for transfers between devices, per_device(): arrived_grad = lax.all_to_all(sent_grad, 'tok', 0, 0, tiled=True)  17.6 us
    all_to_all x1, starting transfers between devices, per_device(): arrived = lax.all_to_all(sent, 'tok', 0, 0, tiled=True)  16.7 us
    ppermute x6, starting transfers between devices, moved(): return lax.ppermute(array, 'head', pairs)  16 us
    all_to_all x1, waiting for transfers between devices, per_device(): arrived = lax.all_to_all(sent, 'tok', 0, 0, tiled=True)  13.1 us
    all_to_all x1, starting transfers between devices, per_device(): arrived_grad = lax.all_to_all(sent_grad, 'tok', 0, 0, tiled=True)  7.98 us
    pallas_call x1, Pallas kernels, per_device(): pl.pallas_call(attention_kernel, out_shape=jax.ShapeDtypeStruct((slot_row...  3.92 us
  transfers between devices with their start and end apart: 8, of which 5 were waited for; matrix products, arithmetic and copies ran while one was open for 6% of the time, Pallas kernels for 3%

profile of v5, /device:TPU:8, one launch (start us, length us, event | category | flops | bytes accessed | tf_op | source)
XLA Modules:
  0.0 140.5 jit_solution(1038587988476303316)
XLA Ops:
  0.0 2.7 %pack.1 = bf16[64,96,128]{2,1,0:T(8,128)(2,1)} custom-call(s32[1536]{0:T(1024)} %table.1, bf16[768,128]{1,0:T(8,128)(2,1)} %query.1, bf16[768,128]{1,0:T(8,128)(2,1)} %key.1, bf16[768,128]{1,0:T(8,128)(2,1)} %value.1), custom_call_target="tpu_custom_call" | custom-call | tf_op jit(solution)/shard_map/pack/pallas_call | solution.py:171
  2.7 16.7 %all-to-all-start = ((bf16[64,96,128]{2,1,0:T(8,128)(2,1)}), bf16[64,96,128]{2,1,0:T(8,128)(2,1)S(1)}, u32[]{:S(2)}, u32[]{:S(2)}) async-start(bf16[64,96,128]{2,1,0:T(8,128)(2,1)} %pack.1), calls=%async_computation | async-start | bytes 3145728 | tf_op jit(solution)/shard_map/all_to_all | solution.py:182
  19.5 4.7 %collective-permute-start.3 = (bf16[768,128]{1,0:T(8,128)(2,1)S(1)}, bf16[768,128]{1,0:T(8,128)(2,1)S(1)}, u32[]{:S(2)}, u32[]{:S(2)}) collective-permute-start(bf16[768,128]{1,0:T(8,128)(2,1)S(1)} %copy-done), channel_id=1, source_target_pairs={{0,384},{64,448},{128,0},{192,64},{256,128},{320,192},{384,256},{4... | collective-permute-start | bytes 589832 | tf_op jit(solution)/shard_map/ppermute | solution.py:166
  24.1 2.7 %collective-permute-start.2 = (bf16[768,128]{1,0:T(8,128)(2,1)S(1)}, bf16[768,128]{1,0:T(8,128)(2,1)S(1)}, u32[]{:S(2)}, u32[]{:S(2)}) collective-permute-start(bf16[768,128]{1,0:T(8,128)(2,1)S(1)} %copy-done), channel_id=1, source_target_pairs={{0,256},{64,320},{128,384},{192,448},{256,0},{320,64},{384,128},{4... | collective-permute-start | bytes 589832 | tf_op jit(solution)/shard_map/ppermute | solution.py:166
  26.8 2.8 %collective-permute-start.1 = (bf16[768,128]{1,0:T(8,128)(2,1)S(1)}, bf16[768,128]{1,0:T(8,128)(2,1)S(1)}, u32[]{:S(2)}, u32[]{:S(2)}) collective-permute-start(bf16[768,128]{1,0:T(8,128)(2,1)S(1)} %copy-done), channel_id=1, source_target_pairs={{0,128},{64,192},{128,256},{192,320},{256,384},{320,448},{384,0},{... | collective-permute-start | bytes 589832 | tf_op jit(solution)/shard_map/ppermute | solution.py:166
  30.7 0.9 copy.22
  31.6 1.9 %collective-permute-start = (bf16[384,512]{1,0:T(8,128)(2,1)}, bf16[384,512]{1,0:T(8,128)(2,1)S(1)}, u32[]{:S(2)}, u32[]{:S(2)}) collective-permute-start(bf16[384,512]{1,0:T(8,128)(2,1)} %bitcast.23), channel_id=1, source_target_pairs={{0,64},{64,0},{128,192},{192,128},{256,320},{320,256},{384,448},{4... | collective-permute-start | bytes 1179656 | tf_op jit(solution)/shard_map/ppermute | solution.py:166
  35.3 2.2 %collective-permute-done.1.refs_1_ = bf16[768,128]{1,0:T(8,128)(2,1)S(1)} collective-permute-done((bf16[768,128]{1,0:T(8,128)(2,1)S(1)}, bf16[768,128]{1,0:T(8,128)(2,1)S(1)}, u32[]{:S(2)}, u32[]{:S(2)}) %collective-permute-start.1) | collective-permute-done | bytes 196640 | tf_op jit(solution)/shard_map/ppermute | solution.py:166
  37.5 1.0 pad_maximum_fusion.1
  38.5 1.9 %collective-permute-start.4 = (bf16[4,768,128]{2,1,0:T(8,128)(2,1)}, bf16[4,768,128]{2,1,0:T(8,128)(2,1)}, u32[]{:S(2)}, u32[]{:S(2)}) collective-permute-start(bf16[4,768,128]{2,1,0:T(8,128)(2,1)} %pad_maximum_fusion.1), channel_id=1, source_target_pairs={{0,64},{64,0},{128,192},{192,128},{256,320},{320,256},{384,448},{4... | collective-permute-start | bytes 2359304 | tf_op jit(solution)/shard_map/ppermute | solution.py:166
  40.6 1.1 copy.18
  41.8 1.2 copy.21
  43.9 2.5 %grad.1 = bf16[64,32,128]{2,1,0:T(8,128)(2,1)} custom-call(s32[24]{0:T(128)S(1)} %dynamic_slice.10.dest, s32[2]{0:T(128)S(1)} %pad_add_fusion.here, bf16[768,128]{1,0:T(8,128)(2,1)S(1)} %copy-done, bf16[768,128]{1,0:T(8,128)(2,1)S(1)} %collective-permute-done.1.refs_1_, bf16[768,128]{1,0:T(8,128)(2,1)S(1)} %collective-permute-done.2.refs_2_, ...), custom_call_target="tpu_custom_call" | custom-call | flops 201326592 | bytes 3145728 | tf_op jit(solution)/shard_map/grad/pallas_call | solution.py:191
  47.2 13.1 %all-to-all-done.arrived = bf16[64,96,128]{2,1,0:T(8,128)(2,1)S(1)} async-done(((bf16[64,96,128]{2,1,0:T(8,128)(2,1)}), bf16[64,96,128]{2,1,0:T(8,128)(2,1)S(1)}, u32[]{:S(2)}, u32[]{:S(2)}) %all-to-all-start) | async-done | bytes 1572896 | tf_op jit(solution)/shard_map/all_to_all | solution.py:182
  60.3 8.0 %all-to-all-start.1 = ((bf16[64,32,128]{2,1,0:T(8,128)(2,1)}), bf16[64,32,128]{2,1,0:T(8,128)(2,1)S(1)}, u32[]{:S(2)}, u32[]{:S(2)}) async-start(bf16[64,32,128]{2,1,0:T(8,128)(2,1)} %grad.1), calls=%async_computation.1 | async-start | bytes 1048576 | tf_op jit(solution)/shard_map/all_to_all | solution.py:220
  68.9 17.6 %all-to-all-done.1.arrived = bf16[64,32,128]{2,1,0:T(8,128)(2,1)S(1)} async-done(((bf16[64,32,128]{2,1,0:T(8,128)(2,1)}), bf16[64,32,128]{2,1,0:T(8,128)(2,1)S(1)}, u32[]{:S(2)}, u32[]{:S(2)}) %all-to-all-start.1) | async-done | bytes 524320 | tf_op jit(solution)/shard_map/all_to_all | solution.py:220
  86.5 3.9 %attention.1.refs_0_ = bf16[1024,384]{1,0:T(8,128)(2,1)S(1)} custom-call(s32[32]{0:T(128)S(1)} %fusion.source, bf16[3,1024,128]{2,1,0:T(8,128)(2,1)S(1)} %assemble.1.paged, bf16[64,32,128]{2,1,0:T(8,128)(2,1)S(1)} %all-to-all-done.1.arrived), custom_call_target="tpu_custom_call" | custom-call | flops 805306368 | bytes 4194304 | tf_op jit(solution)/shard_map/attention/pallas_call | solution.py:230
  90.4 2.1 %collective-permute-start.5 = (bf16[1024,384]{1,0:T(8,128)(2,1)S(1)}, bf16[1024,384]{1,0:T(8,128)(2,1)S(1)}, u32[]{:S(2)}, u32[]{:S(2)}) collective-permute-start(bf16[1024,384]{1,0:T(8,128)(2,1)S(1)} %attention.1.refs_0_), channel_id=1, source_target_pairs={{0,64},{64,0},{128,192},{192,128},{256,320},{320,256},{384,448},{4... | collective-permute-start | bytes 2359304 | tf_op jit(solution)/shard_map/ppermute | solution.py:166
  92.5 1.0 shard_map.91.refs_0_
  93.5 1.3 collective-permute-done.5.refs_1_
  94.7 1.0 shard_map.92
  95.7 19.5 %all_to_all.20.parts = bf16[4,1024,128]{2,1,0:T(8,128)(2,1)S(1)} all-to-all(bf16[4,1024,128]{2,1,0:T(8,128)(2,1)S(1)} %shard_map.92), channel_id=1, replica_groups={{0,128,256,384},{64,192,320,448},{1,129,257,385},{65,193,321,449},{2,13..., dimensions={0} | all-to-all | bytes 2097152 | tf_op jit(solution)/shard_map/all_to_all | solution.py:255
  115.9 23.4 %all_to_all.21.returned = bf16[64,32,128]{2,1,0:T(8,128)(2,1)S(1)} all-to-all(bf16[64,32,128]{2,1,0:T(8,128)(2,1)S(1)} %sum.1), channel_id=1, replica_groups=mesh['head'=8,'tok'=64] {'tok'}, dimensions={0} | all-to-all | bytes 1048576 | tf_op jit(solution)/shard_map/all_to_all | solution.py:264
  139.3 1.2 unpack.1
  (33 shorter events, 5.8 us)
Async XLA Ops:
  2.7 16.8 %copy-start = (bf16[768,128]{1,0:T(8,128)(2,1)S(1)}, bf16[768,128]{1,0:T(8,128)(2,1)}, u32[]{:S(2)}) copy-start(bf16[768,128]{1,0:T(8,128)(2,1)} %refs_0_.1) | copy-start | bytes 589828
  2.7 27.0 %copy-start.3 = (bf16[1024,128]{1,0:T(8,128)(2,1)S(1)}, bf16[1024,128]{1,0:T(8,128)(2,1)}, u32[]{:S(2)}) copy-start(bf16[1024,128]{1,0:T(8,128)(2,1)} %param.15) | copy-start | bytes 786436
  2.7 27.0 %copy-start.4 = (bf16[1024,128]{1,0:T(8,128)(2,1)S(1)}, bf16[1024,128]{1,0:T(8,128)(2,1)}, u32[]{:S(2)}) copy-start(bf16[1024,128]{1,0:T(8,128)(2,1)} %param.14) | copy-start | bytes 786436
  2.7 27.0 %copy-start.5 = (bf16[1024,128]{1,0:T(8,128)(2,1)S(1)}, bf16[1024,128]{1,0:T(8,128)(2,1)}, u32[]{:S(2)}) copy-start(bf16[1024,128]{1,0:T(8,128)(2,1)} %param.13) | copy-start | bytes 786436
  2.7 57.6 %all-to-all-start = ((bf16[64,96,128]{2,1,0:T(8,128)(2,1)}), bf16[64,96,128]{2,1,0:T(8,128)(2,1)S(1)}, u32[]{:S(2)}, u32[]{:S(2)}) async-start(bf16[64,96,128]{2,1,0:T(8,128)(2,1)} %pack.1), calls=%async_computation | async-start | bytes 3145728 | tf_op jit(solution)/shard_map/all_to_all | solution.py:182
  19.5 15.6 %collective-permute-start.3 = (bf16[768,128]{1,0:T(8,128)(2,1)S(1)}, bf16[768,128]{1,0:T(8,128)(2,1)S(1)}, u32[]{:S(2)}, u32[]{:S(2)}) collective-permute-start(bf16[768,128]{1,0:T(8,128)(2,1)S(1)} %copy-done), channel_id=1, source_target_pairs={{0,384},{64,448},{128,0},{192,64},{256,128},{320,192},{384,256},{4... | collective-permute-start | bytes 589832 | tf_op jit(solution)/shard_map/ppermute | solution.py:166
  24.1 11.2 %collective-permute-start.2 = (bf16[768,128]{1,0:T(8,128)(2,1)S(1)}, bf16[768,128]{1,0:T(8,128)(2,1)S(1)}, u32[]{:S(2)}, u32[]{:S(2)}) collective-permute-start(bf16[768,128]{1,0:T(8,128)(2,1)S(1)} %copy-done), channel_id=1, source_target_pairs={{0,256},{64,320},{128,384},{192,448},{256,0},{320,64},{384,128},{4... | collective-permute-start | bytes 589832 | tf_op jit(solution)/shard_map/ppermute | solution.py:166
  26.8 10.7 %collective-permute-start.1 = (bf16[768,128]{1,0:T(8,128)(2,1)S(1)}, bf16[768,128]{1,0:T(8,128)(2,1)S(1)}, u32[]{:S(2)}, u32[]{:S(2)}) collective-permute-start(bf16[768,128]{1,0:T(8,128)(2,1)S(1)} %copy-done), channel_id=1, source_target_pairs={{0,128},{64,192},{128,256},{192,320},{256,384},{320,448},{384,0},{... | collective-permute-start | bytes 589832 | tf_op jit(solution)/shard_map/ppermute | solution.py:166
  29.8 3.7 %copy-start.6 = (s32[1536]{0:T(1024)S(1)}, s32[1536]{0:T(1024)}, u32[]{:S(2)}) copy-start(s32[1536]{0:T(1024)} %table.1) | copy-start | bytes 18436
  31.6 14.8 %collective-permute-start = (bf16[384,512]{1,0:T(8,128)(2,1)}, bf16[384,512]{1,0:T(8,128)(2,1)S(1)}, u32[]{:S(2)}, u32[]{:S(2)}) collective-permute-start(bf16[384,512]{1,0:T(8,128)(2,1)} %bitcast.23), channel_id=1, source_target_pairs={{0,64},{64,0},{128,192},{192,128},{256,320},{320,256},{384,448},{4... | collective-permute-start | bytes 1179656 | tf_op jit(solution)/shard_map/ppermute | solution.py:166
  38.5 5.3 %collective-permute-start.4 = (bf16[4,768,128]{2,1,0:T(8,128)(2,1)}, bf16[4,768,128]{2,1,0:T(8,128)(2,1)}, u32[]{:S(2)}, u32[]{:S(2)}) collective-permute-start(bf16[4,768,128]{2,1,0:T(8,128)(2,1)} %pad_maximum_fusion.1), channel_id=1, source_target_pairs={{0,64},{64,0},{128,192},{192,128},{256,320},{320,256},{384,448},{4... | collective-permute-start | bytes 2359304 | tf_op jit(solution)/shard_map/ppermute | solution.py:166
  46.4 0.8 copy-start.1
  60.3 26.2 %all-to-all-start.1 = ((bf16[64,32,128]{2,1,0:T(8,128)(2,1)}), bf16[64,32,128]{2,1,0:T(8,128)(2,1)S(1)}, u32[]{:S(2)}, u32[]{:S(2)}) async-start(bf16[64,32,128]{2,1,0:T(8,128)(2,1)} %grad.1), calls=%async_computation.1 | async-start | bytes 1048576 | tf_op jit(solution)/shard_map/all_to_all | solution.py:220
  90.4 4.3 %copy-start.2 = (bf16[384,512]{1,0:T(8,128)(2,1)S(1)}, bf16[384,512]{1,0:T(8,128)(2,1)}, u32[]{:S(2)}) copy-start(bf16[384,512]{1,0:T(8,128)(2,1)} %copy-done.1) | copy-start | bytes 1179652
  90.4 4.3 %collective-permute-start.5 = (bf16[1024,384]{1,0:T(8,128)(2,1)S(1)}, bf16[1024,384]{1,0:T(8,128)(2,1)S(1)}, u32[]{:S(2)}, u32[]{:S(2)}) collective-permute-start(bf16[1024,384]{1,0:T(8,128)(2,1)S(1)} %attention.1.refs_0_), channel_id=1, source_target_pairs={{0,64},{64,0},{128,192},{192,128},{256,320},{320,256},{384,448},{4... | collective-permute-start | bytes 2359304 | tf_op jit(solution)/shard_map/ppermute | solution.py:166

commit v6 on v5

--- a/solution.py
+++ b/solution.py
@@ -65,16 +65,16 @@
 
 
 def softmax_of(query, key, here, spans):
-    score = [mm(query[here], key[span], ((1,), (1,))) for span in spans]
-    row_order = lax.broadcasted_iota(jnp.int32, score[-1].shape, 0)
-    causal = lax.broadcasted_iota(jnp.int32, score[-1].shape, 1) <= row_order
+    score = [mm(key[span], query[here], ((1,), (1,))) for span in spans]
+    key_order = lax.broadcasted_iota(jnp.int32, score[-1].shape, 0)
+    causal = key_order <= lax.broadcasted_iota(jnp.int32, score[-1].shape, 1)
     score[-1] = jnp.where(causal, score[-1], NEG)
-    row_max = score[-1].max(axis=1, keepdims=True)
+    top = score[-1].max(axis=0, keepdims=True)
     if len(spans) > 1:
-        row_max = jnp.maximum(row_max, score[0].max(axis=1, keepdims=True))
+        top = jnp.maximum(top, score[0].max(axis=0, keepdims=True))
     factor = HEAD_DIM ** (-0.5) * math.log2(math.e)
-    raised = [jnp.exp2((s - row_max) * factor) for s in score]
-    inverse = 1.0 / sum(r.sum(axis=1, keepdims=True) for r in raised)
+    raised = [jnp.exp2((s - top) * factor) for s in score]
+    inverse = 1.0 / sum(r.sum(axis=0, keepdims=True) for r in raised)
     return [r * inverse for r in raised]
 
 
@@ -97,19 +97,19 @@
     for here, spans in spans_of(query.shape[0]):
         part_query, part_grad = query[here], grad[here]
         part_weights = softmax_of(query, key, here, spans)
-        grad_weights = [mm(part_grad, value[span], ((1,), (1,))) for span in spans]
+        grad_weights = [mm(value[span], part_grad, ((1,), (1,))) for span in spans]
         row_delta = sum(
-            (w * g).sum(axis=1, keepdims=True) for w, g in zip(part_weights, grad_weights)
+            (w * g).sum(axis=0, keepdims=True) for w, g in zip(part_weights, grad_weights)
         )
         grad_score = [
             (w * (g - row_delta)).astype(jnp.bfloat16)
             for w, g in zip(part_weights, grad_weights)
         ]
-        dquery = sum(mm(d, key[span], ((1,), (0,))) for d, span in zip(grad_score, spans))
+        dquery = sum(mm(d, key[span], ((0,), (0,))) for d, span in zip(grad_score, spans))
         grads[here, 0:HEAD_DIM] = (dquery * scale).astype(grads.dtype)
         for w, d, span in zip(part_weights, grad_score, spans):
-            more_key = mm(d, part_query, ((0,), (0,)))
-            more_value = mm(w.astype(jnp.bfloat16), part_grad, ((0,), (0,)))
+            more_key = mm(d, part_query, ((1,), (0,)))
+            more_value = mm(w.astype(jnp.bfloat16), part_grad, ((1,), (0,)))
             if span is here:
                 dkey[span] = more_key
                 dvalue[span] = more_value

time: 141 us -> 141 us (level)
  no operation moved by 1% of the time
where the time goes in v6:
time: 141 us; the launch traced here: 140 us
  blocking collectives  42.9 us (30%)
  starting transfers between devices  40.7 us (29%)
  waiting for transfers between devices  34.5 us (24%)
  Pallas kernels  13.4 us (10%)
  local copies, waits for them, and re-layouts  5.03 us (4%)
  other arithmetic  3.5 us (2%)
    all_to_all x1, blocking collectives, per_device(): returned = lax.all_to_all(summed, 'tok', 0, 0, tiled=True)  23.4 us
    all_to_all x1, blocking collectives, per_device(): lax.all_to_all(partial, 'head', 0, 0, axis_index_groups=across, tiled=True)  19.5 us
    all_to_all x1, waiting for transfers between devices, per_device(): arrived_grad = lax.all_to_all(sent_grad, 'tok', 0, 0, tiled=True)  17.6 us
    all_to_all x1, starting transfers between devices, per_device(): arrived = lax.all_to_all(sent, 'tok', 0, 0, tiled=True)  16.7 us
    ppermute x6, starting transfers between devices, moved(): return lax.ppermute(array, 'head', pairs)  16 us
    all_to_all x1, waiting for transfers between devices, per_device(): arrived = lax.all_to_all(sent, 'tok', 0, 0, tiled=True)  13.1 us
    all_to_all x1, starting transfers between devices, per_device(): arrived_grad = lax.all_to_all(sent_grad, 'tok', 0, 0, tiled=True)  7.98 us
    pallas_call x1, Pallas kernels, per_device(): pl.pallas_call(attention_kernel, out_shape=jax.ShapeDtypeStruct((slot_row...  3.75 us
  transfers between devices with their start and end apart: 8, of which 5 were waited for; matrix products, arithmetic and copies ran while one was open for 6% of the time, Pallas kernels for 3%

profile of v6, /device:TPU:8, one launch (start us, length us, event | category | flops | bytes accessed | tf_op | source)
XLA Modules:
  0.0 140.4 jit_solution(5021361850641815410)
XLA Ops:
  0.0 2.7 %pack.1 = bf16[64,96,128]{2,1,0:T(8,128)(2,1)} custom-call(s32[1536]{0:T(1024)} %table.1, bf16[768,128]{1,0:T(8,128)(2,1)} %query.1, bf16[768,128]{1,0:T(8,128)(2,1)} %key.1, bf16[768,128]{1,0:T(8,128)(2,1)} %value.1), custom_call_target="tpu_custom_call" | custom-call | tf_op jit(solution)/shard_map/pack/pallas_call | solution.py:171
  2.7 16.7 %all-to-all-start = ((bf16[64,96,128]{2,1,0:T(8,128)(2,1)}), bf16[64,96,128]{2,1,0:T(8,128)(2,1)S(1)}, u32[]{:S(2)}, u32[]{:S(2)}) async-start(bf16[64,96,128]{2,1,0:T(8,128)(2,1)} %pack.1), calls=%async_computation | async-start | bytes 3145728 | tf_op jit(solution)/shard_map/all_to_all | solution.py:182
  19.5 4.7 %collective-permute-start.3 = (bf16[768,128]{1,0:T(8,128)(2,1)S(1)}, bf16[768,128]{1,0:T(8,128)(2,1)S(1)}, u32[]{:S(2)}, u32[]{:S(2)}) collective-permute-start(bf16[768,128]{1,0:T(8,128)(2,1)S(1)} %copy-done), channel_id=1, source_target_pairs={{0,384},{64,448},{128,0},{192,64},{256,128},{320,192},{384,256},{4... | collective-permute-start | bytes 589832 | tf_op jit(solution)/shard_map/ppermute | solution.py:166
  24.1 2.7 %collective-permute-start.2 = (bf16[768,128]{1,0:T(8,128)(2,1)S(1)}, bf16[768,128]{1,0:T(8,128)(2,1)S(1)}, u32[]{:S(2)}, u32[]{:S(2)}) collective-permute-start(bf16[768,128]{1,0:T(8,128)(2,1)S(1)} %copy-done), channel_id=1, source_target_pairs={{0,256},{64,320},{128,384},{192,448},{256,0},{320,64},{384,128},{4... | collective-permute-start | bytes 589832 | tf_op jit(solution)/shard_map/ppermute | solution.py:166
  26.8 2.8 %collective-permute-start.1 = (bf16[768,128]{1,0:T(8,128)(2,1)S(1)}, bf16[768,128]{1,0:T(8,128)(2,1)S(1)}, u32[]{:S(2)}, u32[]{:S(2)}) collective-permute-start(bf16[768,128]{1,0:T(8,128)(2,1)S(1)} %copy-done), channel_id=1, source_target_pairs={{0,128},{64,192},{128,256},{192,320},{256,384},{320,448},{384,0},{... | collective-permute-start | bytes 589832 | tf_op jit(solution)/shard_map/ppermute | solution.py:166
  30.7 0.9 copy.22
  31.6 1.9 %collective-permute-start = (bf16[384,512]{1,0:T(8,128)(2,1)}, bf16[384,512]{1,0:T(8,128)(2,1)S(1)}, u32[]{:S(2)}, u32[]{:S(2)}) collective-permute-start(bf16[384,512]{1,0:T(8,128)(2,1)} %bitcast.23), channel_id=1, source_target_pairs={{0,64},{64,0},{128,192},{192,128},{256,320},{320,256},{384,448},{4... | collective-permute-start | bytes 1179656 | tf_op jit(solution)/shard_map/ppermute | solution.py:166
  35.3 2.2 %collective-permute-done.1.refs_1_ = bf16[768,128]{1,0:T(8,128)(2,1)S(1)} collective-permute-done((bf16[768,128]{1,0:T(8,128)(2,1)S(1)}, bf16[768,128]{1,0:T(8,128)(2,1)S(1)}, u32[]{:S(2)}, u32[]{:S(2)}) %collective-permute-start.1) | collective-permute-done | bytes 196640 | tf_op jit(solution)/shard_map/ppermute | solution.py:166
  37.5 1.0 pad_maximum_fusion.1
  38.5 1.9 %collective-permute-start.4 = (bf16[4,768,128]{2,1,0:T(8,128)(2,1)}, bf16[4,768,128]{2,1,0:T(8,128)(2,1)}, u32[]{:S(2)}, u32[]{:S(2)}) collective-permute-start(bf16[4,768,128]{2,1,0:T(8,128)(2,1)} %pad_maximum_fusion.1), channel_id=1, source_target_pairs={{0,64},{64,0},{128,192},{192,128},{256,320},{320,256},{384,448},{4... | collective-permute-start | bytes 2359304 | tf_op jit(solution)/shard_map/ppermute | solution.py:166
  40.6 1.1 copy.18
  41.8 1.2 copy.21
  43.9 2.5 %grad.1 = bf16[64,32,128]{2,1,0:T(8,128)(2,1)} custom-call(s32[24]{0:T(128)S(1)} %dynamic_slice.10.dest, s32[2]{0:T(128)S(1)} %pad_add_fusion.here, bf16[768,128]{1,0:T(8,128)(2,1)S(1)} %copy-done, bf16[768,128]{1,0:T(8,128)(2,1)S(1)} %collective-permute-done.1.refs_1_, bf16[768,128]{1,0:T(8,128)(2,1)S(1)} %collective-permute-done.2.refs_2_, ...), custom_call_target="tpu_custom_call" | custom-call | flops 201326592 | bytes 3145728 | tf_op jit(solution)/shard_map/grad/pallas_call | solution.py:191
  47.2 13.1 %all-to-all-done.arrived = bf16[64,96,128]{2,1,0:T(8,128)(2,1)S(1)} async-done(((bf16[64,96,128]{2,1,0:T(8,128)(2,1)}), bf16[64,96,128]{2,1,0:T(8,128)(2,1)S(1)}, u32[]{:S(2)}, u32[]{:S(2)}) %all-to-all-start) | async-done | bytes 1572896 | tf_op jit(solution)/shard_map/all_to_all | solution.py:182
  60.3 8.0 %all-to-all-start.1 = ((bf16[64,32,128]{2,1,0:T(8,128)(2,1)}), bf16[64,32,128]{2,1,0:T(8,128)(2,1)S(1)}, u32[]{:S(2)}, u32[]{:S(2)}) async-start(bf16[64,32,128]{2,1,0:T(8,128)(2,1)} %grad.1), calls=%async_computation.1 | async-start | bytes 1048576 | tf_op jit(solution)/shard_map/all_to_all | solution.py:220
  68.9 17.6 %all-to-all-done.1.arrived = bf16[64,32,128]{2,1,0:T(8,128)(2,1)S(1)} async-done(((bf16[64,32,128]{2,1,0:T(8,128)(2,1)}), bf16[64,32,128]{2,1,0:T(8,128)(2,1)S(1)}, u32[]{:S(2)}, u32[]{:S(2)}) %all-to-all-start.1) | async-done | bytes 524320 | tf_op jit(solution)/shard_map/all_to_all | solution.py:220
  86.5 3.8 %attention.1.refs_0_ = bf16[1024,384]{1,0:T(8,128)(2,1)S(1)} custom-call(s32[32]{0:T(128)S(1)} %fusion.source, bf16[3,1024,128]{2,1,0:T(8,128)(2,1)S(1)} %assemble.1.paged, bf16[64,32,128]{2,1,0:T(8,128)(2,1)S(1)} %all-to-all-done.1.arrived), custom_call_target="tpu_custom_call" | custom-call | flops 805306368 | bytes 4194304 | tf_op jit(solution)/shard_map/attention/pallas_call | solution.py:230
  90.3 2.1 %collective-permute-start.5 = (bf16[1024,384]{1,0:T(8,128)(2,1)S(1)}, bf16[1024,384]{1,0:T(8,128)(2,1)S(1)}, u32[]{:S(2)}, u32[]{:S(2)}) collective-permute-start(bf16[1024,384]{1,0:T(8,128)(2,1)S(1)} %attention.1.refs_0_), channel_id=1, source_target_pairs={{0,64},{64,0},{128,192},{192,128},{256,320},{320,256},{384,448},{4... | collective-permute-start | bytes 2359304 | tf_op jit(solution)/shard_map/ppermute | solution.py:166
  92.3 1.0 shard_map.91.refs_0_
  93.3 1.3 collective-permute-done.5.refs_1_
  94.6 1.0 shard_map.92
  95.5 19.5 %all_to_all.20.parts = bf16[4,1024,128]{2,1,0:T(8,128)(2,1)S(1)} all-to-all(bf16[4,1024,128]{2,1,0:T(8,128)(2,1)S(1)} %shard_map.92), channel_id=1, replica_groups={{0,128,256,384},{64,192,320,448},{1,129,257,385},{65,193,321,449},{2,13..., dimensions={0} | all-to-all | bytes 2097152 | tf_op jit(solution)/shard_map/all_to_all | solution.py:255
  115.7 23.4 %all_to_all.21.returned = bf16[64,32,128]{2,1,0:T(8,128)(2,1)S(1)} all-to-all(bf16[64,32,128]{2,1,0:T(8,128)(2,1)S(1)} %sum.1), channel_id=1, replica_groups=mesh['head'=8,'tok'=64] {'tok'}, dimensions={0} | all-to-all | bytes 1048576 | tf_op jit(solution)/shard_map/all_to_all | solution.py:264
  139.1 1.2 unpack.1
  (33 shorter events, 5.8 us)
Async XLA Ops:
  2.7 16.8 %copy-start = (bf16[768,128]{1,0:T(8,128)(2,1)S(1)}, bf16[768,128]{1,0:T(8,128)(2,1)}, u32[]{:S(2)}) copy-start(bf16[768,128]{1,0:T(8,128)(2,1)} %refs_0_.1) | copy-start | bytes 589828
  2.7 27.0 %copy-start.3 = (bf16[1024,128]{1,0:T(8,128)(2,1)S(1)}, bf16[1024,128]{1,0:T(8,128)(2,1)}, u32[]{:S(2)}) copy-start(bf16[1024,128]{1,0:T(8,128)(2,1)} %param.15) | copy-start | bytes 786436
  2.7 27.0 %copy-start.4 = (bf16[1024,128]{1,0:T(8,128)(2,1)S(1)}, bf16[1024,128]{1,0:T(8,128)(2,1)}, u32[]{:S(2)}) copy-start(bf16[1024,128]{1,0:T(8,128)(2,1)} %param.14) | copy-start | bytes 786436
  2.7 27.0 %copy-start.5 = (bf16[1024,128]{1,0:T(8,128)(2,1)S(1)}, bf16[1024,128]{1,0:T(8,128)(2,1)}, u32[]{:S(2)}) copy-start(bf16[1024,128]{1,0:T(8,128)(2,1)} %param.13) | copy-start | bytes 786436
  2.7 57.6 %all-to-all-start = ((bf16[64,96,128]{2,1,0:T(8,128)(2,1)}), bf16[64,96,128]{2,1,0:T(8,128)(2,1)S(1)}, u32[]{:S(2)}, u32[]{:S(2)}) async-start(bf16[64,96,128]{2,1,0:T(8,128)(2,1)} %pack.1), calls=%async_computation | async-start | bytes 3145728 | tf_op jit(solution)/shard_map/all_to_all | solution.py:182
  19.5 15.6 %collective-permute-start.3 = (bf16[768,128]{1,0:T(8,128)(2,1)S(1)}, bf16[768,128]{1,0:T(8,128)(2,1)S(1)}, u32[]{:S(2)}, u32[]{:S(2)}) collective-permute-start(bf16[768,128]{1,0:T(8,128)(2,1)S(1)} %copy-done), channel_id=1, source_target_pairs={{0,384},{64,448},{128,0},{192,64},{256,128},{320,192},{384,256},{4... | collective-permute-start | bytes 589832 | tf_op jit(solution)/shard_map/ppermute | solution.py:166
  24.1 11.2 %collective-permute-start.2 = (bf16[768,128]{1,0:T(8,128)(2,1)S(1)}, bf16[768,128]{1,0:T(8,128)(2,1)S(1)}, u32[]{:S(2)}, u32[]{:S(2)}) collective-permute-start(bf16[768,128]{1,0:T(8,128)(2,1)S(1)} %copy-done), channel_id=1, source_target_pairs={{0,256},{64,320},{128,384},{192,448},{256,0},{320,64},{384,128},{4... | collective-permute-start | bytes 589832 | tf_op jit(solution)/shard_map/ppermute | solution.py:166
  26.8 10.7 %collective-permute-start.1 = (bf16[768,128]{1,0:T(8,128)(2,1)S(1)}, bf16[768,128]{1,0:T(8,128)(2,1)S(1)}, u32[]{:S(2)}, u32[]{:S(2)}) collective-permute-start(bf16[768,128]{1,0:T(8,128)(2,1)S(1)} %copy-done), channel_id=1, source_target_pairs={{0,128},{64,192},{128,256},{192,320},{256,384},{320,448},{384,0},{... | collective-permute-start | bytes 589832 | tf_op jit(solution)/shard_map/ppermute | solution.py:166
  29.8 3.7 %copy-start.6 = (s32[1536]{0:T(1024)S(1)}, s32[1536]{0:T(1024)}, u32[]{:S(2)}) copy-start(s32[1536]{0:T(1024)} %table.1) | copy-start | bytes 18436
  31.6 14.8 %collective-permute-start = (bf16[384,512]{1,0:T(8,128)(2,1)}, bf16[384,512]{1,0:T(8,128)(2,1)S(1)}, u32[]{:S(2)}, u32[]{:S(2)}) collective-permute-start(bf16[384,512]{1,0:T(8,128)(2,1)} %bitcast.23), channel_id=1, source_target_pairs={{0,64},{64,0},{128,192},{192,128},{256,320},{320,256},{384,448},{4... | collective-permute-start | bytes 1179656 | tf_op jit(solution)/shard_map/ppermute | solution.py:166
  38.5 5.3 %collective-permute-start.4 = (bf16[4,768,128]{2,1,0:T(8,128)(2,1)}, bf16[4,768,128]{2,1,0:T(8,128)(2,1)}, u32[]{:S(2)}, u32[]{:S(2)}) collective-permute-start(bf16[4,768,128]{2,1,0:T(8,128)(2,1)} %pad_maximum_fusion.1), channel_id=1, source_target_pairs={{0,64},{64,0},{128,192},{192,128},{256,320},{320,256},{384,448},{4... | collective-permute-start | bytes 2359304 | tf_op jit(solution)/shard_map/ppermute | solution.py:166
  46.4 0.8 copy-start.1
  60.3 26.2 %all-to-all-start.1 = ((bf16[64,32,128]{2,1,0:T(8,128)(2,1)}), bf16[64,32,128]{2,1,0:T(8,128)(2,1)S(1)}, u32[]{:S(2)}, u32[]{:S(2)}) async-start(bf16[64,32,128]{2,1,0:T(8,128)(2,1)} %grad.1), calls=%async_computation.1 | async-start | bytes 1048576 | tf_op jit(solution)/shard_map/all_to_all | solution.py:220
  90.2 4.3 %copy-start.2 = (bf16[384,512]{1,0:T(8,128)(2,1)S(1)}, bf16[384,512]{1,0:T(8,128)(2,1)}, u32[]{:S(2)}) copy-start(bf16[384,512]{1,0:T(8,128)(2,1)} %copy-done.1) | copy-start | bytes 1179652
  90.3 4.3 %collective-permute-start.5 = (bf16[1024,384]{1,0:T(8,128)(2,1)S(1)}, bf16[1024,384]{1,0:T(8,128)(2,1)S(1)}, u32[]{:S(2)}, u32[]{:S(2)}) collective-permute-start(bf16[1024,384]{1,0:T(8,128)(2,1)S(1)} %attention.1.refs_0_), channel_id=1, source_target_pairs={{0,64},{64,0},{128,192},{192,128},{256,320},{320,256},{384,448},{4... | collective-permute-start | bytes 2359304 | tf_op jit(solution)/shard_map/ppermute | solution.py:166
